TPU v7x, 8 devices: a whole 2x2x1 slice. The times are simulated.
8 devices in a mesh: dp: 1 (over z), yz: 2 (over y), x: 4 (over x, core).
Axes of the slice: x: 2, y: 2, z: 1, core: 2. Of those that a mesh axis runs over, the one named last changes fastest.
Arguments:
- hidden: bfloat16 [256, 6144], P('dp', ('x', 'yz'))
- norm_gain: bfloat16 [1, 6144], P(None, 'x')
- w_q: bfloat16 [1, 6144, 6144], P(None, 'x', 'yz')
- w_kv: bfloat16 [1, 6144, 256], P(None, 'x', 'yz')
- w_gate: bfloat16 [1, 6144, 24576], P(None, 'x', 'yz')
- w_up: bfloat16 [1, 6144, 24576], P(None, 'x', 'yz')
- w_o: bfloat16 [1, 6144, 6144], P(None, 'yz', 'x')
- w_down: bfloat16 [1, 24576, 6144], P(None, 'yz', 'x')
- k_cache: bfloat16 [1, 256, 2048, 128], P(None, ('dp', 'x', 'yz'))
- v_cache: bfloat16 [1, 256, 2048, 128], P(None, ('dp', 'x', 'yz'))
- seq_len: int32 [256], P(('dp', 'x', 'yz'))
Outputs:
- output 1: bfloat16 [256, 6144], P('dp', ('x', 'yz'))
- output 2: bfloat16 [1, 256, 2048, 128], P(None, ('dp', 'x', 'yz'))
- output 3: bfloat16 [1, 256, 2048, 128], P(None, ('dp', 'x', 'yz'))
All inputs are finite; a program needn't handle non-finite values.
Results may differ from a plain program's by a relative error of at most 0.0163719.
Values are sent between devices in bfloat16 or wider.
A program may use at most 1 GiB of HBM per device.

v0:
```python
import jax
import jax.numpy as jnp
from jax import lax
from jax.sharding import PartitionSpec as P

NORM_EPS = 1e-6


def solution(mesh):
    x_size = mesh.shape["x"]
    y_size = mesh.shape["yz"]
    row_spec = P("dp", ("x", "yz"))
    tile_in = P(None, "x", "yz")
    tile_out = P(None, "yz", "x")
    cache_spec = P(None, ("dp", "x", "yz"))
    len_spec = P(("dp", "x", "yz"))

    def device_step(hidden, norm_gain, w_q, w_kv, w_gate, w_up, w_o, w_down, k_cache, v_cache, seq_len):
        d_model = hidden.shape[1] * x_size * y_size
        local_seqs = k_cache.shape[1]
        cache_len = k_cache.shape[2]
        head_dim = k_cache.shape[3]
        q_cols = w_q.shape[2]
        kv_cols = w_kv.shape[2]
        ff_cols = w_gate.shape[2]
        attn_cols = q_cols + kv_cols
        n_heads = q_cols * y_size // head_dim
        positions = jnp.arange(cache_len)
        slot_hit = (positions[None, :] == seq_len[:, None])[:, :, None]
        visible = positions[None, None, :] <= seq_len[:, None, None]
        k_layers = []
        v_layers = []
        for layer_idx in range(w_q.shape[0]):
            feat_rows = lax.all_gather(hidden, "yz", axis=1, tiled=True)
            feat_f32 = feat_rows.astype(jnp.float32)
            sq_sum = lax.psum(jnp.sum(feat_f32 * feat_f32, axis=1, keepdims=True), "x")
            inv_rms = lax.rsqrt(sq_sum / d_model + NORM_EPS)
            normed = (feat_f32 * inv_rms * norm_gain[layer_idx].astype(jnp.float32)).astype(jnp.bfloat16)
            part_sum = jnp.concatenate([jnp.dot(normed, weight[layer_idx], preferred_element_type=jnp.float32) for weight in (w_q, w_kv, w_gate, w_up)], axis=1).astype(jnp.bfloat16)
            proj_rows = lax.psum_scatter(part_sum, "x", scatter_dimension=0, tiled=True)
            gate_act = proj_rows[:, attn_cols:attn_cols + ff_cols].astype(jnp.float32)
            up_act = proj_rows[:, attn_cols + ff_cols:].astype(jnp.float32)
            mlp_act = (jax.nn.silu(gate_act) * up_act).astype(jnp.bfloat16)
            mlp_rows = lax.all_gather(mlp_act, "x", axis=0, tiled=True)
            by_seq = lax.all_to_all(proj_rows[:, :attn_cols], "yz", 0, 1, tiled=True).reshape(local_seqs, y_size, attn_cols)
            query_heads = by_seq[:, :, :q_cols].reshape(local_seqs, n_heads, head_dim)
            kv_new = by_seq[:, :, q_cols:].reshape(local_seqs, 2 * head_dim)
            new_k = jnp.where(slot_hit, kv_new[:, None, :head_dim], k_cache[layer_idx])
            new_v = jnp.where(slot_hit, kv_new[:, None, head_dim:], v_cache[layer_idx])
            scores = jnp.einsum("bhd,bsd->bhs", query_heads, new_k, preferred_element_type=jnp.float32) * head_dim ** -0.5
            scores = jnp.where(visible, scores, -1e30)
            weights = jnp.exp(scores - jnp.max(scores, axis=-1, keepdims=True))
            probs_bf = (weights / jnp.sum(weights, axis=-1, keepdims=True)).astype(jnp.bfloat16)
            attn_out = jnp.einsum("bhs,bsd->bhd", probs_bf, new_v, preferred_element_type=jnp.float32).astype(jnp.bfloat16)
            attn_back = lax.all_to_all(attn_out.reshape(local_seqs, n_heads * head_dim), "yz", 1, 0, tiled=True)
            attn_rows = lax.all_gather(attn_back, "x", axis=0, tiled=True)
            update = jnp.dot(attn_rows, w_o[layer_idx], preferred_element_type=jnp.float32) + jnp.dot(mlp_rows, w_down[layer_idx], preferred_element_type=jnp.float32)
            update = lax.psum_scatter(update.astype(jnp.bfloat16), "yz", scatter_dimension=1, tiled=True)
            hidden = (hidden.astype(jnp.float32) + update.astype(jnp.float32)).astype(jnp.bfloat16)
            k_layers.append(new_k)
            v_layers.append(new_v)
        return hidden, jnp.stack(k_layers), jnp.stack(v_layers)

    sharded_step = jax.shard_map(
        device_step,
        mesh=mesh,
        in_specs=(row_spec, P(None, "x"), tile_in, tile_in, tile_in, tile_in, tile_out, tile_out, cache_spec, cache_spec, len_spec),
        out_specs=(row_spec, cache_spec, cache_spec),
        check_vma=False,
    )
    return sharded_step
```

profile of v0, /device:TPU:0, one launch (start us, length us, event | category | flops | bytes accessed | tf_op | source)
XLA Modules:
  0.0 359.6 jit_solution(17666479068222804123)
XLA Ops:
  7.2 0.8 convert_reduce_fusion
  8.0 13.1 %all_gather.9 = bf16[256,1536]{1,0:T(8,128)(2,1)S(1)} all-gather(bf16[256,768]{1,0:T(8,128)(2,1)} %param.11), channel_id=1, replica_groups=mesh['dp'=1,'yz'=2,'x'=4] {'yz'}, dimensions={1}, use_global_device_ids=true | all-gather | bytes 1179648 | tf_op jit(solution)/shard_map/all_gather | solution.py:34
  21.4 6.0 %psum.7 = f32[256,1]{0,1:T(1,128)S(1)} all-reduce(f32[256,1]{0,1:T(1,128)S(1)} %bitcast.60), channel_id=1, replica_groups=mesh['dp'=1,'yz'=2,'x'=4] {'x'}, use_global_device_ids=true, to_apply=%region_1.0 | all-reduce | flops 256 | bytes 2048 | tf_op jit(solution)/shard_map/psum | solution.py:36
  27.3 0.5 convolution_convert_fusion
  27.9 6.4 %fusion.28 = bf16[256,3072]{1,0:T(8,128)(2,1)S(1)} fusion(bf16[1,1536,3072]{2,1,0:T(8,128)(2,1)} %param.13, bf16[256,1536]{1,0:T(8,128)(2,1)S(1)} %all_gather.9, f32[1536]{0:T(1024)S(1)} %convert_reduce_fusion, f32[256]{0:T(256)S(1)} %bitcast.62), kind=kOutput, calls=%fused_computation.34 | convolution fusion | flops 2418278400 | bytes 11803648 | tf_op jit(solution)/shard_map/dot_general | solution.py:39
  34.3 18.6 %fusion.11 = bf16[256,12288]{1,0:T(8,128)(2,1)} fusion(bf16[1,1536,12288]{2,1,0:T(8,128)(2,1)} %param.15, bf16[256,1536]{1,0:T(8,128)(2,1)S(1)} %all_gather.9, f32[1536]{0:T(1024)S(1)} %convert_reduce_fusion, f32[256]{0:T(256)S(1)} %bitcast.63), kind=kOutput, calls=%fused_computation.15 | convolution fusion | flops 9668395008 | bytes 44833792 | tf_op jit(solution)/shard_map/dot_general | solution.py:39
  52.9 18.5 %fusion.14 = bf16[256,12288]{1,0:T(8,128)(2,1)} fusion(bf16[1,1536,12288]{2,1,0:T(8,128)(2,1)} %param.16, bf16[256,1536]{1,0:T(8,128)(2,1)S(1)} %all_gather.9, f32[1536]{0:T(1024)S(1)} %convert_reduce_fusion, f32[256]{0:T(256)S(1)} %bitcast.64), kind=kOutput, calls=%fused_computation.16 | convolution fusion | flops 9668395008 | bytes 44833792 | tf_op jit(solution)/shard_map/dot_general | solution.py:39
  71.4 11.6 %pad_maximum_fusion = bf16[256,27776]{1,0:T(8,128)(2,1)} fusion(bf16[256,12288]{1,0:T(8,128)(2,1)} %fusion.14, bf16[256,12288]{1,0:T(8,128)(2,1)} %fusion.11, bf16[256,128]{1,0:T(8,128)(2,1)S(1)} %copy.19, bf16[256,3072]{1,0:T(8,128)(2,1)S(1)} %fusion.28), kind=kLoop, calls=%fused_computation.17 | loop fusion | flops 56885248 | bytes 28442624 | tf_op jit(solution)/shard_map/concatenate | solution.py:39
  83.0 101.8 %reduce-scatter.3.cloned.1.call-done = bf16[64,27776]{1,0:T(8,128)(2,1)} async-done(((bf16[256,27776]{1,0:T(8,128)(2,1)}), bf16[64,27776]{1,0:T(8,128)(2,1)}) %reduce-scatter.3.cloned.1.call-update) | async-done | bytes 3555344 | tf_op jit(solution)/shard_map/reduce_scatter | solution.py:40
  184.8 1.8 slice.28
  186.6 3.5 all-to-all-start
  190.5 6.2 %all-to-all-done = bf16[2,32,3200]{2,1,0:T(8,128)(2,1)S(1)} async-done(((bf16[2,32,3200]{2,1,0:T(8,128)(2,1)}), bf16[2,32,3200]{2,1,0:T(8,128)(2,1)S(1)}, u32[]{:S(2)}, u32[]{:S(2)}) %all-to-all-start) | async-done | bytes 409632 | tf_op jit(solution)/shard_map/all_to_all | solution.py:45
  196.7 0.4 copy.20
  197.4 18.0 %fusion.8 = f32[32,48,2048]{2,1,0:T(8,128)S(1)} fusion(bf16[32,48,128]{2,1,0:T(8,128)(2,1)S(1)} %reshape.68, bf16[1,32,2048,128]{3,2,1,0:T(8,128)(2,1)} %param.19, pred[32,2048]{1,0:T(8,128)(4,1)S(1)} %get-tuple-element.8, bf16[32,128]{1,0:T(8,128)(2,1)S(1)} %get-tuple-element.5), kind=kOutput, calls=%fused_computation.10 | convolution fusion | flops 813694976 | bytes 29827072 | tf_op jit(solution)/shard_map/bhd,bsd->bhs/dot_general | solution.py:50
  215.4 7.2 %fusion.54 = (f32[32,48]{1,0:T(8,128)S(1)}, f32[32,48,2048]{2,1,0:T(8,128)}) fusion(f32[32,48,2048]{2,1,0:T(8,128)S(1)} %fusion.8, pred[32,2048]{1,0:T(8,128)(4,1)S(1)} %get-tuple-element.7), kind=kOutput, calls=%fused_computation.60 | output fusion | flops 18876416 | bytes 25237504 | tf_op jit(solution)/shard_map/sub | solution.py:52
  222.6 14.8 %fusion.45 = bf16[32,48,128]{2,1,0:T(8,128)(2,1)S(1)} fusion(bf16[1,32,2048,128]{3,2,1,0:T(8,128)(2,1)} %param.20, pred[32,2048]{1,0:T(8,128)(4,1)S(1)} %get-tuple-element.8, bf16[32,128]{1,0:T(8,128)(2,1)S(1)} %get-tuple-element.6, f32[32,48,2048]{2,1,0:T(8,128)} %get-tuple-element.10, f32[32,48]{1,0:T(8,128)S(1)} %get-tuple-element.9), kind=kOutput, calls=%fused_computation.47 | convolution fusion | flops 820183040 | bytes 29833216 | tf_op jit(solution)/shard_map/bhs,bsd->bhd/dot_general | solution.py:54
  237.5 8.9 %all_to_all.35 = bf16[32,2,3072]{2,0,1:T(8,128)(2,1)} all-to-all(bf16[32,2,3072]{2,0,1:T(8,128)(2,1)S(1)} %copy.22), channel_id=1, replica_groups=mesh['dp'=1,'yz'=2,'x'=4] {'yz'}, dimensions={1} | all-to-all | bytes 786432 | tf_op jit(solution)/shard_map/all_to_all | solution.py:55
  246.5 3.9 %fusion.35 = bf16[64,12288]{1,0:T(8,128)(2,1)} fusion(bf16[64,27776]{1,0:T(8,128)(2,1)} %reduce-scatter.3.cloned.1.call-done), kind=kLoop, calls=%fused_computation.39 | loop fusion | flops 6291456 | bytes 4718592 | tf_op jit(solution)/shard_map/convert_element_type | solution.py:43
  250.5 12.0 %all-gather.3.cloned.1.call-done = bf16[256,3072]{1,0:T(8,128)(2,1)} async-done(((bf16[64,3072]{1,0:T(8,128)(2,1)}), bf16[256,3072]{1,0:T(8,128)(2,1)}) %all-gather.3.cloned.1.call-update) | async-done | bytes 1572880 | tf_op jit(solution)/shard_map/all_gather | solution.py:56
  262.4 5.6 %fusion.18 = f32[256,1536]{1,0:T(8,128)S(1)} fusion(bf16[256,3072]{1,0:T(8,128)(2,1)} %all-gather.3.cloned.1.call-done, bf16[1,3072,1536]{2,1,0:T(8,128)(2,1)} %param.17), kind=kOutput, calls=%fused_computation.22 | convolution fusion | flops 2415919104 | bytes 12582912 | tf_op jit(solution)/shard_map/dot_general | solution.py:57
  268.1 40.1 %all-gather.5.cloned.1.call-done = bf16[256,12288]{1,0:T(8,128)(2,1)} async-done(((bf16[64,12288]{1,0:T(8,128)(2,1)}), bf16[256,12288]{1,0:T(8,128)(2,1)}) %all-gather.5.cloned.1.call-update) | async-done | bytes 6291472 | tf_op jit(solution)/shard_map/all_gather | solution.py:44
  308.2 19.4 %fusion.39 = bf16[256,1536]{1,0:T(8,128)(2,1)} fusion(f32[256,1536]{1,0:T(8,128)S(1)} %fusion.18, bf16[256,12288]{1,0:T(8,128)(2,1)} %all-gather.5.cloned.1.call-done, bf16[1,12288,1536]{2,1,0:T(8,128)(2,1)} %param.18), kind=kOutput, calls=%fused_computation.41 | convolution fusion | flops 9664462848 | bytes 46399488 | tf_op jit(solution)/shard_map/dot_general | solution.py:57
  327.7 23.5 %broadcast_select_fusion = (bf16[1,32,2048,128]{3,2,1,0:T(8,128)(2,1)}, bf16[1,32,2048,128]{3,2,1,0:T(8,128)(2,1)}) fusion(bf16[1,32,2048,128]{3,2,1,0:T(8,128)(2,1)} %param.20, pred[32,2048]{1,0:T(8,128)(4,1)S(1)} %get-tuple-element.8, bf16[32,128]{1,0:T(8,128)(2,1)S(1)} %get-tuple-element.6, bf16[1,32,2048,128]{3,2,1,0:T(8,128)(2,1)} %param.19, ...), kind=kLoop, calls=%fused_computation.11 | loop fusion | flops 16777216 | bytes 67190784 | tf_op jit(solution)/shard_map/jit(_where)/select_n | solution.py:49
  351.2 1.8 add_convert_fusion
  (27 shorter events, 1.4 us)
Async XLA Ops:
  7.2 20.2 %copy-start = (bf16[1,1536,128]{2,1,0:T(8,128)(2,1)S(1)}, bf16[1,1536,128]{2,1,0:T(8,128)(2,1)}, u32[]{:S(2)}) copy-start(bf16[1,1536,128]{2,1,0:T(8,128)(2,1)} %param.14) | copy-start | bytes 1179652
  7.2 177.7 %reduce-scatter.3.cloned.1.call-start = ((), (), s32[]{:S(2)}) async-start(), calls=%async_computation.4 | async-start | bytes 17776640 | tf_op jit(solution)/shard_map/reduce_scatter | solution.py:40
  83.0 107.4 %copy-start.3 = (s32[32]{0:T(128)S(1)}, s32[32]{0:T(128)}, u32[]{:S(2)}) copy-start(s32[32]{0:T(128)} %param.21) | copy-start | bytes 388
  186.6 10.0 %all-to-all-start = ((bf16[2,32,3200]{2,1,0:T(8,128)(2,1)}), bf16[2,32,3200]{2,1,0:T(8,128)(2,1)S(1)}, u32[]{:S(2)}, u32[]{:S(2)}) async-start(bf16[2,32,3200]{2,1,0:T(8,128)(2,1)} %bitcast.6), calls=%async_computation.1 | async-start | bytes 819200 | tf_op jit(solution)/shard_map/all_to_all | solution.py:45
  190.1 72.4 %all-gather.3.cloned.1.call-start = ((), (), s32[]{:S(2)}) async-start(), calls=%async_computation.5 | async-start | bytes 1966080 | tf_op jit(solution)/shard_map/all_gather | solution.py:56
  246.4 61.8 %all-gather.5.cloned.1.call-start = ((), (), s32[]{:S(2)}) async-start(), calls=%async_computation.6 | async-start | bytes 7864320 | tf_op jit(solution)/shard_map/all_gather | solution.py:44
  250.4 100.8 %reduce-scatter.5.cloned.1.call-start = ((), (), s32[]{:S(2)}) async-start(), calls=%async_computation.7 | async-start | bytes 1179648 | tf_op jit(solution)/shard_map/reduce_scatter | solution.py:58
  327.7 23.6 %copy-start.2 = (bf16[256,768]{1,0:T(8,128)(2,1)S(1)}, bf16[256,768]{1,0:T(8,128)(2,1)}, u32[]{:S(2)}) copy-start(bf16[256,768]{1,0:T(8,128)(2,1)} %param.11) | copy-start | bytes 1179652
  327.7 25.4 %copy-start.1 = (bf16[1,1536,128]{2,1,0:T(8,128)(2,1)S(1)}, bf16[1,1536,128]{2,1,0:T(8,128)(2,1)}, u32[]{:S(2)}) copy-start(bf16[1,1536,128]{2,1,0:T(8,128)(2,1)} %param.14) | copy-start | bytes 1179652
Sparse Core Ops, SparseCore 0:
  83.1 101.6 reduce-scatter.2
  246.5 15.8 all-gather.2
  264.6 43.6 all-gather.4
  327.8 14.6 reduce-scatter.4
where the time goes:
time: 360 us
  waiting for transfers between devices  160 us (44%)
  matrix products  102 us (28%)
  other arithmetic  49.2 us (14%)
  blocking collectives  28 us (8%)
  between operations  13.9 us (4%)
  starting transfers between devices  3.81 us (1%)
    reduce_scatter x1, waiting for transfers between devices, device_step(): proj_rows = lax.psum_scatter(part_sum, 'x', scatter_dimension=0, tiled=True)  102 us
    dot_general x4, matrix products, device_step(): jnp.dot(normed, weight[layer_idx], preferred_element_type=jnp.float32)  44 us
    all_gather x1, waiting for transfers between devices, device_step(): mlp_rows = lax.all_gather(mlp_act, 'x', axis=0, tiled=True)  40.1 us
    select_n x1, other arithmetic, device_step(): new_v = jnp.where(slot_hit, kv_new[:, None, head_dim:], v_cache[layer_idx])  23.5 us
    dot_general x1, matrix products, device_step(): jnp.dot(mlp_rows, w_down[layer_idx], preferred_element_type=jnp.float32)  19.4 us
    dot_general x1, matrix products, device_step(): jnp.einsum('bhd,bsd->bhs', query_heads, new_k, preferred_element_type=jnp...  18 us
    dot_general x1, matrix products, device_step(): jnp.einsum('bhs,bsd->bhd', probs_bf, new_v, preferred_element_type=jnp.fl...  14.8 us
    all_gather x1, blocking collectives, device_step(): feat_rows = lax.all_gather(hidden, 'yz', axis=1, tiled=True)  13.1 us
  transfers between devices with their start and end apart: 5, of which 4 were waited for; matrix products, arithmetic and copies ran while one was open for 9% of the time, Pallas kernels for 0%

commit v1 on v0

v1 whole, which is shorter than its diff:
```python
import functools

import jax
import jax.numpy as jnp
from jax import lax
from jax.experimental import pallas as pl
from jax.experimental.pallas import tpu as pltpu
from jax.sharding import PartitionSpec as P

NORM_EPS = 1e-6
W = 512
NBUF1 = 4
NBUF3 = 10
EARLY = 10
SEQ_STEP = 2
VMEM_LIMIT = 64_000_000
F32 = jnp.float32
BF16 = jnp.bfloat16
LOG2E = 1.4426950408889634
MASKED = -1e30


def dev(**axes):
    return dict(device_id=axes, device_id_type=pl.DeviceIdType.MESH)


def silu_mul(gate, up):
    gate = gate.astype(BF16).astype(F32)
    up = up.astype(BF16).astype(F32)
    return (jax.nn.silu(gate) * up).astype(BF16)


def project_kernel(
    n_q, n_ff, d_model, hidden, gain, wq, wkv, wg, wu,
    qkv_out, m_out, keep_out, send_out,
    h_other, u, sq_all, wbuf, wkv_buf, part, part_kv, near, near_kv, keep, keep_kv, far_src, far_src_kv,
    far, far_kv, z_rows, z_other,
    w_sem, wkv_sem, h_sems, sq_send, sq_recv, near_send, near_recv, far_send, far_recv, y_sems, out_sem,
):
    xi = lax.axis_index("x")
    yj = lax.axis_index("yz")
    core = lax.rem(xi, 2)
    chip = xi // 2
    mate = xi + 1 - 2 * core
    across = lax.rem(xi + 2, 4)
    other_y = 1 - yj
    me = xi * 2 + yj
    half = hidden.shape[1]
    n_all = n_q + n_ff

    def weight_copies(g, slot):
        return g, slot

    def start_weights(g):
        slot = lax.rem(g, NBUF1)

        @pl.when(g < n_q)
        def _():
            for k in range(2):
                cols = pl.ds(pl.multiple_of((2 * g + k) * W, W), W)
                pltpu.make_async_copy(wq.at[0, :, cols], wbuf.at[slot, k], w_sem.at[slot, k]).start()

        @pl.when(g >= n_q)
        def _():
            cols = pl.ds(pl.multiple_of((g - n_q) * W, W), W)
            pltpu.make_async_copy(wg.at[0, :, cols], wbuf.at[slot, 0], w_sem.at[slot, 0]).start()
            pltpu.make_async_copy(wu.at[0, :, cols], wbuf.at[slot, 1], w_sem.at[slot, 1]).start()

    for g in range(NBUF1):
        start_weights(jnp.int32(g))
    kv_copy = pltpu.make_async_copy(wkv.at[0], wkv_buf, wkv_sem)
    kv_copy.start()

    barrier = pltpu.get_barrier_semaphore()
    for k in range(1, 8):
        peer = lax.rem(me + k, 8)
        pl.semaphore_signal(barrier, inc=1, **dev(x=peer // 2, yz=lax.rem(peer, 2)))
    pl.semaphore_wait(barrier, 7)

    h_copy = pltpu.make_async_remote_copy(
        src_ref=hidden, dst_ref=h_other, send_sem=h_sems.at[0], recv_sem=h_sems.at[1], **dev(x=xi, yz=other_y))
    h_copy.start()

    h_f32 = hidden[...].astype(F32)
    sq_all[me] = lax.dot_general(
        jnp.ones((8, half), F32), h_f32 * h_f32, (((1,), (1,)), ((), ())),
        precision=lax.Precision.HIGHEST, preferred_element_type=F32)

    def sq_copy(peer, src):
        return pltpu.make_async_remote_copy(
            src_ref=sq_all.at[src], dst_ref=sq_all.at[src], send_sem=sq_send.at[peer], recv_sem=sq_recv.at[src],
            **dev(x=peer // 2, yz=lax.rem(peer, 2)))

    for k in range(1, 8):
        sq_copy(lax.rem(me + k, 8), me).start()
    for k in range(1, 8):
        peer = lax.rem(me + k, 8)
        sq_copy(peer, peer).wait_recv()
    total = jnp.sum(sq_all[...], axis=0)
    inv = lax.rsqrt(total / d_model + NORM_EPS)
    inv_col = jnp.transpose(jnp.concatenate([inv] * 16, axis=0))[:, :1]

    def norm_half(values, which):
        cols = pl.ds(pl.multiple_of(which * half, 128), half)
        u[:, cols] = (values.astype(F32) * inv_col * gain[:, cols].astype(F32)).astype(BF16)

    norm_half(hidden[...], yj)
    h_copy.wait_recv()
    norm_half(h_other[...], other_y)

    def near_copy(g):
        return pltpu.make_async_remote_copy(
            src_ref=part.at[g, :, 1 - core], dst_ref=near.at[g], send_sem=near_send.at[g], recv_sem=near_recv.at[g],
            **dev(x=mate, yz=yj))

    def near_copy_kv():
        return pltpu.make_async_remote_copy(
            src_ref=part_kv.at[:, 1 - core], dst_ref=near_kv, send_sem=near_send.at[n_all],
            recv_sem=near_recv.at[n_all], **dev(x=mate, yz=yj))

    def far_copy(g):
        return pltpu.make_async_remote_copy(
            src_ref=far_src.at[g], dst_ref=far.at[g], send_sem=far_send.at[g], recv_sem=far_recv.at[g],
            **dev(x=across, yz=yj))

    def far_copy_kv():
        return pltpu.make_async_remote_copy(
            src_ref=far_src_kv, dst_ref=far_kv, send_sem=far_send.at[n_q + EARLY],
            recv_sem=far_recv.at[n_q + EARLY], **dev(x=across, yz=yj))

    def out_copies(g):
        k = g - (n_q + EARLY)
        return (
            pltpu.make_async_copy(keep.at[g], keep_out.at[k], out_sem.at[k, 0]),
            pltpu.make_async_copy(far_src.at[g], send_out.at[k], out_sem.at[k, 1]),
        )

    def multiply(g):
        slot = lax.rem(g, NBUF1)
        for k in range(2):
            pltpu.make_async_copy(wq.at[0, :, pl.ds(0, W)], wbuf.at[slot, k], w_sem.at[slot, k]).wait()
            res = jnp.dot(u[...], wbuf[slot, k], preferred_element_type=F32).astype(BF16)
            part[g, :, :, :, k * W:(k + 1) * W] = res.reshape(2, 2, 64, W)
        near_copy(g).start()

        @pl.when(g + NBUF1 < n_all)
        def _():
            start_weights(g + NBUF1)

    def reduce_near(g, send):
        near_copy(g).wait_recv()
        keep[g] = (part[g, chip, core].astype(F32) + near[g, chip].astype(F32)).astype(BF16)
        far_src[g] = (part[g, 1 - chip, core].astype(F32) + near[g, 1 - chip].astype(F32)).astype(BF16)
        if send:
            far_copy(g).start()
        else:
            for copy in out_copies(g):
                copy.start()

    @pl.loop(0, n_q)
    def _(g):
        multiply(g)

        @pl.when(g >= 1)
        def _():
            reduce_near(g - 1, True)

    kv_copy.wait()
    res = jnp.dot(u[...], wkv_buf[...], preferred_element_type=F32).astype(BF16)
    part_kv[...] = res.reshape(2, 2, 64, res.shape[1])
    near_copy_kv().start()
    reduce_near(n_q - 1, True)
    near_copy_kv().wait_recv()
    keep_kv[...] = (part_kv[chip, core].astype(F32) + near_kv[chip].astype(F32)).astype(BF16)
    far_src_kv[...] = (part_kv[1 - chip, core].astype(F32) + near_kv[1 - chip].astype(F32)).astype(BF16)
    far_copy_kv().start()

    @pl.loop(n_q, n_q + EARLY)
    def _(g):
        multiply(g)

        @pl.when(g >= n_q + 1)
        def _():
            reduce_near(g - 1, True)

    q_cols = n_q * 2 * W
    for g in range(n_q):
        far_copy(g).wait_recv()
        z = (keep[g].astype(F32) + far[g].astype(F32)).astype(BF16)
        z_rows[:, :, g * 2 * W:(g + 1) * 2 * W] = z.reshape(2, 32, 2 * W)
    far_copy_kv().wait_recv()
    z = (keep_kv[...].astype(F32) + far_kv[...].astype(F32)).astype(BF16)
    z_rows[:, :, q_cols:] = z.reshape(2, 32, z.shape[1])
    y_copy = pltpu.make_async_remote_copy(
        src_ref=z_rows.at[other_y], dst_ref=z_other, send_sem=y_sems.at[0], recv_sem=y_sems.at[1],
        **dev(x=xi, yz=other_y))
    y_copy.start()
    qkv_out[yj] = z_rows[yj]

    multiply(n_q + EARLY)
    reduce_near(n_q + EARLY - 1, True)

    @pl.loop(n_q + EARLY + 1, n_all)
    def _(g):
        multiply(g)
        reduce_near(g - 1, False)

    reduce_near(n_all - 1, False)
    y_copy.wait_recv()
    qkv_out[other_y] = z_other[...]

    @pl.loop(n_q, n_q + EARLY)
    def _(g):
        far_copy(g).wait_recv()
        z = keep[g].astype(F32) + far[g].astype(F32)
        m_out[g - n_q] = silu_mul(z[:, :W], z[:, W:])

    h_copy.wait_send()
    for k in range(1, 8):
        sq_copy(lax.rem(me + k, 8), me).wait_send()
    y_copy.wait_send()
    near_copy_kv().wait_send()
    far_copy_kv().wait_send()

    @pl.loop(0, n_all)
    def _(g):
        near_copy(g).wait_send()

    @pl.loop(0, n_q + EARLY)
    def _(g):
        far_copy(g).wait_send()

    @pl.loop(n_q + EARLY, n_all)
    def _(g):
        for copy in out_copies(g):
            copy.wait()


def project(hidden, gain, w_q, w_kv, w_gate, w_up, d_model):
    rows, half = hidden.shape
    feats = w_q.shape[1]
    kv = w_kv.shape[2]
    n_q = w_q.shape[2] // (2 * W)
    n_ff = w_gate.shape[2] // W
    n_all = n_q + n_ff
    n_far = n_q + EARLY
    late = n_ff - EARLY
    dma = pltpu.SemaphoreType.DMA
    any_spec = pl.BlockSpec(memory_space=pl.ANY)
    vmem = pl.BlockSpec(memory_space=pltpu.VMEM)
    cols = w_q.shape[2] + kv
    flops = 2 * rows * feats * (w_q.shape[2] + kv + 2 * w_gate.shape[2])
    return pl.pallas_call(
        functools.partial(project_kernel, n_q, n_ff, d_model),
        name="project",
        out_shape=(
            jax.ShapeDtypeStruct((2, 32, cols), BF16),
            jax.ShapeDtypeStruct((EARLY, 64, W), BF16),
            jax.ShapeDtypeStruct((late, 64, 2 * W), BF16),
            jax.ShapeDtypeStruct((late, 64, 2 * W), BF16),
        ),
        in_specs=[vmem, vmem, any_spec, any_spec, any_spec, any_spec],
        out_specs=(vmem, vmem, any_spec, any_spec),
        scratch_shapes=[
            pltpu.VMEM((rows, half), BF16),
            pltpu.VMEM((rows, feats), BF16),
            pltpu.VMEM((8, 8, rows), F32),
            pltpu.VMEM((NBUF1, 2, feats, W), BF16),
            pltpu.VMEM((feats, kv), BF16),
            pltpu.VMEM((n_all, 2, 2, 64, 2 * W), BF16),
            pltpu.VMEM((2, 2, 64, kv), BF16),
            pltpu.VMEM((n_all, 2, 64, 2 * W), BF16),
            pltpu.VMEM((2, 64, kv), BF16),
            pltpu.VMEM((n_all, 64, 2 * W), BF16),
            pltpu.VMEM((64, kv), BF16),
            pltpu.VMEM((n_all, 64, 2 * W), BF16),
            pltpu.VMEM((64, kv), BF16),
            pltpu.VMEM((n_far, 64, 2 * W), BF16),
            pltpu.VMEM((64, kv), BF16),
            pltpu.VMEM((2, 32, cols), BF16),
            pltpu.VMEM((32, cols), BF16),
            dma((NBUF1, 2)),
            dma,
            dma((2,)),
            dma((8,)),
            dma((8,)),
            dma((n_all + 1,)),
            dma((n_all + 1,)),
            dma((n_far + 1,)),
            dma((n_far + 1,)),
            dma((2,)),
            dma((late, 2)),
        ],
        compiler_params=pltpu.CompilerParams(collective_id=0, has_side_effects=True, vmem_limit_bytes=VMEM_LIMIT),
        cost_estimate=pl.CostEstimate(flops=flops, bytes_accessed=feats * (flops // (rows * feats)), transcendentals=0),
    )(hidden, gain, w_q, w_kv, w_gate, w_up)


def attend_kernel(lens, q_ref, kv_ref, k_ref, v_ref, k_out, v_out, o_ref):
    step = pl.program_id(0)
    n_pos = k_ref.shape[2]
    scale = q_ref.shape[2] ** -0.5 * LOG2E
    for s in range(SEQ_STEP):
        length = lens[step * SEQ_STEP + s]
        base = pl.multiple_of((length // 16) * 16, 16)
        k_out[0, s] = k_ref[0, s]
        v_out[0, s] = v_ref[0, s]
        hit = lax.broadcasted_iota(jnp.int32, (16, k_ref.shape[3]), 0) == length - base
        for src, dst, which in ((k_ref, k_out, 0), (v_ref, v_out, 1)):
            old = src[0, s, pl.ds(base, 16), :].astype(F32)
            new = kv_ref[s, which:which + 1, :].astype(F32)
            dst[0, s, pl.ds(base, 16), :] = jnp.where(hit, new, old).astype(BF16)
        scores = lax.dot_general(q_ref[s], k_out[0, s], (((1,), (1,)), ((), ())), preferred_element_type=F32) * scale
        visible = lax.broadcasted_iota(jnp.int32, scores.shape, 1) <= length
        scores = jnp.where(visible, scores, MASKED)
        weights = jnp.exp2(scores - jnp.max(scores, axis=1, keepdims=True))
        probs = (weights * (1.0 / jnp.sum(weights, axis=1, keepdims=True))).astype(BF16)
        o_ref[s] = jnp.dot(probs, v_out[0, s], preferred_element_type=F32).astype(BF16)


def attend(lens, q, kv, k_cache, v_cache):
    seqs, heads, dim = q.shape
    n_pos = k_cache.shape[2]
    cache_spec = pl.BlockSpec((1, SEQ_STEP, n_pos, dim), lambda b, lens: (0, b, 0, 0))
    q_spec = pl.BlockSpec((SEQ_STEP, heads, dim), lambda b, lens: (b, 0, 0))
    return pl.pallas_call(
        attend_kernel,
        name="attend",
        out_shape=(
            jax.ShapeDtypeStruct(k_cache.shape, BF16),
            jax.ShapeDtypeStruct(v_cache.shape, BF16),
            jax.ShapeDtypeStruct(q.shape, BF16),
        ),
        grid_spec=pltpu.PrefetchScalarGridSpec(
            num_scalar_prefetch=1,
            grid=(seqs // SEQ_STEP,),
            in_specs=[q_spec, pl.BlockSpec((SEQ_STEP, 2, dim), lambda b, lens: (b, 0, 0)), cache_spec, cache_spec],
            out_specs=(cache_spec, cache_spec, q_spec),
        ),
        compiler_params=pltpu.CompilerParams(dimension_semantics=("arbitrary",), vmem_limit_bytes=40_000_000),
        cost_estimate=pl.CostEstimate(
            flops=10**10, bytes_accessed=8 * k_cache.size, transcendentals=seqs * heads * n_pos),
    )(lens, q, kv, k_cache, v_cache)


def output_kernel(
    n_ff, n_o, o_in, m_in, keep, recv, hidden, w_o, w_down, out,
    acts, wbuf, acc, y_src, y_dst,
    w_sem, o_sems, far_send, far_recv, near_send, near_recv, y_sems,
):
    xi = lax.axis_index("x")
    yj = lax.axis_index("yz")
    core = lax.rem(xi, 2)
    mate = xi + 1 - 2 * core
    across = lax.rem(xi + 2, 4)
    other_y = 1 - yj
    n_m2 = n_ff // 2
    n2 = n_m2 + n_o // 2
    d_out = w_down.shape[2]
    half = d_out // 2

    def start_weights(g):
        slot = lax.rem(g, NBUF3)

        @pl.when(g < n_m2)
        def _():
            pltpu.make_async_copy(
                w_down.at[0, pl.ds(pl.multiple_of(g * 2 * W, W), 2 * W)], wbuf.at[slot], w_sem.at[slot]).start()

        @pl.when(g >= n_m2)
        def _():
            pltpu.make_async_copy(
                w_o.at[0, pl.ds(pl.multiple_of((g - n_m2) * 2 * W, W), 2 * W)], wbuf.at[slot], w_sem.at[slot]).start()

    for g in range(NBUF3):
        start_weights(jnp.int32(g))

    barrier = pltpu.get_barrier_semaphore()
    for x_, y_ in ((mate, yj), (across, yj), (xi, other_y)):
        pl.semaphore_signal(barrier, inc=1, **dev(x=x_, yz=y_))
    pl.semaphore_wait(barrier, 3)

    def rows_of(block):
        return pl.ds(pl.multiple_of(block * 64, 64), 64)

    def o_rows(j):
        return acts.at[pl.ds(n_ff, n_o), pl.ds(pl.multiple_of(xi * 64 + j * 32, 32), 32)]

    o_copy = pltpu.make_async_remote_copy(
        src_ref=o_in.at[other_y], dst_ref=o_rows(yj), send_sem=o_sems.at[0], recv_sem=o_sems.at[1],
        **dev(x=xi, yz=other_y))
    o_copy.start()

    def far_copy(g):
        block = acts.at[pl.ds(2 * g, 2), rows_of(xi)]
        return pltpu.make_async_remote_copy(
            src_ref=block, dst_ref=block, send_sem=far_send.at[g], recv_sem=far_recv.at[g], **dev(x=across, yz=yj))

    def near_copy(g, which):
        block = acts.at[pl.ds(2 * g, 2), rows_of(xi if which == 0 else across)]
        return pltpu.make_async_remote_copy(
            src_ref=block, dst_ref=block, send_sem=near_send.at[g, which], recv_sem=near_recv.at[g, which],
            **dev(x=mate, yz=yj))

    def give(g):
        far_copy(g).start()
        near_copy(g, 0).start()

    @pl.loop(0, EARLY // 2)
    def _(g):
        for k in range(2):
            acts[2 * g + k, rows_of(xi)] = m_in[2 * g + k]
        give(g)

    @pl.loop(EARLY // 2, n_m2)
    def _(g):
        for k in range(2):
            t = 2 * g + k - EARLY
            z = keep[t].astype(F32) + recv[t].astype(F32)
            acts[2 * g + k, rows_of(xi)] = silu_mul(z[:, :W], z[:, W:])
        give(g)

    for k in range(n_o):
        acts[n_ff + k, pl.ds(pl.multiple_of(xi * 64 + yj * 32, 32), 32)] = o_in[yj, k]
    o_copy.wait_recv()

    @pl.loop(n_m2, n2)
    def _(g):
        give(g)

    acc[...] = jnp.zeros_like(acc)

    def forward(g):
        far_copy(g).wait_recv()
        near_copy(g, 1).start()

    def multiply(g):
        slot = lax.rem(g, NBUF3)
        pltpu.make_async_copy(w_down.at[0, pl.ds(0, 2 * W)], wbuf.at[slot], w_sem.at[slot]).wait()
        near_copy(g, 0).wait_recv()
        near_copy(g, 1).wait_recv()
        for n in range(d_out // W):
            cols = slice(n * W, (n + 1) * W)
            acc[:, cols] += jnp.dot(acts[2 * g], wbuf[slot, :W, cols], preferred_element_type=F32) + jnp.dot(
                acts[2 * g + 1], wbuf[slot, W:, cols], preferred_element_type=F32)

        @pl.when(g + NBUF3 < n2)
        def _():
            start_weights(g + NBUF3)

    forward(0)

    @pl.loop(1, n2)
    def _(g):
        forward(g)
        multiply(g - 1)

    multiply(n2 - 1)

    def cols_of(j):
        return pl.ds(pl.multiple_of(j * half, 128), half)

    y_src[...] = acc[:, cols_of(other_y)].astype(BF16)
    y_copy = pltpu.make_async_remote_copy(
        src_ref=y_src, dst_ref=y_dst, send_sem=y_sems.at[0], recv_sem=y_sems.at[1], **dev(x=xi, yz=other_y))
    y_copy.start()
    acc[:, cols_of(yj)] += hidden[...].astype(F32)
    y_copy.wait_recv()
    out[...] = (acc[:, cols_of(yj)] + y_dst[...].astype(F32)).astype(BF16)

    y_copy.wait_send()
    o_copy.wait_send()

    @pl.loop(0, n2)
    def _(g):
        far_copy(g).wait_send()
        near_copy(g, 0).wait_send()
        near_copy(g, 1).wait_send()


def finish(o, m_early, keep, recv, hidden, w_o, w_down):
    rows, half = hidden.shape
    n_ff = w_down.shape[1] // W
    n_o = w_o.shape[1] // W
    n2 = (n_ff + n_o) // 2
    d_out = w_down.shape[2]
    dma = pltpu.SemaphoreType.DMA
    any_spec = pl.BlockSpec(memory_space=pl.ANY)
    vmem = pl.BlockSpec(memory_space=pltpu.VMEM)
    flops = 2 * rows * d_out * (w_down.shape[1] + w_o.shape[1])
    return pl.pallas_call(
        functools.partial(output_kernel, n_ff, n_o),
        name="finish",
        out_shape=jax.ShapeDtypeStruct((rows, half), BF16),
        in_specs=[vmem, vmem, vmem, vmem, vmem, any_spec, any_spec],
        out_specs=vmem,
        scratch_shapes=[
            pltpu.VMEM((n_ff + n_o, rows, W), BF16),
            pltpu.VMEM((NBUF3, 2 * W, d_out), BF16),
            pltpu.VMEM((rows, d_out), F32),
            pltpu.VMEM((rows, half), BF16),
            pltpu.VMEM((rows, half), BF16),
            dma((NBUF3,)),
            dma((2,)),
            dma((n2,)),
            dma((n2,)),
            dma((n2, 2)),
            dma((n2, 2)),
            dma((2,)),
        ],
        compiler_params=pltpu.CompilerParams(collective_id=1, has_side_effects=True, vmem_limit_bytes=VMEM_LIMIT),
        cost_estimate=pl.CostEstimate(flops=flops, bytes_accessed=2 * d_out * (w_down.shape[1] + w_o.shape[1]), transcendentals=0),
    )(o, m_early, keep, recv, hidden, w_o, w_down)


def solution(mesh):
    x_size = mesh.shape["x"]
    y_size = mesh.shape["yz"]
    row_spec = P("dp", ("x", "yz"))
    tile_in = P(None, "x", "yz")
    tile_out = P(None, "yz", "x")
    cache_spec = P(None, ("dp", "x", "yz"))
    len_spec = P(("dp", "x", "yz"))

    def device_step(hidden, norm_gain, w_q, w_kv, w_gate, w_up, w_o, w_down, k_cache, v_cache, seq_len):
        d_model = hidden.shape[1] * x_size * y_size
        seqs = k_cache.shape[1]
        dim = k_cache.shape[3]
        q_cols = w_q.shape[2]
        heads = q_cols // dim
        qkv, m_early, keep, send = project(hidden, norm_gain, w_q, w_kv, w_gate, w_up, d_model)
        recv = lax.ppermute(send, "x", [(i, (i + x_size // 2) % x_size) for i in range(x_size)])
        q = qkv[:, :, :q_cols].reshape(y_size, seqs, heads, dim).transpose(1, 0, 2, 3).reshape(seqs, y_size * heads, dim)
        kv = qkv[:, :, q_cols:].transpose(1, 0, 2)
        k_new, v_new, o = attend(seq_len, q, kv, k_cache, v_cache)
        o = o.reshape(seqs, y_size, q_cols // W, W).transpose(1, 2, 0, 3)
        hidden_out = finish(o, m_early, keep, recv, hidden, w_o, w_down)
        return hidden_out, k_new, v_new

    return jax.shard_map(
        device_step,
        mesh=mesh,
        in_specs=(row_spec, P(None, "x"), tile_in, tile_in, tile_in, tile_in, tile_out, tile_out, cache_spec, cache_spec, len_spec),
        out_specs=(row_spec, cache_spec, cache_spec),
        check_vma=False,
    )
```

time: 360 us -> 168 us (0.47)
  waiting for transfers between devices: 160 us -> 6.93 us
  Pallas kernels: 0 us -> 152 us
  matrix products: 102 us -> 0 us
  other arithmetic: 49.2 us -> 0 us
  blocking collectives: 28 us -> 0 us
  between operations: 13.9 us -> 0.7 us
  local copies, waits for them, and re-layouts: 2.77 us -> 6.65 us
    pallas_call x0 -> x3, Pallas kernels: none -> 152 us  [the longest x1 62.4 us: finish(): pl.pallas_call(functools.partial(output_kernel, n_ff, n_o), name='finish'...]
    reduce_scatter x2 -> x0, waiting for transfers between devices: 102 us -> none  [the longest x1 102 us: device_step(): proj_rows = lax.psum_scatter(part_sum, 'x', scatter_dimension=0, tiled=True)]
    dot_general x8 -> x0, matrix products: 102 us -> none  [the longest x4 44 us: device_step(): jnp.dot(normed, weight[layer_idx], preferred_element_type=jnp.float32)]
    all_gather x2 -> x0, waiting for transfers between devices: 52.1 us -> none  [the longest x1 40.1 us: device_step(): mlp_rows = lax.all_gather(mlp_act, 'x', axis=0, tiled=True)]
    select_n x1 -> x0, other arithmetic: 23.5 us -> none  [device_step(): new_v = jnp.where(slot_hit, kv_new[:, None, head_dim:], v_cache[layer_idx])]
    all_gather x1 -> x0, blocking collectives: 13.1 us -> none  [device_step(): feat_rows = lax.all_gather(hidden, 'yz', axis=1, tiled=True)]
    concatenate x1 -> x0, other arithmetic: 11.6 us -> none  [device_step(): jnp.concatenate([jnp.dot(normed, weight[layer_idx], preferred_element_typ...]
    all_to_all x1 -> x0, blocking collectives: 8.88 us -> none  [device_step(): lax.all_to_all(attn_out.reshape(local_seqs, n_heads * head_dim), 'yz', 1,...]
  transfers between devices with their start and end apart: 5 -> 1, of which waited for: 4 -> 1; matrix products, arithmetic and copies ran while one was open for 9% -> 2% of each run, Pallas kernels for 0% -> 18%
where the time goes in v1:
time: 168 us
  Pallas kernels  152 us (90%)
  waiting for transfers between devices  6.93 us (4%)
  local copies, waits for them, and re-layouts  6.65 us (4%)
    pallas_call x1, Pallas kernels, finish(): pl.pallas_call(functools.partial(output_kernel, n_ff, n_o), name='finish'...  62.4 us
    pallas_call x1, Pallas kernels, project(): pl.pallas_call(functools.partial(project_kernel, n_q, n_ff, d_model), nam...  60 us
    pallas_call x1, Pallas kernels, attend(): pl.pallas_call(attend_kernel, name='attend', out_shape=(jax.ShapeDtypeStr...  29.6 us
    ppermute x1, waiting for transfers between devices, device_step(): lax.ppermute(send, 'x', [(i, (i + x_size // 2) % x_size) for i in range(x...  6.93 us
  transfers between devices with their start and end apart: 1, of which 1 were waited for; matrix products, arithmetic and copies ran while one was open for 2% of the time, Pallas kernels for 18%

profile of v1, /device:TPU:0, one launch (start us, length us, event | category | flops | bytes accessed | tf_op | source)
XLA Modules:
  0.0 167.8 jit_solution(9605617563770732484)
XLA Ops:
  0.6 0.0 copy-start
  0.6 60.0 %project.1 = (bf16[2,32,3200]{2,1,0:T(8,128)(2,1)}, bf16[10,64,512]{2,1,0:T(8,128)(2,1)}, bf16[14,64,1024]{2,1,0:T(8,128)(2,1)}, bf16[14,64,1024]{2,1,0:T(8,128)(2,1)}) custom-call(bf16[256,768]{1,0:T(8,128)(2,1)} %hidden.3, bf16[1,1536]{1,0:T(2,128)(2,1)} %gain.1, bf16[1,1536,3072]{2,1,0:T(8,128)(2,1)} %wq.1, bf16[1,1536,128]{2,1,0:T(8,128)(2,1)} %wkv.1, ...), custom_call_target="tpu_custom_call" | custom-call | flops 21843935232 | bytes 85327872 | tf_op jit(solution)/shard_map/project/pallas_call | solution.py:253
  60.6 1.5 collective-permute-start
  62.2 1.0 slice.6
  63.2 1.3 copy.17
  64.5 0.1 copy.19
  64.6 0.0 copy-done
  64.7 29.6 %attend.1 = (bf16[1,32,2048,128]{3,2,1,0:T(8,128)(2,1)}, bf16[1,32,2048,128]{3,2,1,0:T(8,128)(2,1)}, bf16[32,48,128]{2,1,0:T(8,128)(2,1)S(1)}) custom-call(s32[32]{0:T(128)S(1)} %copy-done, bf16[32,48,128]{2,1,0:T(8,128)(2,1)S(1)} %bitcast.12, bf16[32,2,128]{2,1,0:T(2,128)(2,1)S(1)} %slice_bitcast_fusion.kv_ref, bf16[1,32,2048,128]{3,2,1,0:T(8,128)(2,1)} %k_ref.1, ...), custom_call_target="tpu_custom_call" | custom-call | flops 10000000000 | bytes 67108864 | tf_op jit(solution)/shard_map/attend/pallas_call | solution.py:326
  94.3 0.2 reshape.17
  94.5 1.0 copy.21
  95.5 6.9 %collective-permute-done.recv = bf16[14,64,1024]{2,1,0:T(8,128)(2,1)S(1)} collective-permute-done((bf16[14,64,1024]{2,1,0:T(8,128)(2,1)}, bf16[14,64,1024]{2,1,0:T(8,128)(2,1)S(1)}, u32[]{:S(2)}, u32[]{:S(2)}) %collective-permute-start) | collective-permute-done | bytes 1835040 | tf_op jit(solution)/shard_map/ppermute | solution.py:532
  102.4 0.0 copy-start.1
  102.4 1.2 copy-done.1
  103.6 62.4 %finish.1 = bf16[256,768]{1,0:T(8,128)(2,1)} custom-call(bf16[2,6,32,512]{3,2,1,0:T(8,128)(2,1)} %bitcast.13, bf16[10,64,512]{2,1,0:T(8,128)(2,1)} %get-tuple-element.12.m_in, bf16[14,64,1024]{2,1,0:T(8,128)(2,1)} %get-tuple-element.13.keep, bf16[14,64,1024]{2,1,0:T(8,128)(2,1)} %copy-done.1, bf16[256,768]{1,0:T(8,128)(2,1)} %hidden.3, ...), custom_call_target="tpu_custom_call" | custom-call | flops 12079595520 | bytes 47185920 | tf_op jit(solution)/shard_map/finish/pallas_call | solution.py:491
  166.0 1.8 %copy.23 = bf16[256,768]{1,0:T(8,128)(2,1)} copy(bf16[256,768]{1,0:T(8,128)(2,1)} %finish.1) | data formatting | bytes 786432
  (2 shorter events, 0.1 us)
Async XLA Ops:
  0.6 64.0 %copy-start = (s32[32]{0:T(128)S(1)}, s32[32]{0:T(128)}, u32[]{:S(2)}) copy-start(s32[32]{0:T(128)} %lens.1) | copy-start | bytes 388
  60.6 41.7 %collective-permute-start = (bf16[14,64,1024]{2,1,0:T(8,128)(2,1)}, bf16[14,64,1024]{2,1,0:T(8,128)(2,1)S(1)}, u32[]{:S(2)}, u32[]{:S(2)}) collective-permute-start(bf16[14,64,1024]{2,1,0:T(8,128)(2,1)} %get-tuple-element.14), channel_id=1, source_target_pairs={{0,2},{1,3},{2,0},{3,1},{4,6},{5,7},{6,4},{7,5}} | collective-permute-start | bytes 5505032 | tf_op jit(solution)/shard_map/ppermute | solution.py:532
  102.4 1.2 copy-start.1

commit v2 on v1

v2 whole, which is shorter than its diff:
```python
import functools

import jax
import jax.numpy as jnp
from jax import lax
from jax.experimental import pallas as pl
from jax.experimental.pallas import tpu as pltpu
from jax.sharding import PartitionSpec as P

NORM_EPS = 1e-6
W = 512
NBUF1 = 4
NBUF3 = 6
GROUP = 3
EARLY = 12
SEQ_STEP = 2
VMEM_LIMIT = 64_000_000
F32 = jnp.float32
BF16 = jnp.bfloat16
LOG2E = 1.4426950408889634
MASKED = -1e30


def dev(**axes):
    return dict(device_id=axes, device_id_type=pl.DeviceIdType.MESH)


def silu_mul(gate, up):
    gate = gate.astype(BF16).astype(F32)
    up = up.astype(BF16).astype(F32)
    return (jax.nn.silu(gate) * up).astype(BF16)


def project_kernel(
    n_q, n_ff, d_model, hidden, gain, wq, wkv, wg, wu,
    qkv_out, m_out, keep_out, send_out,
    h_other, u, inv_all, sq_all, wbuf, wkv_buf, part, part_kv, near, near_kv, keep, keep_kv, far_src, far_src_kv,
    far, far_kv, z_rows, z_other, m_rows,
    w_sem, wkv_sem, h_sems, sq_send, sq_recv, near_send, near_recv, far_send, far_recv, y_sems, out_sem, m_sem, qkv_sem,
):
    xi = lax.axis_index("x")
    yj = lax.axis_index("yz")
    core = lax.rem(xi, 2)
    chip = xi // 2
    mate = xi + 1 - 2 * core
    across = lax.rem(xi + 2, 4)
    other_y = 1 - yj
    me = xi * 2 + yj
    half = hidden.shape[1]
    n_all = n_q + n_ff
    n_far = n_q + EARLY

    barrier = pltpu.get_barrier_semaphore()
    for k in range(1, 8):
        peer = lax.rem(me + k, 8)
        pl.semaphore_signal(barrier, inc=1, **dev(x=peer // 2, yz=lax.rem(peer, 2)))

    def start_weights(g):
        slot = lax.rem(g, NBUF1)

        @pl.when(g < n_q)
        def _():
            for k in range(2):
                cols = pl.ds(pl.multiple_of((2 * g + k) * W, W), W)
                pltpu.make_async_copy(wq.at[0, :, cols], wbuf.at[slot, k], w_sem.at[slot, k]).start()

        @pl.when(g >= n_q)
        def _():
            cols = pl.ds(pl.multiple_of((g - n_q) * W, W), W)
            pltpu.make_async_copy(wg.at[0, :, cols], wbuf.at[slot, 0], w_sem.at[slot, 0]).start()
            pltpu.make_async_copy(wu.at[0, :, cols], wbuf.at[slot, 1], w_sem.at[slot, 1]).start()

    def wait_weights(slot, k):
        pltpu.make_async_copy(wq.at[0, :, pl.ds(0, W)], wbuf.at[slot, k], w_sem.at[slot, k]).wait()

    for g in range(NBUF1):
        start_weights(jnp.int32(g))
    kv_copy = pltpu.make_async_copy(wkv.at[0], wkv_buf, wkv_sem)
    kv_copy.start()

    h_f32 = hidden[...].astype(F32)
    sq_all[me] = lax.dot_general(
        jnp.ones((8, half), F32), h_f32 * h_f32, (((1,), (1,)), ((), ())),
        precision=lax.Precision.HIGHEST, preferred_element_type=F32)
    pl.semaphore_wait(barrier, 7)

    def sq_copy(peer, src):
        return pltpu.make_async_remote_copy(
            src_ref=sq_all.at[src], dst_ref=sq_all.at[src], send_sem=sq_send.at[peer], recv_sem=sq_recv.at[src],
            **dev(x=peer // 2, yz=lax.rem(peer, 2)))

    def rows_of(which):
        return pl.ds(pl.multiple_of((1 - chip if which == 0 else chip) * 128, 128), 128)

    def h_copy(which):
        return pltpu.make_async_remote_copy(
            src_ref=hidden.at[rows_of(which)], dst_ref=h_other.at[rows_of(which)],
            send_sem=h_sems.at[which, 0], recv_sem=h_sems.at[which, 1], **dev(x=xi, yz=other_y))

    for k in range(1, 8):
        sq_copy(lax.rem(me + k, 8), me).start()
    h_copy(0).start()
    h_copy(1).start()
    for k in range(1, 8):
        peer = lax.rem(me + k, 8)
        sq_copy(peer, peer).wait_recv()
    total = jnp.sum(sq_all[...], axis=0)
    inv = lax.rsqrt(total / d_model + NORM_EPS)
    inv_all[...] = jnp.transpose(jnp.concatenate([inv] * 16, axis=0))

    def normalize(values, rows, which):
        cols = pl.ds(pl.multiple_of(which * half, 128), half)
        u[rows, cols] = (
            values[rows].astype(F32) * inv_all[rows, :1] * gain[:, cols].astype(F32)).astype(BF16)

    def near_copy(g):
        return pltpu.make_async_remote_copy(
            src_ref=part.at[g, :, 1 - core], dst_ref=near.at[g], send_sem=near_send.at[g], recv_sem=near_recv.at[g],
            **dev(x=mate, yz=yj))

    def near_copy_q(g, which):
        side = 1 - chip if which == 0 else chip
        sem = g + which * (n_all + 1)
        return pltpu.make_async_remote_copy(
            src_ref=part.at[g, side, 1 - core], dst_ref=near.at[g, side], send_sem=near_send.at[sem],
            recv_sem=near_recv.at[sem], **dev(x=mate, yz=yj))

    def near_copy_kv(which):
        side = 1 - chip if which == 0 else chip
        sem = n_all + which * (n_q + 1)
        return pltpu.make_async_remote_copy(
            src_ref=part_kv.at[side, 1 - core], dst_ref=near_kv.at[side], send_sem=near_send.at[sem],
            recv_sem=near_recv.at[sem], **dev(x=mate, yz=yj))

    def far_copy(g):
        return pltpu.make_async_remote_copy(
            src_ref=far_src.at[g], dst_ref=far.at[g], send_sem=far_send.at[g], recv_sem=far_recv.at[g],
            **dev(x=across, yz=yj))

    def far_copy_kv():
        return pltpu.make_async_remote_copy(
            src_ref=far_src_kv, dst_ref=far_kv, send_sem=far_send.at[n_far],
            recv_sem=far_recv.at[n_far], **dev(x=across, yz=yj))

    def out_copies(g):
        k = g - n_far
        return (
            pltpu.make_async_copy(keep.at[g], keep_out.at[k], out_sem.at[k, 0]),
            pltpu.make_async_copy(far_src.at[g], send_out.at[k], out_sem.at[k, 1]),
        )

    def add(a, b):
        return (a.astype(F32) + b.astype(F32)).astype(BF16)

    def multiply(g):
        slot = lax.rem(g, NBUF1)
        for k in range(2):
            wait_weights(slot, k)
            res = jnp.dot(u[...], wbuf[slot, k], preferred_element_type=F32).astype(BF16)
            part[g, :, :, :, k * W:(k + 1) * W] = res.reshape(2, 2, 64, W)
        near_copy(g).start()

        @pl.when(g + NBUF1 < n_all)
        def _():
            start_weights(g + NBUF1)

    def reduce_near(g, send):
        near_copy(g).wait_recv()
        keep[g] = add(part[g, chip, core], near[g, chip])
        far_src[g] = add(part[g, 1 - chip, core], near[g, 1 - chip])
        if send:
            far_copy(g).start()
        else:
            for copy in out_copies(g):
                copy.start()

    for which in range(2):
        side = 1 - chip if which == 0 else chip
        rows = rows_of(which)
        normalize(hidden, rows, yj)
        h_copy(which).wait_recv()
        normalize(h_other, rows, other_y)

        def reduce_q(g):
            near_copy_q(g, which).wait_recv()
            total_q = add(part[g, side, core], near[g, side])
            if which == 0:
                far_src[g] = total_q
                far_copy(g).start()
            else:
                keep[g] = total_q

        for g in range(n_q):
            for k in range(2):
                if which == 0:
                    wait_weights(g, k)
                res = jnp.dot(u[rows], wbuf[g, k], preferred_element_type=F32).astype(BF16)
                part[g, side, :, :, k * W:(k + 1) * W] = res.reshape(2, 64, W)
            near_copy_q(g, which).start()
            if which == 1:
                start_weights(jnp.int32(g + NBUF1))
            if g >= 1:
                reduce_q(g - 1)
        if which == 0:
            kv_copy.wait()
        res = jnp.dot(u[rows], wkv_buf[...], preferred_element_type=F32).astype(BF16)
        part_kv[side] = res.reshape(2, 64, res.shape[1])
        near_copy_kv(which).start()
        reduce_q(n_q - 1)
        near_copy_kv(which).wait_recv()
        total_kv = add(part_kv[side, core], near_kv[side])
        if which == 0:
            far_src_kv[...] = total_kv
            far_copy_kv().start()
        else:
            keep_kv[...] = total_kv

    @pl.loop(n_q, n_far)
    def _(g):
        multiply(g)

        @pl.when(g >= n_q + 1)
        def _():
            reduce_near(g - 1, True)

    q_cols = n_q * 2 * W
    for g in range(n_q):
        far_copy(g).wait_recv()
        z_rows[:, :, g * 2 * W:(g + 1) * 2 * W] = add(keep[g], far[g]).reshape(2, 32, 2 * W)
    far_copy_kv().wait_recv()
    z_kv = add(keep_kv[...], far_kv[...])
    z_rows[:, :, q_cols:] = z_kv.reshape(2, 32, z_kv.shape[1])
    y_copy = pltpu.make_async_remote_copy(
        src_ref=z_rows.at[other_y], dst_ref=z_other, send_sem=y_sems.at[0], recv_sem=y_sems.at[1],
        **dev(x=xi, yz=other_y))
    y_copy.start()
    qkv_own = pltpu.make_async_copy(z_rows.at[yj], qkv_out.at[yj], qkv_sem.at[0])
    qkv_own.start()

    multiply(n_far)
    reduce_near(n_far - 1, True)

    @pl.loop(n_far + 1, n_all)
    def _(g):
        multiply(g)
        reduce_near(g - 1, False)

    reduce_near(n_all - 1, False)
    y_copy.wait_recv()
    qkv_other = pltpu.make_async_copy(z_other, qkv_out.at[other_y], qkv_sem.at[1])
    qkv_other.start()

    def m_copy(g):
        return pltpu.make_async_copy(m_rows.at[g - n_q], m_out.at[g - n_q], m_sem.at[g - n_q])

    @pl.loop(n_q, n_far)
    def _(g):
        far_copy(g).wait_recv()
        z = keep[g].astype(F32) + far[g].astype(F32)
        m_rows[g - n_q] = silu_mul(z[:, :W], z[:, W:])
        m_copy(g).start()

    for which in range(2):
        h_copy(which).wait_send()
        near_copy_kv(which).wait_send()
        for g in range(n_q):
            near_copy_q(g, which).wait_send()
    for k in range(1, 8):
        sq_copy(lax.rem(me + k, 8), me).wait_send()
    y_copy.wait_send()
    far_copy_kv().wait_send()
    qkv_own.wait()
    qkv_other.wait()

    @pl.loop(n_q, n_all)
    def _(g):
        near_copy(g).wait_send()

    @pl.loop(0, n_far)
    def _(g):
        far_copy(g).wait_send()

    @pl.loop(n_far, n_all)
    def _(g):
        for copy in out_copies(g):
            copy.wait()

    @pl.loop(n_q, n_far)
    def _(g):
        m_copy(g).wait()


def project(hidden, gain, w_q, w_kv, w_gate, w_up, d_model):
    rows, half = hidden.shape
    feats = w_q.shape[1]
    kv = w_kv.shape[2]
    n_q = w_q.shape[2] // (2 * W)
    n_ff = w_gate.shape[2] // W
    n_all = n_q + n_ff
    n_far = n_q + EARLY
    late = n_ff - EARLY
    dma = pltpu.SemaphoreType.DMA
    any_spec = pl.BlockSpec(memory_space=pl.ANY)
    vmem = pl.BlockSpec(memory_space=pltpu.VMEM)
    cols = w_q.shape[2] + kv
    flops = 2 * rows * feats * (w_q.shape[2] + kv + 2 * w_gate.shape[2])
    return pl.pallas_call(
        functools.partial(project_kernel, n_q, n_ff, d_model),
        name="project",
        out_shape=(
            jax.ShapeDtypeStruct((2, 32, cols), BF16),
            jax.ShapeDtypeStruct((EARLY, 64, W), BF16),
            jax.ShapeDtypeStruct((late, 64, 2 * W), BF16),
            jax.ShapeDtypeStruct((late, 64, 2 * W), BF16),
        ),
        in_specs=[vmem, vmem, any_spec, any_spec, any_spec, any_spec],
        out_specs=(any_spec, any_spec, any_spec, any_spec),
        scratch_shapes=[
            pltpu.VMEM((rows, half), BF16),
            pltpu.VMEM((rows, feats), BF16),
            pltpu.VMEM((rows, 128), F32),
            pltpu.VMEM((8, 8, rows), F32),
            pltpu.VMEM((NBUF1, 2, feats, W), BF16),
            pltpu.VMEM((feats, kv), BF16),
            pltpu.VMEM((n_all, 2, 2, 64, 2 * W), BF16),
            pltpu.VMEM((2, 2, 64, kv), BF16),
            pltpu.VMEM((n_all, 2, 64, 2 * W), BF16),
            pltpu.VMEM((2, 64, kv), BF16),
            pltpu.VMEM((n_all, 64, 2 * W), BF16),
            pltpu.VMEM((64, kv), BF16),
            pltpu.VMEM((n_all, 64, 2 * W), BF16),
            pltpu.VMEM((64, kv), BF16),
            pltpu.VMEM((n_far, 64, 2 * W), BF16),
            pltpu.VMEM((64, kv), BF16),
            pltpu.VMEM((2, 32, cols), BF16),
            pltpu.VMEM((32, cols), BF16),
            pltpu.VMEM((EARLY, 64, W), BF16),
            dma((NBUF1, 2)),
            dma,
            dma((2, 2)),
            dma((8,)),
            dma((8,)),
            dma((n_all + n_q + 2,)),
            dma((n_all + n_q + 2,)),
            dma((n_far + 1,)),
            dma((n_far + 1,)),
            dma((2,)),
            dma((late, 2)),
            dma((EARLY,)),
            dma((2,)),
        ],
        compiler_params=pltpu.CompilerParams(collective_id=0, has_side_effects=True, vmem_limit_bytes=VMEM_LIMIT),
        cost_estimate=pl.CostEstimate(flops=flops, bytes_accessed=feats * (flops // (rows * feats)), transcendentals=0),
    )(hidden, gain, w_q, w_kv, w_gate, w_up)


def attend_kernel(lens, q_ref, kv_ref, k_ref, v_ref, k_out, v_out, o_ref):
    step = pl.program_id(0)
    n_pos = k_ref.shape[2]
    scale = q_ref.shape[2] ** -0.5 * LOG2E
    for s in range(SEQ_STEP):
        length = lens[step * SEQ_STEP + s]
        base = pl.multiple_of((length // 16) * 16, 16)
        k_out[0, s] = k_ref[0, s]
        v_out[0, s] = v_ref[0, s]
        hit = lax.broadcasted_iota(jnp.int32, (16, k_ref.shape[3]), 0) == length - base
        for src, dst, which in ((k_ref, k_out, 0), (v_ref, v_out, 1)):
            old = src[0, s, pl.ds(base, 16), :].astype(F32)
            new = kv_ref[s, which:which + 1, :].astype(F32)
            dst[0, s, pl.ds(base, 16), :] = jnp.where(hit, new, old).astype(BF16)
        scores = lax.dot_general(q_ref[s], k_out[0, s], (((1,), (1,)), ((), ())), preferred_element_type=F32) * scale
        visible = lax.broadcasted_iota(jnp.int32, scores.shape, 1) <= length
        scores = jnp.where(visible, scores, MASKED)
        weights = jnp.exp2(scores - jnp.max(scores, axis=1, keepdims=True))
        probs = (weights * (1.0 / jnp.sum(weights, axis=1, keepdims=True))).astype(BF16)
        o_ref[s] = jnp.dot(probs, v_out[0, s], preferred_element_type=F32).astype(BF16)


def attend(lens, q, kv, k_cache, v_cache):
    seqs, heads, dim = q.shape
    n_pos = k_cache.shape[2]
    cache_spec = pl.BlockSpec((1, SEQ_STEP, n_pos, dim), lambda b, lens: (0, b, 0, 0))
    q_spec = pl.BlockSpec((SEQ_STEP, heads, dim), lambda b, lens: (b, 0, 0))
    return pl.pallas_call(
        attend_kernel,
        name="attend",
        out_shape=(
            jax.ShapeDtypeStruct(k_cache.shape, BF16),
            jax.ShapeDtypeStruct(v_cache.shape, BF16),
            jax.ShapeDtypeStruct(q.shape, BF16),
        ),
        grid_spec=pltpu.PrefetchScalarGridSpec(
            num_scalar_prefetch=1,
            grid=(seqs // SEQ_STEP,),
            in_specs=[q_spec, pl.BlockSpec((SEQ_STEP, 2, dim), lambda b, lens: (b, 0, 0)), cache_spec, cache_spec],
            out_specs=(cache_spec, cache_spec, q_spec),
        ),
        compiler_params=pltpu.CompilerParams(dimension_semantics=("arbitrary",), vmem_limit_bytes=60_000_000),
        cost_estimate=pl.CostEstimate(
            flops=10**10, bytes_accessed=8 * k_cache.size, transcendentals=seqs * heads * n_pos),
    )(lens, q, kv, k_cache, v_cache)


def output_kernel(
    n_ff, n_o, o_in, m_in, keep, recv, hidden, w_o, w_down, out,
    acts, wbuf, acc, keep_v, recv_v, h_v, y_src, y_dst,
    w_sem, in_sems, m_sem, o_sems, far_send, far_recv, near_send, near_recv, y_sems,
):
    xi = lax.axis_index("x")
    yj = lax.axis_index("yz")
    core = lax.rem(xi, 2)
    mate = xi + 1 - 2 * core
    across = lax.rem(xi + 2, 4)
    other_y = 1 - yj
    n_m = n_ff // GROUP
    n_g = n_m + n_o // GROUP
    n_early = EARLY // GROUP
    depth = GROUP * W
    d_out = w_down.shape[2]
    half = d_out // 2

    barrier = pltpu.get_barrier_semaphore()
    for x_, y_ in ((mate, yj), (across, yj), (xi, other_y)):
        pl.semaphore_signal(barrier, inc=1, **dev(x=x_, yz=y_))

    def block(h, g, owner):
        return acts.at[h, pl.ds(GROUP * g, GROUP), pl.ds(pl.multiple_of(owner * 32, 32), 32)]

    def m_block(h, g):
        return m_in.at[pl.ds(GROUP * g, GROUP), pl.ds(32 * h, 32)]

    def m_copy(h, g):
        return pltpu.make_async_copy(m_block(h, g), block(h, g, xi), m_sem.at[h, g])

    def o_block(h):
        return acts.at[h, pl.ds(n_ff, n_o), pl.ds(pl.multiple_of(xi * 32, 32), 32)]

    keep_copy = pltpu.make_async_copy(keep, keep_v, in_sems.at[0])
    recv_copy = pltpu.make_async_copy(recv, recv_v, in_sems.at[1])
    h_copy = pltpu.make_async_copy(hidden, h_v, in_sems.at[2])
    o_own = pltpu.make_async_copy(o_in.at[yj], o_block(yj), in_sems.at[3])

    def start_weights(s):
        slot = lax.rem(s, NBUF3)
        g = lax.rem(s, n_g)

        @pl.when(g < n_m)
        def _():
            pltpu.make_async_copy(
                w_down.at[0, pl.ds(pl.multiple_of(g * depth, W), depth)], wbuf.at[slot], w_sem.at[slot]).start()

        @pl.when(g >= n_m)
        def _():
            pltpu.make_async_copy(
                w_o.at[0, pl.ds(pl.multiple_of((g - n_m) * depth, W), depth)], wbuf.at[slot], w_sem.at[slot]).start()

    pl.semaphore_wait(barrier, 3)

    def far_copy(h, g, src):
        return pltpu.make_async_remote_copy(
            src_ref=src, dst_ref=block(h, g, xi), send_sem=far_send.at[h, g], recv_sem=far_recv.at[h, g],
            **dev(x=across, yz=yj))

    def near_copy(h, g, which, src):
        return pltpu.make_async_remote_copy(
            src_ref=src, dst_ref=block(h, g, xi if which == 0 else across), send_sem=near_send.at[h, g, which],
            recv_sem=near_recv.at[h, g, which], **dev(x=mate, yz=yj))

    o_copy = pltpu.make_async_remote_copy(
        src_ref=o_in.at[other_y], dst_ref=o_block(yj), send_sem=o_sems.at[0], recv_sem=o_sems.at[1],
        **dev(x=xi, yz=other_y))

    def give(h, g, src):
        far_copy(h, g, src).start()
        near_copy(h, g, 0, src).start()

    def give_early(h):
        @pl.loop(0, n_early)
        def _(g):
            give(h, g, m_block(h, g))

    def give_late(h):
        @pl.loop(n_early, n_m)
        def _(g):
            for k in range(GROUP):
                t = GROUP * g + k - EARLY
                rows = slice(32 * h, 32 * h + 32)
                z = keep_v[t, rows].astype(F32) + recv_v[t, rows].astype(F32)
                acts[h, GROUP * g + k, pl.ds(pl.multiple_of(xi * 32, 32), 32)] = silu_mul(z[:, :W], z[:, W:])
            give(h, g, block(h, g, xi))

    def give_o(h):
        @pl.loop(n_m, n_g)
        def _(g):
            give(h, g, block(h, g, xi))

    give_early(0)
    o_copy.start()
    o_own.start()
    keep_copy.start()
    recv_copy.start()
    for h in range(2):
        for g in range(n_early):
            m_copy(h, g).start()
    for s in range(NBUF3):
        start_weights(jnp.int32(s))
    h_copy.start()
    keep_copy.wait()
    recv_copy.wait()
    give_late(0)
    acc[...] = jnp.zeros_like(acc)
    o_own.wait()
    o_copy.wait_recv()
    give_o(0)
    give_early(1)
    give_late(1)
    give_o(1)
    for h in range(2):
        for g in range(n_early):
            m_copy(h, g).wait()

    def forward(h, g):
        far_copy(h, g, block(h, g, xi)).wait_recv()
        near_copy(h, g, 1, block(h, g, across)).start()

    def multiply(h, g):
        s = h * n_g + g
        slot = lax.rem(s, NBUF3)
        pltpu.make_async_copy(w_down.at[0, pl.ds(0, depth)], wbuf.at[slot], w_sem.at[slot]).wait()
        near_copy(h, g, 0, block(h, g, xi)).wait_recv()
        near_copy(h, g, 1, block(h, g, across)).wait_recv()
        for n in range(d_out // W):
            cols = slice(n * W, (n + 1) * W)
            total = acc[h, :, cols]
            for k in range(GROUP):
                total += jnp.dot(
                    acts[h, GROUP * g + k], wbuf[slot, k * W:(k + 1) * W, cols], preferred_element_type=F32)
            acc[h, :, cols] = total

        @pl.when(s + NBUF3 < 2 * n_g)
        def _():
            start_weights(s + NBUF3)

    def cols_of(j):
        return pl.ds(pl.multiple_of(j * half, 128), half)

    def y_copy(h):
        return pltpu.make_async_remote_copy(
            src_ref=y_src.at[h], dst_ref=y_dst.at[h], send_sem=y_sems.at[h, 0], recv_sem=y_sems.at[h, 1],
            **dev(x=xi, yz=other_y))

    def exchange(h):
        y_src[h] = acc[h, :, cols_of(other_y)].astype(BF16)
        y_copy(h).start()

    def finalize(h):
        y_copy(h).wait_recv()
        total = acc[h, :, cols_of(yj)] + y_dst[h].astype(F32)
        out[:, h] = (h_v[:, h].astype(F32) + total.reshape(4, 32, half)).astype(BF16)

    forward(0, 0)

    @pl.loop(1, n_g)
    def _(g):
        forward(0, g)
        multiply(0, g - 1)

    forward(1, 0)
    multiply(0, n_g - 1)
    exchange(0)
    h_copy.wait()

    @pl.loop(1, n_g)
    def _(g):
        forward(1, g)
        multiply(1, g - 1)

    multiply(1, n_g - 1)
    exchange(1)
    finalize(0)
    finalize(1)

    o_copy.wait_send()
    for h in range(2):
        y_copy(h).wait_send()

        @pl.loop(0, n_g)
        def _(g):
            far_copy(h, g, block(h, g, xi)).wait_send()
            near_copy(h, g, 0, block(h, g, xi)).wait_send()
            near_copy(h, g, 1, block(h, g, across)).wait_send()


def finish(o, m_early, keep, recv, hidden, w_o, w_down):
    rows, half = hidden.shape
    n_ff = w_down.shape[1] // W
    n_o = w_o.shape[1] // W
    n_g = (n_ff + n_o) // GROUP
    d_out = w_down.shape[2]
    dma = pltpu.SemaphoreType.DMA
    any_spec = pl.BlockSpec(memory_space=pl.ANY)
    vmem = pl.BlockSpec(memory_space=pltpu.VMEM)
    flops = 2 * rows * d_out * (w_down.shape[1] + w_o.shape[1])
    out = pl.pallas_call(
        functools.partial(output_kernel, n_ff, n_o),
        name="finish",
        out_shape=jax.ShapeDtypeStruct((4, 2, 32, half), BF16),
        in_specs=[any_spec] * 7,
        out_specs=vmem,
        scratch_shapes=[
            pltpu.VMEM((2, n_ff + n_o, rows // 2, W), BF16),
            pltpu.VMEM((NBUF3, GROUP * W, d_out), BF16),
            pltpu.VMEM((2, rows // 2, d_out), F32),
            pltpu.VMEM(keep.shape, BF16),
            pltpu.VMEM(recv.shape, BF16),
            pltpu.VMEM((4, 2, 32, half), BF16),
            pltpu.VMEM((2, rows // 2, half), BF16),
            pltpu.VMEM((2, rows // 2, half), BF16),
            dma((NBUF3,)),
            dma((4,)),
            dma((2, EARLY // GROUP)),
            dma((2,)),
            dma((2, n_g)),
            dma((2, n_g)),
            dma((2, n_g, 2)),
            dma((2, n_g, 2)),
            dma((2, 2)),
        ],
        compiler_params=pltpu.CompilerParams(collective_id=1, has_side_effects=True, vmem_limit_bytes=56_000_000),
        cost_estimate=pl.CostEstimate(flops=flops, bytes_accessed=2 * d_out * (w_down.shape[1] + w_o.shape[1]), transcendentals=0),
    )(o, m_early, keep, recv, hidden.reshape(4, 2, 32, half), w_o, w_down)
    return out.reshape(rows, half)


def solution(mesh):
    x_size = mesh.shape["x"]
    y_size = mesh.shape["yz"]
    row_spec = P("dp", ("x", "yz"))
    tile_in = P(None, "x", "yz")
    tile_out = P(None, "yz", "x")
    cache_spec = P(None, ("dp", "x", "yz"))
    len_spec = P(("dp", "x", "yz"))

    def device_step(hidden, norm_gain, w_q, w_kv, w_gate, w_up, w_o, w_down, k_cache, v_cache, seq_len):
        d_model = hidden.shape[1] * x_size * y_size
        seqs = k_cache.shape[1]
        dim = k_cache.shape[3]
        q_cols = w_q.shape[2]
        heads = q_cols // dim
        qkv, m_early, keep, send = project(hidden, norm_gain, w_q, w_kv, w_gate, w_up, d_model)
        recv = lax.ppermute(send, "x", [(i, (i + x_size // 2) % x_size) for i in range(x_size)])
        q = qkv[:, :, :q_cols].reshape(y_size, seqs, heads, dim).transpose(1, 0, 2, 3).reshape(seqs, y_size * heads, dim)
        kv = qkv[:, :, q_cols:].transpose(1, 0, 2)
        k_new, v_new, o = attend(seq_len, q, kv, k_cache, v_cache)
        o = o.reshape(seqs, y_size, q_cols // W, W).transpose(1, 2, 0, 3)
        hidden_out = finish(o, m_early, keep, recv, hidden, w_o, w_down)
        return hidden_out, k_new, v_new

    return jax.shard_map(
        device_step,
        mesh=mesh,
        in_specs=(row_spec, P(None, "x"), tile_in, tile_in, tile_in, tile_in, tile_out, tile_out, cache_spec, cache_spec, len_spec),
        out_specs=(row_spec, cache_spec, cache_spec),
        check_vma=False,
    )
```

time: 168 us -> 155 us (0.923)
  Pallas kernels: 152 us -> 143 us
  waiting for transfers between devices: 6.93 us -> 1.82 us
    pallas_call x1, Pallas kernels: 62.4 us -> 54.4 us  [finish(): pl.pallas_call(functools.partial(output_kernel, n_ff, n_o), name='finish'...]
    ppermute x1, waiting for transfers between devices: 6.93 us -> 1.82 us  [device_step(): lax.ppermute(send, 'x', [(i, (i + x_size // 2) % x_size) for i in range(x...]
    pallas_call x1, Pallas kernels: 29.6 us -> 27.5 us  [attend(): pl.pallas_call(attend_kernel, name='attend', out_shape=(jax.ShapeDtypeStr...]
  transfers between devices with their start and end apart: 1 -> 1, of which waited for: 1 -> 1; matrix products, arithmetic and copies ran while one was open for 2% -> 4% of each run, Pallas kernels for 18% -> 18%
where the time goes in v2:
time: 155 us
  Pallas kernels  143 us (92%)
  local copies, waits for them, and re-layouts  7.9 us (5%)
  waiting for transfers between devices  1.82 us (1%)
    pallas_call x1, Pallas kernels, project(): pl.pallas_call(functools.partial(project_kernel, n_q, n_ff, d_model), nam...  61.6 us
    pallas_call x1, Pallas kernels, finish(): pl.pallas_call(functools.partial(output_kernel, n_ff, n_o), name='finish'...  54.4 us
    pallas_call x1, Pallas kernels, attend(): pl.pallas_call(attend_kernel, name='attend', out_shape=(jax.ShapeDtypeStr...  27.5 us
  transfers between devices with their start and end apart: 1, of which 1 were waited for; matrix products, arithmetic and copies ran while one was open for 4% of the time, Pallas kernels for 18%

profile of v2, /device:TPU:0, one launch (start us, length us, event | category | flops | bytes accessed | tf_op | source)
XLA Modules:
  0.0 154.7 jit_solution(11861565072942061569)
XLA Ops:
  0.6 61.6 %project.1 = (bf16[2,32,3200]{2,1,0:T(8,128)(2,1)}, bf16[12,64,512]{2,1,0:T(8,128)(2,1)}, bf16[12,64,1024]{2,1,0:T(8,128)(2,1)}, bf16[12,64,1024]{2,1,0:T(8,128)(2,1)}) custom-call(bf16[256,768]{1,0:T(8,128)(2,1)} %hidden.1, bf16[1,1536]{1,0:T(2,128)(2,1)} %gain.1, bf16[1,1536,3072]{2,1,0:T(8,128)(2,1)} %wq.1, bf16[1,1536,128]{2,1,0:T(8,128)(2,1)} %wkv.1, ...), custom_call_target="tpu_custom_call" | custom-call | flops 21843935232 | bytes 85327872 | tf_op jit(solution)/shard_map/project/pallas_call | solution.py:307
  62.2 0.8 collective-permute-start
  63.0 1.0 slice.6
  64.0 1.3 copy.17
  65.3 0.1 copy.19
  65.4 0.8 copy.16
  66.2 0.6 slice_bitcast_fusion.kv_ref
  66.8 27.5 %attend.1 = (bf16[1,32,2048,128]{3,2,1,0:T(8,128)(2,1)}, bf16[1,32,2048,128]{3,2,1,0:T(8,128)(2,1)}, bf16[32,48,128]{2,1,0:T(8,128)(2,1)}) custom-call(s32[32]{0:T(128)} %lens.1, bf16[32,48,128]{2,1,0:T(8,128)(2,1)} %bitcast.19, bf16[32,2,128]{2,1,0:T(2,128)(2,1)} %slice_bitcast_fusion.kv_ref, bf16[1,32,2048,128]{3,2,1,0:T(8,128)(2,1)} %k_ref.1, ...), custom_call_target="tpu_custom_call" | custom-call | flops 10000000000 | bytes 67108864 | tf_op jit(solution)/shard_map/attend/pallas_call | solution.py:384
  94.3 1.2 reshape.23
  95.6 1.0 copy.21
  96.5 1.8 %collective-permute-done.recv = bf16[12,64,1024]{2,1,0:T(8,128)(2,1)S(1)} collective-permute-done((bf16[12,64,1024]{2,1,0:T(8,128)(2,1)}, bf16[12,64,1024]{2,1,0:T(8,128)(2,1)S(1)}, u32[]{:S(2)}, u32[]{:S(2)}) %collective-permute-start) | collective-permute-done | bytes 1572896 | tf_op jit(solution)/shard_map/ppermute | solution.py:651
  98.4 0.0 copy-start
  98.4 1.2 copy-done
  99.5 54.4 %finish.1 = bf16[4,2,32,768]{3,2,1,0:T(8,128)(2,1)S(1)} custom-call(bf16[2,6,32,512]{3,2,1,0:T(8,128)(2,1)} %bitcast.16, bf16[12,64,512]{2,1,0:T(8,128)(2,1)} %get-tuple-element.12.m_in, bf16[12,64,1024]{2,1,0:T(8,128)(2,1)} %get-tuple-element.13.keep, bf16[12,64,1024]{2,1,0:T(8,128)(2,1)} %copy-done, bf16[4,2,32,768]{3,2,1,0:T(8,128)(2,1)} %bitcast.15, ...), custom_call_target="tpu_custom_call" | custom-call | flops 12079595520 | bytes 47185920 | tf_op jit(solution)/shard_map/finish/pallas_call | solution.py:604
  153.9 0.7 copy.23
Async XLA Ops:
  62.2 36.2 %collective-permute-start = (bf16[12,64,1024]{2,1,0:T(8,128)(2,1)}, bf16[12,64,1024]{2,1,0:T(8,128)(2,1)S(1)}, u32[]{:S(2)}, u32[]{:S(2)}) collective-permute-start(bf16[12,64,1024]{2,1,0:T(8,128)(2,1)} %get-tuple-element.14), channel_id=1, source_target_pairs={{0,2},{1,3},{2,0},{3,1},{4,6},{5,7},{6,4},{7,5}} | collective-permute-start | bytes 4718600 | tf_op jit(solution)/shard_map/ppermute | solution.py:651
  98.4 1.2 copy-start

commit v3 on v2

v3 whole, which is shorter than its diff:
```python
import functools

import jax
import jax.numpy as jnp
from jax import lax
from jax.experimental import pallas as pl
from jax.experimental.pallas import tpu as pltpu
from jax.sharding import PartitionSpec as P

NORM_EPS = 1e-6
W = 512
NBUF1 = 4
NBUF3 = 6
GROUP = 3
PARTS = ((0, 32), (32, 16), (48, 16))
EARLY = 12
SEQ_STEP = 2
VMEM_LIMIT = 64_000_000
F32 = jnp.float32
BF16 = jnp.bfloat16
LOG2E = 1.4426950408889634
MASKED = -1e30


def dev(**axes):
    return dict(device_id=axes, device_id_type=pl.DeviceIdType.MESH)


def silu_mul(gate, up):
    gate = gate.astype(BF16).astype(F32)
    up = up.astype(BF16).astype(F32)
    return (jax.nn.silu(gate) * up).astype(BF16)


def project_kernel(
    n_q, n_ff, d_model, hidden, gain, wq, wkv, wg, wu,
    qkv_out, keep_out, recv_out, send_out,
    h_own, h_other, u, inv_all, sq_all, wbuf, wkv_buf, part, part_kv, near, near_kv, keep, keep_kv, far_src,
    far_src_kv, far_q, far_kv, z_rows, z_other,
    w_sem, wkv_sem, h_in, h_sems, sq_send, sq_recv, near_send, near_recv, qn_send, qn_recv, kn_send, kn_recv,
    far_send, far_recv, qf_send, qf_recv, kf_send, kf_recv, y_sems, out_sem, qkv_sem,
):
    xi = lax.axis_index("x")
    yj = lax.axis_index("yz")
    core = lax.rem(xi, 2)
    chip = xi // 2
    mate = xi + 1 - 2 * core
    across = lax.rem(xi + 2, 4)
    other_y = 1 - yj
    me = xi * 2 + yj
    half = hidden.shape[-1]
    n_all = n_q + n_ff
    to_mate = dev(x=mate, yz=yj)
    to_across = dev(x=across, yz=yj)

    barrier = pltpu.get_barrier_semaphore()
    for k in range(1, 8):
        peer = lax.rem(me + k, 8)
        pl.semaphore_signal(barrier, inc=1, **dev(x=peer // 2, yz=lax.rem(peer, 2)))
    h_load = pltpu.make_async_copy(hidden, h_own, h_in)
    h_load.start()

    def start_weights(g):
        slot = lax.rem(g, NBUF1)

        @pl.when(g < n_q)
        def _():
            for k in range(2):
                cols = pl.ds(pl.multiple_of((2 * g + k) * W, W), W)
                pltpu.make_async_copy(wq.at[0, :, cols], wbuf.at[slot, k], w_sem.at[slot, k]).start()

        @pl.when(g >= n_q)
        def _():
            cols = pl.ds(pl.multiple_of((g - n_q) * W, W), W)
            pltpu.make_async_copy(wg.at[0, :, cols], wbuf.at[slot, 0], w_sem.at[slot, 0]).start()
            pltpu.make_async_copy(wu.at[0, :, cols], wbuf.at[slot, 1], w_sem.at[slot, 1]).start()

    def wait_weights(slot, k):
        pltpu.make_async_copy(wq.at[0, :, pl.ds(0, W)], wbuf.at[slot, k], w_sem.at[slot, k]).wait()

    for g in range(NBUF1):
        start_weights(jnp.int32(g))
    kv_copy = pltpu.make_async_copy(wkv.at[0], wkv_buf, wkv_sem)
    kv_copy.start()

    h_load.wait()
    h_f32 = h_own[...].reshape(256, half).astype(F32)
    sq_all[me] = lax.dot_general(
        jnp.ones((8, half), F32), h_f32 * h_f32, (((1,), (1,)), ((), ())),
        precision=lax.Precision.HIGHEST, preferred_element_type=F32)
    pl.semaphore_wait(barrier, 7)

    def sq_copy(peer, src):
        return pltpu.make_async_remote_copy(
            src_ref=sq_all.at[src], dst_ref=sq_all.at[src], send_sem=sq_send.at[peer], recv_sem=sq_recv.at[src],
            **dev(x=peer // 2, yz=lax.rem(peer, 2)))

    def side_of(step):
        return 1 - chip if step < 2 else chip

    def h_copy(step):
        block = (side_of(step), slice(None), step % 2)
        return pltpu.make_async_remote_copy(
            src_ref=h_own.at[block], dst_ref=h_other.at[block],
            send_sem=h_sems.at[step, 0], recv_sem=h_sems.at[step, 1], **dev(x=xi, yz=other_y))

    for k in range(1, 8):
        sq_copy(lax.rem(me + k, 8), me).start()
    for step in range(4):
        h_copy(step).start()
    for k in range(1, 8):
        peer = lax.rem(me + k, 8)
        sq_copy(peer, peer).wait_recv()
    total = jnp.sum(sq_all[...], axis=0)
    inv = lax.rsqrt(total / d_model + NORM_EPS)
    inv_all[...] = jnp.transpose(jnp.concatenate([inv] * 16, axis=0)).reshape(inv_all.shape)

    def normalize(values, step, which):
        cols = pl.ds(pl.multiple_of(which * half, 128), half)
        side, piece = side_of(step), step % 2
        inv_rows = inv_all[side, :, piece].reshape(64, 128)[:, :1]
        res = (values[side, :, piece].reshape(64, half).astype(F32) * inv_rows
               * gain[:, cols].astype(F32)).astype(BF16)
        u[side, piece, :, cols] = res

    def near_copy(g):
        return pltpu.make_async_remote_copy(
            src_ref=part.at[g, :, :, 1 - core], dst_ref=near.at[g], send_sem=near_send.at[g],
            recv_sem=near_recv.at[g], **to_mate)

    def near_copy_q(g, step):
        side, piece = side_of(step), step % 2
        return pltpu.make_async_remote_copy(
            src_ref=part.at[g, side, piece, 1 - core], dst_ref=near.at[g, side, piece],
            send_sem=qn_send.at[g, step], recv_sem=qn_recv.at[g, step], **to_mate)

    def near_copy_kv(step):
        side, piece = side_of(step), step % 2
        return pltpu.make_async_remote_copy(
            src_ref=part_kv.at[side, piece, 1 - core], dst_ref=near_kv.at[side, piece],
            send_sem=kn_send.at[step], recv_sem=kn_recv.at[step], **to_mate)

    def far_copy(g):
        return pltpu.make_async_remote_copy(
            src_ref=far_src.at[g], dst_ref=recv_out.at[g - n_q], send_sem=far_send.at[g - n_q],
            recv_sem=far_recv.at[g - n_q], **to_across)

    def far_copy_q(g, step):
        rows = slice(32 * step, 32 * step + 32)
        return pltpu.make_async_remote_copy(
            src_ref=far_src.at[g, rows], dst_ref=far_q.at[g, rows], send_sem=qf_send.at[g, step],
            recv_sem=qf_recv.at[g, step], **to_across)

    def far_copy_kv(step):
        rows = slice(32 * step, 32 * step + 32)
        return pltpu.make_async_remote_copy(
            src_ref=far_src_kv.at[rows], dst_ref=far_kv.at[rows], send_sem=kf_send.at[step],
            recv_sem=kf_recv.at[step], **to_across)

    def keep_copy(g):
        return pltpu.make_async_copy(keep.at[g], keep_out.at[g - n_q], out_sem.at[g - n_q, 0])

    def send_copy(g):
        k = g - n_q
        return pltpu.make_async_copy(far_src.at[g], send_out.at[k - EARLY], out_sem.at[k, 1])

    def add(a, b):
        return (a.astype(F32) + b.astype(F32)).astype(BF16)

    def multiply(g):
        slot = lax.rem(g, NBUF1)
        for k in range(2):
            wait_weights(slot, k)
            res = jnp.dot(u[...].reshape(256, u.shape[-1]), wbuf[slot, k], preferred_element_type=F32).astype(BF16)
            part[g, :, :, :, :, k * W:(k + 1) * W] = res.reshape(2, 2, 2, 32, W)
        near_copy(g).start()

        @pl.when(g + NBUF1 < n_all)
        def _():
            start_weights(g + NBUF1)

    def reduce_near(g, send):
        near_copy(g).wait_recv()
        far_src[g] = add(part[g, 1 - chip, :, core], near[g, 1 - chip]).reshape(64, 2 * W)
        if send:
            far_copy(g).start()
        else:
            send_copy(g).start()
        keep[g] = add(part[g, chip, :, core], near[g, chip]).reshape(64, 2 * W)
        keep_copy(g).start()

    for step in range(4):
        side, piece = side_of(step), step % 2
        rows = slice(32 * piece, 32 * piece + 32)
        normalize(h_own, step, yj)
        h_copy(step).wait_recv()
        normalize(h_other, step, other_y)

        def reduce_q(g):
            near_copy_q(g, step).wait_recv()
            total_q = add(part[g, side, piece, core], near[g, side, piece])
            if step < 2:
                far_src[g, rows] = total_q
                far_copy_q(g, step).start()
            else:
                keep[g, rows] = total_q

        for g in range(n_q):
            for k in range(2):
                if step == 0:
                    wait_weights(g, k)
                res = jnp.dot(u[side, piece], wbuf[g, k], preferred_element_type=F32).astype(BF16)
                part[g, side, piece, :, :, k * W:(k + 1) * W] = res.reshape(2, 32, W)
            near_copy_q(g, step).start()
            if step == 3:
                start_weights(jnp.int32(g + NBUF1))
            if g >= 1:
                reduce_q(g - 1)
        if step == 0:
            kv_copy.wait()
        res = jnp.dot(u[side, piece], wkv_buf[...], preferred_element_type=F32).astype(BF16)
        part_kv[side, piece] = res.reshape(2, 32, res.shape[1])
        near_copy_kv(step).start()
        reduce_q(n_q - 1)
        near_copy_kv(step).wait_recv()
        total_kv = add(part_kv[side, piece, core], near_kv[side, piece])
        if step < 2:
            far_src_kv[rows] = total_kv
            far_copy_kv(step).start()
        else:
            keep_kv[rows] = total_kv

    n_far = n_q + EARLY

    @pl.loop(n_q, n_far)
    def _(g):
        multiply(g)

        @pl.when(g >= n_q + 1)
        def _():
            reduce_near(g - 1, True)

    q_cols = n_q * 2 * W
    for g in range(n_q):
        for step in range(2):
            far_copy_q(g, step).wait_recv()
        z_rows[:, :, g * 2 * W:(g + 1) * 2 * W] = add(keep[g], far_q[g]).reshape(2, 32, 2 * W)
    for step in range(2):
        far_copy_kv(step).wait_recv()
    z_kv = add(keep_kv[...], far_kv[...])
    z_rows[:, :, q_cols:] = z_kv.reshape(2, 32, z_kv.shape[1])
    y_copy = pltpu.make_async_remote_copy(
        src_ref=z_rows.at[other_y], dst_ref=z_other, send_sem=y_sems.at[0], recv_sem=y_sems.at[1],
        **dev(x=xi, yz=other_y))
    y_copy.start()
    qkv_own = pltpu.make_async_copy(z_rows.at[yj], qkv_out.at[yj], qkv_sem.at[0])
    qkv_own.start()

    multiply(n_far)
    reduce_near(n_far - 1, True)

    @pl.loop(n_far + 1, n_all)
    def _(g):
        multiply(g)
        reduce_near(g - 1, False)

    reduce_near(n_all - 1, False)
    y_copy.wait_recv()
    qkv_other = pltpu.make_async_copy(z_other, qkv_out.at[other_y], qkv_sem.at[1])
    qkv_other.start()

    for step in range(4):
        h_copy(step).wait_send()
        near_copy_kv(step).wait_send()
        for g in range(n_q):
            near_copy_q(g, step).wait_send()
    for step in range(2):
        far_copy_kv(step).wait_send()
        for g in range(n_q):
            far_copy_q(g, step).wait_send()
    for k in range(1, 8):
        sq_copy(lax.rem(me + k, 8), me).wait_send()
    y_copy.wait_send()

    @pl.loop(n_q, n_all)
    def _(g):
        near_copy(g).wait_send()
        keep_copy(g).wait()

    @pl.loop(n_far, n_all)
    def _(g):
        send_copy(g).wait()

    qkv_own.wait()
    qkv_other.wait()

    @pl.loop(n_q, n_far)
    def _(g):
        far_copy(g).wait_send()
        far_copy(g).wait_recv()


def project(hidden, gain, w_q, w_kv, w_gate, w_up, d_model):
    rows, half = hidden.shape
    feats = w_q.shape[1]
    kv = w_kv.shape[2]
    n_q = w_q.shape[2] // (2 * W)
    n_ff = w_gate.shape[2] // W
    n_all = n_q + n_ff
    late = n_ff - EARLY
    dma = pltpu.SemaphoreType.DMA
    any_spec = pl.BlockSpec(memory_space=pl.ANY)
    vmem = pl.BlockSpec(memory_space=pltpu.VMEM)
    cols = w_q.shape[2] + kv
    flops = 2 * rows * feats * (w_q.shape[2] + kv + 2 * w_gate.shape[2])
    h_shape = (2, 2, 2, 32, half)
    return pl.pallas_call(
        functools.partial(project_kernel, n_q, n_ff, d_model),
        name="project",
        out_shape=(
            jax.ShapeDtypeStruct((2, 32, cols), BF16),
            jax.ShapeDtypeStruct((n_ff, 64, 2 * W), BF16),
            jax.ShapeDtypeStruct((EARLY, 64, 2 * W), BF16),
            jax.ShapeDtypeStruct((late, 64, 2 * W), BF16),
        ),
        in_specs=[any_spec, vmem, any_spec, any_spec, any_spec, any_spec],
        out_specs=(any_spec, any_spec, any_spec, any_spec),
        scratch_shapes=[
            pltpu.VMEM(h_shape, BF16),
            pltpu.VMEM(h_shape, BF16),
            pltpu.VMEM((2, 2, 64, feats), BF16),
            pltpu.VMEM((2, 2, 2, 32, 128), F32),
            pltpu.VMEM((8, 8, rows), F32),
            pltpu.VMEM((NBUF1, 2, feats, W), BF16),
            pltpu.VMEM((feats, kv), BF16),
            pltpu.VMEM((n_all, 2, 2, 2, 32, 2 * W), BF16),
            pltpu.VMEM((2, 2, 2, 32, kv), BF16),
            pltpu.VMEM((n_all, 2, 2, 32, 2 * W), BF16),
            pltpu.VMEM((2, 2, 32, kv), BF16),
            pltpu.VMEM((n_all, 64, 2 * W), BF16),
            pltpu.VMEM((64, kv), BF16),
            pltpu.VMEM((n_all, 64, 2 * W), BF16),
            pltpu.VMEM((64, kv), BF16),
            pltpu.VMEM((n_q, 64, 2 * W), BF16),
            pltpu.VMEM((64, kv), BF16),
            pltpu.VMEM((2, 32, cols), BF16),
            pltpu.VMEM((32, cols), BF16),
            dma((NBUF1, 2)),
            dma,
            dma,
            dma((4, 2)),
            dma((8,)),
            dma((8,)),
            dma((n_all,)),
            dma((n_all,)),
            dma((n_q, 4)),
            dma((n_q, 4)),
            dma((4,)),
            dma((4,)),
            dma((EARLY,)),
            dma((EARLY,)),
            dma((n_q, 2)),
            dma((n_q, 2)),
            dma((2,)),
            dma((2,)),
            dma((2,)),
            dma((n_ff, 2)),
            dma((2,)),
        ],
        compiler_params=pltpu.CompilerParams(collective_id=0, has_side_effects=True, vmem_limit_bytes=VMEM_LIMIT),
        cost_estimate=pl.CostEstimate(flops=flops, bytes_accessed=feats * (flops // (rows * feats)), transcendentals=0),
    )(hidden.reshape(h_shape), gain, w_q, w_kv, w_gate, w_up)


def attend_kernel(lens, q_ref, kv_ref, k_ref, v_ref, k_out, v_out, o_ref):
    step = pl.program_id(0)
    n_pos = k_ref.shape[2]
    scale = q_ref.shape[2] ** -0.5 * LOG2E
    for s in range(SEQ_STEP):
        length = lens[step * SEQ_STEP + s]
        base = pl.multiple_of((length // 16) * 16, 16)
        k_out[0, s] = k_ref[0, s]
        v_out[0, s] = v_ref[0, s]
        hit = lax.broadcasted_iota(jnp.int32, (16, k_ref.shape[3]), 0) == length - base
        for src, dst, which in ((k_ref, k_out, 0), (v_ref, v_out, 1)):
            old = src[0, s, pl.ds(base, 16), :].astype(F32)
            new = kv_ref[s, which:which + 1, :].astype(F32)
            dst[0, s, pl.ds(base, 16), :] = jnp.where(hit, new, old).astype(BF16)
        scores = lax.dot_general(q_ref[s], k_out[0, s], (((1,), (1,)), ((), ())), preferred_element_type=F32) * scale
        visible = lax.broadcasted_iota(jnp.int32, scores.shape, 1) <= length
        scores = jnp.where(visible, scores, MASKED)
        weights = jnp.exp2(scores - jnp.max(scores, axis=1, keepdims=True))
        probs = (weights * (1.0 / jnp.sum(weights, axis=1, keepdims=True))).astype(BF16)
        o_ref[s] = jnp.dot(probs, v_out[0, s], preferred_element_type=F32).astype(BF16)


def attend(lens, q, kv, k_cache, v_cache):
    seqs, heads, dim = q.shape
    n_pos = k_cache.shape[2]
    cache_spec = pl.BlockSpec((1, SEQ_STEP, n_pos, dim), lambda b, lens: (0, b, 0, 0))
    q_spec = pl.BlockSpec((SEQ_STEP, heads, dim), lambda b, lens: (b, 0, 0))
    return pl.pallas_call(
        attend_kernel,
        name="attend",
        out_shape=(
            jax.ShapeDtypeStruct(k_cache.shape, BF16),
            jax.ShapeDtypeStruct(v_cache.shape, BF16),
            jax.ShapeDtypeStruct(q.shape, BF16),
        ),
        grid_spec=pltpu.PrefetchScalarGridSpec(
            num_scalar_prefetch=1,
            grid=(seqs // SEQ_STEP,),
            in_specs=[q_spec, pl.BlockSpec((SEQ_STEP, 2, dim), lambda b, lens: (b, 0, 0)), cache_spec, cache_spec],
            out_specs=(cache_spec, cache_spec, q_spec),
        ),
        compiler_params=pltpu.CompilerParams(dimension_semantics=("arbitrary",), vmem_limit_bytes=66_000_000),
        cost_estimate=pl.CostEstimate(
            flops=10**10, bytes_accessed=8 * k_cache.size, transcendentals=seqs * heads * n_pos),
    )(lens, q, kv, k_cache, v_cache)


def output_kernel(
    n_ff, n_o, o_in, keep, recv_e, recv_l, hidden, w_o, w_down, out,
    acts, wbuf, acc, keep_v, recv_v, h_v, y_src, y_dst,
    w_sem, keep_sem, recv_sem, h_sem, oo_sems, on_send, on_recv, far_send, far_recv, near_send, near_recv, y_sems,
):
    xi = lax.axis_index("x")
    yj = lax.axis_index("yz")
    core = lax.rem(xi, 2)
    mate = xi + 1 - 2 * core
    across = lax.rem(xi + 2, 4)
    other_y = 1 - yj
    n_m = n_ff // GROUP
    n_g = n_m + n_o // GROUP
    n_early = EARLY // GROUP
    depth = GROUP * W
    d_out = w_down.shape[2]
    half = d_out // 2

    barrier = pltpu.get_barrier_semaphore()
    for x_, y_ in ((mate, yj), (across, yj), (xi, other_y)):
        pl.semaphore_signal(barrier, inc=1, **dev(x=x_, yz=y_))

    def keep_copy(g):
        return pltpu.make_async_copy(
            keep.at[pl.ds(GROUP * g, GROUP)], keep_v.at[pl.ds(GROUP * g, GROUP)], keep_sem.at[g])

    def recv_copy(g):
        src = recv_e.at[pl.ds(GROUP * g, GROUP)] if g < n_early else recv_l.at[pl.ds(GROUP * (g - n_early), GROUP)]
        return pltpu.make_async_copy(src, recv_v.at[pl.ds(GROUP * g, GROUP)], recv_sem.at[g])

    for g in range(n_m):
        keep_copy(g).start()
        recv_copy(g).start()

    def rows_of(p, owner):
        off, size = PARTS[p]
        return pl.ds(pl.multiple_of(4 * off + owner * size, 16), size)

    def block(p, g, owner):
        return acts.at[pl.ds(GROUP * g, GROUP), rows_of(p, owner)]

    def o_rows(s):
        row = (1 - yj) * (32 * xi + 16 * s) + yj * (128 + 64 * s + 16 * xi)
        return acts.at[pl.ds(n_ff, n_o), pl.ds(pl.multiple_of(row, 16), 16)]

    def o_own(s):
        return pltpu.make_async_copy(o_in.at[yj, :, pl.ds(16 * s, 16)], o_rows(s), oo_sems.at[s])

    def o_copy(s):
        return pltpu.make_async_remote_copy(
            src_ref=o_in.at[other_y, :, pl.ds(16 * s, 16)], dst_ref=o_rows(s), send_sem=on_send.at[s],
            recv_sem=on_recv.at[s], **dev(x=xi, yz=other_y))

    h_load = pltpu.make_async_copy(hidden, h_v, h_sem)

    def load_weights(g):
        slot = lax.rem(g, NBUF3)

        @pl.when(g < n_m)
        def _():
            pltpu.make_async_copy(
                w_down.at[0, pl.ds(pl.multiple_of(g * depth, W), depth)], wbuf.at[slot], w_sem.at[slot]).start()

        @pl.when(g >= n_m)
        def _():
            pltpu.make_async_copy(
                w_o.at[0, pl.ds(pl.multiple_of((g - n_m) * depth, W), depth)], wbuf.at[slot], w_sem.at[slot]).start()

    def far_copy(p, g):
        return pltpu.make_async_remote_copy(
            src_ref=block(p, g, xi), dst_ref=block(p, g, xi), send_sem=far_send.at[p, g], recv_sem=far_recv.at[p, g],
            **dev(x=across, yz=yj))

    def near_copy(p, g, which):
        rows = block(p, g, xi if which == 0 else across)
        return pltpu.make_async_remote_copy(
            src_ref=rows, dst_ref=rows, send_sem=near_send.at[p, g, which], recv_sem=near_recv.at[p, g, which],
            **dev(x=mate, yz=yj))

    def give(p, g):
        far_copy(p, g).start()
        near_copy(p, g, 0).start()

    def give_m(p, g):
        off, size = PARTS[p]
        for k in range(GROUP):
            t = GROUP * g + k
            z = keep_v[t, off:off + size].astype(F32) + recv_v[t, off:off + size].astype(F32)
            acts[t, rows_of(p, xi)] = silu_mul(z[:, :W], z[:, W:])
        give(p, g)

    pl.semaphore_wait(barrier, 3)
    for g in range(n_m):
        keep_copy(g).wait()
        recv_copy(g).wait()
        give_m(0, g)
        if g == 0:
            for s in range(2):
                o_copy(s).start()
                o_own(s).start()
            for s in range(NBUF3):
                load_weights(jnp.int32(s))
            h_load.start()
    acc[...] = jnp.zeros_like(acc)
    for s in range(2):
        o_own(s).wait()
        o_copy(s).wait_recv()

    def chunk(p, k):
        return k if p % 2 == 0 else n_g - 1 - k

    for g in range(n_m, n_g):
        give(0, g)
    for p in range(1, len(PARTS)):
        @pl.loop(0, n_g)
        def _(k):
            g = chunk(p, k)

            @pl.when(g < n_m)
            def _():
                give_m(p, g)

            @pl.when(g >= n_m)
            def _():
                give(p, g)

    def forward(p, k):
        g = chunk(p, k)
        far_copy(p, g).wait_recv()
        near_copy(p, g, 1).start()

    def multiply(p, k):
        g = chunk(p, k)
        slot = lax.rem(g, NBUF3)

        @pl.when(k >= (0 if p == 0 else NBUF3))
        def _():
            pltpu.make_async_copy(w_down.at[0, pl.ds(0, depth)], wbuf.at[slot], w_sem.at[slot]).wait()

        near_copy(p, g, 0).wait_recv()
        near_copy(p, g, 1).wait_recv()
        off, size = PARTS[p]
        rows = slice(4 * off, 4 * (off + size))
        for n in range(d_out // W):
            cols = slice(n * W, (n + 1) * W)
            total = acc[rows, cols]
            for j in range(GROUP):
                total += jnp.dot(
                    acts[GROUP * g + j, rows], wbuf[slot, j * W:(j + 1) * W, cols], preferred_element_type=F32)
            acc[rows, cols] = total

        @pl.when(k + NBUF3 < n_g)
        def _():
            load_weights(chunk(p, k + NBUF3))

    def cols_of(j):
        return pl.ds(pl.multiple_of(j * half, 128), half)

    def y_copy(p):
        rows = slice(4 * PARTS[p][0], 4 * sum(PARTS[p]))
        return pltpu.make_async_remote_copy(
            src_ref=y_src.at[rows], dst_ref=y_dst.at[rows], send_sem=y_sems.at[p, 0], recv_sem=y_sems.at[p, 1],
            **dev(x=xi, yz=other_y))

    def exchange(p):
        rows = slice(4 * PARTS[p][0], 4 * sum(PARTS[p]))
        y_src[rows] = acc[rows, cols_of(other_y)].astype(BF16)
        y_copy(p).start()

    def finalize(p):
        off, size = PARTS[p]
        rows = slice(4 * off, 4 * (off + size))
        y_copy(p).wait_recv()
        total = (acc[rows, cols_of(yj)] + y_dst[rows].astype(F32)).reshape(4, size, half)
        out[:, off:off + size] = (h_v[:, off:off + size].astype(F32) + total).astype(BF16)

    for p in range(len(PARTS)):
        forward(p, jnp.int32(0))
        if p > 0:
            multiply(p - 1, jnp.int32(n_g - 1))
            exchange(p - 1)
        if p == 1:
            h_load.wait()

        @pl.loop(1, n_g)
        def _(k):
            forward(p, k)
            multiply(p, k - 1)

        if p > 0:
            finalize(p - 1)

    last = len(PARTS) - 1
    multiply(last, jnp.int32(n_g - 1))
    exchange(last)
    for s in range(2):
        o_copy(s).wait_send()
    for p in range(len(PARTS)):
        @pl.loop(0, n_g)
        def _(g):
            far_copy(p, g).wait_send()
            near_copy(p, g, 0).wait_send()
            near_copy(p, g, 1).wait_send()

    finalize(last)
    for p in range(len(PARTS)):
        y_copy(p).wait_send()


def finish(o, keep, recv_e, recv_l, hidden, w_o, w_down):
    rows, half = hidden.shape
    n_ff = w_down.shape[1] // W
    n_o = w_o.shape[1] // W
    n_m = n_ff // GROUP
    n_g = n_m + n_o // GROUP
    n_p = len(PARTS)
    d_out = w_down.shape[2]
    dma = pltpu.SemaphoreType.DMA
    any_spec = pl.BlockSpec(memory_space=pl.ANY)
    vmem = pl.BlockSpec(memory_space=pltpu.VMEM)
    flops = 2 * rows * d_out * (w_down.shape[1] + w_o.shape[1])
    out = pl.pallas_call(
        functools.partial(output_kernel, n_ff, n_o),
        name="finish",
        out_shape=jax.ShapeDtypeStruct((4, 64, half), BF16),
        in_specs=[any_spec] * 7,
        out_specs=vmem,
        scratch_shapes=[
            pltpu.VMEM((n_ff + n_o, rows, W), BF16),
            pltpu.VMEM((NBUF3, GROUP * W, d_out), BF16),
            pltpu.VMEM((rows, d_out), F32),
            pltpu.VMEM(keep.shape, BF16),
            pltpu.VMEM(keep.shape, BF16),
            pltpu.VMEM((4, 64, half), BF16),
            pltpu.VMEM((rows, half), BF16),
            pltpu.VMEM((rows, half), BF16),
            dma((NBUF3,)),
            dma((n_m,)),
            dma((n_m,)),
            dma,
            dma((2,)),
            dma((2,)),
            dma((2,)),
            dma((n_p, n_g)),
            dma((n_p, n_g)),
            dma((n_p, n_g, 2)),
            dma((n_p, n_g, 2)),
            dma((n_p, 2)),
        ],
        compiler_params=pltpu.CompilerParams(collective_id=1, has_side_effects=True, vmem_limit_bytes=56_000_000),
        cost_estimate=pl.CostEstimate(flops=flops, bytes_accessed=2 * d_out * (w_down.shape[1] + w_o.shape[1]), transcendentals=0),
    )(o, keep, recv_e, recv_l, hidden.reshape(4, 64, half), w_o, w_down)
    return out.reshape(rows, half)


def solution(mesh):
    x_size = mesh.shape["x"]
    y_size = mesh.shape["yz"]
    row_spec = P("dp", ("x", "yz"))
    tile_in = P(None, "x", "yz")
    tile_out = P(None, "yz", "x")
    cache_spec = P(None, ("dp", "x", "yz"))
    len_spec = P(("dp", "x", "yz"))

    def device_step(hidden, norm_gain, w_q, w_kv, w_gate, w_up, w_o, w_down, k_cache, v_cache, seq_len):
        d_model = hidden.shape[1] * x_size * y_size
        seqs = k_cache.shape[1]
        dim = k_cache.shape[3]
        q_cols = w_q.shape[2]
        heads = q_cols // dim
        qkv, keep, recv_e, send = project(hidden, norm_gain, w_q, w_kv, w_gate, w_up, d_model)
        recv_l = lax.ppermute(send, "x", [(i, (i + x_size // 2) % x_size) for i in range(x_size)])
        q = qkv[:, :, :q_cols].reshape(y_size, seqs, heads, dim).transpose(1, 0, 2, 3).reshape(seqs, y_size * heads, dim)
        kv = qkv[:, :, q_cols:].transpose(1, 0, 2)
        k_new, v_new, o = attend(seq_len, q, kv, k_cache, v_cache)
        o = o.reshape(seqs, y_size, q_cols // W, W).transpose(1, 2, 0, 3)
        hidden_out = finish(o, keep, recv_e, recv_l, hidden, w_o, w_down)
        return hidden_out, k_new, v_new

    return jax.shard_map(
        device_step,
        mesh=mesh,
        in_specs=(row_spec, P(None, "x"), tile_in, tile_in, tile_in, tile_in, tile_out, tile_out, cache_spec, cache_spec, len_spec),
        out_specs=(row_spec, cache_spec, cache_spec),
        check_vma=False,
    )
```

time: 155 us -> 161 us (1.039)
  Pallas kernels: 143 us -> 150 us
    pallas_call x1, Pallas kernels: 61.6 us -> 69.8 us  [project(): pl.pallas_call(functools.partial(project_kernel, n_q, n_ff, d_model), nam...]
  transfers between devices with their start and end apart: 1 -> 1, of which waited for: 1 -> 1; matrix products, arithmetic and copies ran while one was open for 4% -> 4% of each run, Pallas kernels for 18% -> 17%
where the time goes in v3:
time: 161 us
  Pallas kernels  150 us (93%)
  local copies, waits for them, and re-layouts  6.74 us (4%)
  waiting for transfers between devices  1.91 us (1%)
    pallas_call x1, Pallas kernels, project(): pl.pallas_call(functools.partial(project_kernel, n_q, n_ff, d_model), nam...  69.8 us
    pallas_call x1, Pallas kernels, finish(): pl.pallas_call(functools.partial(output_kernel, n_ff, n_o), name='finish'...  53.2 us
    pallas_call x1, Pallas kernels, attend(): pl.pallas_call(attend_kernel, name='attend', out_shape=(jax.ShapeDtypeStr...  27.5 us
  transfers between devices with their start and end apart: 1, of which 1 were waited for; matrix products, arithmetic and copies ran while one was open for 4% of the time, Pallas kernels for 17%

profile of v3, /device:TPU:0, one launch (start us, length us, event | category | flops | bytes accessed | tf_op | source)
XLA Modules:
  0.0 160.6 jit_solution(14535261746210615298)
XLA Ops:
  0.6 69.8 %project.1 = (bf16[2,32,3200]{2,1,0:T(8,128)(2,1)}, bf16[24,64,1024]{2,1,0:T(8,128)(2,1)}, bf16[12,64,1024]{2,1,0:T(8,128)(2,1)}, bf16[12,64,1024]{2,1,0:T(8,128)(2,1)}) custom-call(bf16[2,2,2,32,768]{4,3,2,1,0:T(8,128)(2,1)} %bitcast.18, bf16[1,1536]{1,0:T(2,128)(2,1)} %gain.1, bf16[1,1536,3072]{2,1,0:T(8,128)(2,1)} %wq.1, bf16[1,1536,128]{2,1,0:T(8,128)(2,1)} %wkv.1, ...), custom_call_target="tpu_custom_call" | custom-call | flops 21843935232 | bytes 85327872 | tf_op jit(solution)/shard_map/project/pallas_call | solution.py:317
  70.4 0.8 collective-permute-start
  71.2 1.0 slice.6
  72.2 1.3 copy.17
  73.5 0.1 copy.19
  73.6 0.8 copy.16
  74.4 0.6 slice_bitcast_fusion.kv_ref
  75.0 27.5 %attend.1 = (bf16[1,32,2048,128]{3,2,1,0:T(8,128)(2,1)}, bf16[1,32,2048,128]{3,2,1,0:T(8,128)(2,1)}, bf16[32,48,128]{2,1,0:T(8,128)(2,1)}) custom-call(s32[32]{0:T(128)} %lens.1, bf16[32,48,128]{2,1,0:T(8,128)(2,1)} %bitcast.21, bf16[32,2,128]{2,1,0:T(2,128)(2,1)} %slice_bitcast_fusion.kv_ref, bf16[1,32,2048,128]{3,2,1,0:T(8,128)(2,1)} %k_ref.1, ...), custom_call_target="tpu_custom_call" | custom-call | flops 10000000000 | bytes 67108864 | tf_op jit(solution)/shard_map/attend/pallas_call | solution.py:402
  102.5 1.2 reshape.27
  103.7 1.0 copy.21
  104.7 1.9 %collective-permute-done.recv_l = bf16[12,64,1024]{2,1,0:T(8,128)(2,1)} collective-permute-done((bf16[12,64,1024]{2,1,0:T(8,128)(2,1)}, bf16[12,64,1024]{2,1,0:T(8,128)(2,1)}, u32[]{:S(2)}, u32[]{:S(2)}) %collective-permute-start) | collective-permute-done | bytes 1572896 | tf_op jit(solution)/shard_map/ppermute | solution.py:693
  106.6 53.2 %finish.1 = bf16[4,64,768]{2,1,0:T(8,128)(2,1)S(1)} custom-call(bf16[2,6,32,512]{3,2,1,0:T(8,128)(2,1)} %bitcast.20, bf16[24,64,1024]{2,1,0:T(8,128)(2,1)} %get-tuple-element.12.keep, bf16[12,64,1024]{2,1,0:T(8,128)(2,1)} %get-tuple-element.13.recv_e, bf16[12,64,1024]{2,1,0:T(8,128)(2,1)} %collective-permute-done.recv_l, bf16[4,64,768]{2,1,0:T(8,128)(2,1)} %bitcast.19, ...), custom_call_target="tpu_custom_call" | custom-call | flops 12079595520 | bytes 47185920 | tf_op jit(solution)/shard_map/finish/pallas_call | solution.py:643
  159.8 0.7 copy.23
Async XLA Ops:
  70.4 36.2 %collective-permute-start = (bf16[12,64,1024]{2,1,0:T(8,128)(2,1)}, bf16[12,64,1024]{2,1,0:T(8,128)(2,1)}, u32[]{:S(2)}, u32[]{:S(2)}) collective-permute-start(bf16[12,64,1024]{2,1,0:T(8,128)(2,1)} %get-tuple-element.14), channel_id=1, source_target_pairs={{0,2},{1,3},{2,0},{3,1},{4,6},{5,7},{6,4},{7,5}} | collective-permute-start | bytes 4718600 | tf_op jit(solution)/shard_map/ppermute | solution.py:693

commit v4 on v3

--- a/solution.py
+++ b/solution.py
@@ -9,7 +9,7 @@
 
 NORM_EPS = 1e-6
 W = 512
-NBUF1 = 4
+NBUF1 = 6
 NBUF3 = 6
 GROUP = 3
 PARTS = ((0, 32), (32, 16), (48, 16))
@@ -50,6 +50,7 @@
     me = xi * 2 + yj
     half = hidden.shape[-1]
     n_all = n_q + n_ff
+    n_far = n_q + EARLY
     to_mate = dev(x=mate, yz=yj)
     to_across = dev(x=across, yz=yj)
 
@@ -179,68 +180,85 @@
         def _():
             start_weights(g + NBUF1)
 
-    def reduce_near(g, send):
+    def reduce_near(g):
         near_copy(g).wait_recv()
         far_src[g] = add(part[g, 1 - chip, :, core], near[g, 1 - chip]).reshape(64, 2 * W)
-        if send:
+
+        @pl.when(g < n_far)
+        def _():
             far_copy(g).start()
-        else:
+
+        @pl.when(g >= n_far)
+        def _():
             send_copy(g).start()
+
         keep[g] = add(part[g, chip, :, core], near[g, chip]).reshape(64, 2 * W)
         keep_copy(g).start()
 
-    for step in range(4):
+    def multiply_q(step, g):
+        side, piece = side_of(step), step % 2
+        if g == n_q:
+            if step == 0:
+                kv_copy.wait()
+            res = jnp.dot(u[side, piece], wkv_buf[...], preferred_element_type=F32).astype(BF16)
+            part_kv[side, piece] = res.reshape(2, 32, res.shape[1])
+            near_copy_kv(step).start()
+            return
+        for k in range(2):
+            if step == 0:
+                wait_weights(g, k)
+            res = jnp.dot(u[side, piece], wbuf[g, k], preferred_element_type=F32).astype(BF16)
+            part[g, side, piece, :, :, k * W:(k + 1) * W] = res.reshape(2, 32, W)
+        near_copy_q(g, step).start()
+        if step == 3:
+            start_weights(jnp.int32(g + NBUF1))
+
+    def reduce_q(step, g):
         side, piece = side_of(step), step % 2
         rows = slice(32 * piece, 32 * piece + 32)
+        if g == n_q:
+            near_copy_kv(step).wait_recv()
+            total_q = add(part_kv[side, piece, core], near_kv[side, piece])
+            if step < 2:
+                far_src_kv[rows] = total_q
+                far_copy_kv(step).start()
+            else:
+                keep_kv[rows] = total_q
+            return
+        near_copy_q(g, step).wait_recv()
+        total_q = add(part[g, side, piece, core], near[g, side, piece])
+        if step < 2:
+            far_src[g, rows] = total_q
+            far_copy_q(g, step).start()
+        else:
+            keep[g, rows] = total_q
+
+    for step in range(4):
         normalize(h_own, step, yj)
         h_copy(step).wait_recv()
         normalize(h_other, step, other_y)
-
-        def reduce_q(g):
-            near_copy_q(g, step).wait_recv()
-            total_q = add(part[g, side, piece, core], near[g, side, piece])
-            if step < 2:
-                far_src[g, rows] = total_q
-                far_copy_q(g, step).start()
-            else:
-                keep[g, rows] = total_q
-
-        for g in range(n_q):
-            for k in range(2):
-                if step == 0:
-                    wait_weights(g, k)
-                res = jnp.dot(u[side, piece], wbuf[g, k], preferred_element_type=F32).astype(BF16)
-                part[g, side, piece, :, :, k * W:(k + 1) * W] = res.reshape(2, 32, W)
-            near_copy_q(g, step).start()
-            if step == 3:
-                start_weights(jnp.int32(g + NBUF1))
-            if g >= 1:
-                reduce_q(g - 1)
+        for g in range(n_q + 1):
+            multiply_q(step, g)
+            if step == 0 and g >= 2:
+                reduce_q(0, g - 2)
+            if step == 2:
+                reduce_q(1, g)
         if step == 0:
-            kv_copy.wait()
-        res = jnp.dot(u[side, piece], wkv_buf[...], preferred_element_type=F32).astype(BF16)
-        part_kv[side, piece] = res.reshape(2, 32, res.shape[1])
-        near_copy_kv(step).start()
-        reduce_q(n_q - 1)
-        near_copy_kv(step).wait_recv()
-        total_kv = add(part_kv[side, piece, core], near_kv[side, piece])
-        if step < 2:
-            far_src_kv[rows] = total_kv
-            far_copy_kv(step).start()
-        else:
-            keep_kv[rows] = total_kv
-
-    n_far = n_q + EARLY
+            reduce_q(0, n_q - 1)
+            reduce_q(0, n_q)
 
     @pl.loop(n_q, n_far)
     def _(g):
         multiply(g)
 
-        @pl.when(g >= n_q + 1)
-        def _():
-            reduce_near(g - 1, True)
+        @pl.when(g >= n_q + 2)
+        def _():
+            reduce_near(g - 2)
 
     q_cols = n_q * 2 * W
+    for g in range(n_q + 1):
+        reduce_q(2, g)
+        reduce_q(3, g)
     for g in range(n_q):
         for step in range(2):
             far_copy_q(g, step).wait_recv()
@@ -256,15 +274,13 @@
     qkv_own = pltpu.make_async_copy(z_rows.at[yj], qkv_out.at[yj], qkv_sem.at[0])
     qkv_own.start()
 
-    multiply(n_far)
-    reduce_near(n_far - 1, True)
-
-    @pl.loop(n_far + 1, n_all)
+    @pl.loop(n_far, n_all)
     def _(g):
         multiply(g)
-        reduce_near(g - 1, False)
-
-    reduce_near(n_all - 1, False)
+        reduce_near(g - 2)
+
+    reduce_near(jnp.int32(n_all - 2))
+    reduce_near(jnp.int32(n_all - 1))
     y_copy.wait_recv()
     qkv_other = pltpu.make_async_copy(z_other, qkv_out.at[other_y], qkv_sem.at[1])
     qkv_other.start()

time: 161 us -> 160 us (level)
  no operation moved by 1% of the time
where the time goes in v4:
time: 160 us; the launch traced here: 159 us
  Pallas kernels  149 us (93%)
  local copies, waits for them, and re-layouts  6.74 us (4%)
  waiting for transfers between devices  2.25 us (1%)
    pallas_call x1, Pallas kernels, project(): pl.pallas_call(functools.partial(project_kernel, n_q, n_ff, d_model), nam...  68.2 us
    pallas_call x1, Pallas kernels, finish(): pl.pallas_call(functools.partial(output_kernel, n_ff, n_o), name='finish'...  53.3 us
    pallas_call x1, Pallas kernels, attend(): pl.pallas_call(attend_kernel, name='attend', out_shape=(jax.ShapeDtypeStr...  27.5 us
  transfers between devices with their start and end apart: 1, of which 1 were waited for; matrix products, arithmetic and copies ran while one was open for 4% of the time, Pallas kernels for 17%

profile of v4, /device:TPU:0, one launch (start us, length us, event | category | flops | bytes accessed | tf_op | source)
XLA Modules:
  0.0 159.5 jit_solution(7059760597170519341)
XLA Ops:
  0.6 68.2 %project.1 = (bf16[2,32,3200]{2,1,0:T(8,128)(2,1)}, bf16[24,64,1024]{2,1,0:T(8,128)(2,1)}, bf16[12,64,1024]{2,1,0:T(8,128)(2,1)}, bf16[12,64,1024]{2,1,0:T(8,128)(2,1)}) custom-call(bf16[2,2,2,32,768]{4,3,2,1,0:T(8,128)(2,1)} %bitcast.18, bf16[1,1536]{1,0:T(2,128)(2,1)} %gain.1, bf16[1,1536,3072]{2,1,0:T(8,128)(2,1)} %wq.1, bf16[1,1536,128]{2,1,0:T(8,128)(2,1)} %wkv.1, ...), custom_call_target="tpu_custom_call" | custom-call | flops 21843935232 | bytes 85327872 | tf_op jit(solution)/shard_map/project/pallas_call | solution.py:333
  68.9 0.7 collective-permute-start
  69.6 1.0 slice.6
  70.6 1.3 copy.17
  72.0 0.1 copy.19
  72.0 0.8 copy.16
  72.8 0.6 slice_bitcast_fusion.kv_ref
  73.4 27.5 %attend.1 = (bf16[1,32,2048,128]{3,2,1,0:T(8,128)(2,1)}, bf16[1,32,2048,128]{3,2,1,0:T(8,128)(2,1)}, bf16[32,48,128]{2,1,0:T(8,128)(2,1)}) custom-call(s32[32]{0:T(128)} %lens.1, bf16[32,48,128]{2,1,0:T(8,128)(2,1)} %bitcast.21, bf16[32,2,128]{2,1,0:T(2,128)(2,1)} %slice_bitcast_fusion.kv_ref, bf16[1,32,2048,128]{3,2,1,0:T(8,128)(2,1)} %k_ref.1, ...), custom_call_target="tpu_custom_call" | custom-call | flops 10000000000 | bytes 67108864 | tf_op jit(solution)/shard_map/attend/pallas_call | solution.py:418
  100.9 1.2 reshape.27
  102.2 1.0 copy.21
  103.1 2.3 %collective-permute-done.recv_l = bf16[12,64,1024]{2,1,0:T(8,128)(2,1)} collective-permute-done((bf16[12,64,1024]{2,1,0:T(8,128)(2,1)}, bf16[12,64,1024]{2,1,0:T(8,128)(2,1)}, u32[]{:S(2)}, u32[]{:S(2)}) %collective-permute-start) | collective-permute-done | bytes 1572896 | tf_op jit(solution)/shard_map/ppermute | solution.py:709
  105.4 53.3 %finish.1 = bf16[4,64,768]{2,1,0:T(8,128)(2,1)S(1)} custom-call(bf16[2,6,32,512]{3,2,1,0:T(8,128)(2,1)} %bitcast.20, bf16[24,64,1024]{2,1,0:T(8,128)(2,1)} %get-tuple-element.12.keep, bf16[12,64,1024]{2,1,0:T(8,128)(2,1)} %get-tuple-element.13.recv_e, bf16[12,64,1024]{2,1,0:T(8,128)(2,1)} %collective-permute-done.recv_l, bf16[4,64,768]{2,1,0:T(8,128)(2,1)} %bitcast.19, ...), custom_call_target="tpu_custom_call" | custom-call | flops 12079595520 | bytes 47185920 | tf_op jit(solution)/shard_map/finish/pallas_call | solution.py:659
  158.7 0.7 copy.23
Async XLA Ops:
  68.9 36.5 %collective-permute-start = (bf16[12,64,1024]{2,1,0:T(8,128)(2,1)}, bf16[12,64,1024]{2,1,0:T(8,128)(2,1)}, u32[]{:S(2)}, u32[]{:S(2)}) collective-permute-start(bf16[12,64,1024]{2,1,0:T(8,128)(2,1)} %get-tuple-element.14), channel_id=1, source_target_pairs={{0,2},{1,3},{2,0},{3,1},{4,6},{5,7},{6,4},{7,5}} | collective-permute-start | bytes 4718600 | tf_op jit(solution)/shard_map/ppermute | solution.py:709

commit v5 on v4

--- a/solution.py
+++ b/solution.py
@@ -9,7 +9,7 @@
 
 NORM_EPS = 1e-6
 W = 512
-NBUF1 = 6
+NBUF1 = 4
 NBUF3 = 6
 GROUP = 3
 PARTS = ((0, 32), (32, 16), (48, 16))
@@ -35,10 +35,10 @@
 def project_kernel(
     n_q, n_ff, d_model, hidden, gain, wq, wkv, wg, wu,
     qkv_out, keep_out, recv_out, send_out,
-    h_own, h_other, u, inv_all, sq_all, wbuf, wkv_buf, part, part_kv, near, near_kv, keep, keep_kv, far_src,
-    far_src_kv, far_q, far_kv, z_rows, z_other,
-    w_sem, wkv_sem, h_in, h_sems, sq_send, sq_recv, near_send, near_recv, qn_send, qn_recv, kn_send, kn_recv,
-    far_send, far_recv, qf_send, qf_recv, kf_send, kf_recv, y_sems, out_sem, qkv_sem,
+    h_own, h_other, u, inv_all, sq_all, wq_buf, wbuf, wkv_buf, part, part_kv, near, near_kv, keep, keep_kv, far_src,
+    far_src_kv, far, far_kv, z_rows, z_other,
+    wq_sem, w_sem, wkv_sem, h_in, h_sems, sq_send, sq_recv, near_send, near_recv, qn_send, qn_recv, kn_send, kn_recv,
+    far_send, far_recv, kf_sems, y_sems, out_sem, recv_sem, qkv_sem,
 ):
     xi = lax.axis_index("x")
     yj = lax.axis_index("yz")
@@ -63,29 +63,25 @@
 
     def start_weights(g):
         slot = lax.rem(g, NBUF1)
-
-        @pl.when(g < n_q)
-        def _():
-            for k in range(2):
-                cols = pl.ds(pl.multiple_of((2 * g + k) * W, W), W)
-                pltpu.make_async_copy(wq.at[0, :, cols], wbuf.at[slot, k], w_sem.at[slot, k]).start()
-
-        @pl.when(g >= n_q)
-        def _():
-            cols = pl.ds(pl.multiple_of((g - n_q) * W, W), W)
-            pltpu.make_async_copy(wg.at[0, :, cols], wbuf.at[slot, 0], w_sem.at[slot, 0]).start()
-            pltpu.make_async_copy(wu.at[0, :, cols], wbuf.at[slot, 1], w_sem.at[slot, 1]).start()
+        cols = pl.ds(pl.multiple_of((g - n_q) * W, W), W)
+        pltpu.make_async_copy(wg.at[0, :, cols], wbuf.at[slot, 0], w_sem.at[slot, 0]).start()
+        pltpu.make_async_copy(wu.at[0, :, cols], wbuf.at[slot, 1], w_sem.at[slot, 1]).start()
 
     def wait_weights(slot, k):
-        pltpu.make_async_copy(wq.at[0, :, pl.ds(0, W)], wbuf.at[slot, k], w_sem.at[slot, k]).wait()
-
-    for g in range(NBUF1):
-        start_weights(jnp.int32(g))
+        pltpu.make_async_copy(wg.at[0, :, pl.ds(0, W)], wbuf.at[slot, k], w_sem.at[slot, k]).wait()
+
+    def wq_copy(g):
+        return pltpu.make_async_copy(wq.at[0, :, g * 2 * W:(g + 1) * 2 * W], wq_buf.at[g], wq_sem.at[g])
+
+    for g in range(n_q):
+        wq_copy(g).start()
     kv_copy = pltpu.make_async_copy(wkv.at[0], wkv_buf, wkv_sem)
     kv_copy.start()
+    for g in range(n_q, n_q + NBUF1):
+        start_weights(jnp.int32(g))
 
     h_load.wait()
-    h_f32 = h_own[...].reshape(256, half).astype(F32)
+    h_f32 = h_own[...].astype(F32)
     sq_all[me] = lax.dot_general(
         jnp.ones((8, half), F32), h_f32 * h_f32, (((1,), (1,)), ((), ())),
         precision=lax.Precision.HIGHEST, preferred_element_type=F32)
@@ -97,66 +93,57 @@
             **dev(x=peer // 2, yz=lax.rem(peer, 2)))
 
     def side_of(step):
-        return 1 - chip if step < 2 else chip
+        return 1 - chip if step == 0 else chip
+
+    def side_rows(step):
+        return pl.ds(pl.multiple_of(side_of(step) * 128, 128), 128)
 
     def h_copy(step):
-        block = (side_of(step), slice(None), step % 2)
-        return pltpu.make_async_remote_copy(
-            src_ref=h_own.at[block], dst_ref=h_other.at[block],
+        return pltpu.make_async_remote_copy(
+            src_ref=h_own.at[side_rows(step)], dst_ref=h_other.at[side_rows(step)],
             send_sem=h_sems.at[step, 0], recv_sem=h_sems.at[step, 1], **dev(x=xi, yz=other_y))
 
     for k in range(1, 8):
         sq_copy(lax.rem(me + k, 8), me).start()
-    for step in range(4):
+    for step in range(2):
         h_copy(step).start()
     for k in range(1, 8):
         peer = lax.rem(me + k, 8)
         sq_copy(peer, peer).wait_recv()
     total = jnp.sum(sq_all[...], axis=0)
     inv = lax.rsqrt(total / d_model + NORM_EPS)
-    inv_all[...] = jnp.transpose(jnp.concatenate([inv] * 16, axis=0)).reshape(inv_all.shape)
+    inv_all[...] = jnp.transpose(jnp.concatenate([inv] * 16, axis=0))
 
     def normalize(values, step, which):
         cols = pl.ds(pl.multiple_of(which * half, 128), half)
-        side, piece = side_of(step), step % 2
-        inv_rows = inv_all[side, :, piece].reshape(64, 128)[:, :1]
-        res = (values[side, :, piece].reshape(64, half).astype(F32) * inv_rows
-               * gain[:, cols].astype(F32)).astype(BF16)
-        u[side, piece, :, cols] = res
+        rows = side_rows(step)
+        u[rows, cols] = (
+            values[rows].astype(F32) * inv_all[rows, :1] * gain[:, cols].astype(F32)).astype(BF16)
 
     def near_copy(g):
         return pltpu.make_async_remote_copy(
-            src_ref=part.at[g, :, :, 1 - core], dst_ref=near.at[g], send_sem=near_send.at[g],
+            src_ref=part.at[g, :, 1 - core], dst_ref=near.at[g], send_sem=near_send.at[g],
             recv_sem=near_recv.at[g], **to_mate)
 
     def near_copy_q(g, step):
-        side, piece = side_of(step), step % 2
-        return pltpu.make_async_remote_copy(
-            src_ref=part.at[g, side, piece, 1 - core], dst_ref=near.at[g, side, piece],
+        side = side_of(step)
+        return pltpu.make_async_remote_copy(
+            src_ref=part.at[g, side, 1 - core], dst_ref=near.at[g, side],
             send_sem=qn_send.at[g, step], recv_sem=qn_recv.at[g, step], **to_mate)
 
     def near_copy_kv(step):
-        side, piece = side_of(step), step % 2
-        return pltpu.make_async_remote_copy(
-            src_ref=part_kv.at[side, piece, 1 - core], dst_ref=near_kv.at[side, piece],
+        side = side_of(step)
+        return pltpu.make_async_remote_copy(
+            src_ref=part_kv.at[side, 1 - core], dst_ref=near_kv.at[side],
             send_sem=kn_send.at[step], recv_sem=kn_recv.at[step], **to_mate)
 
     def far_copy(g):
         return pltpu.make_async_remote_copy(
-            src_ref=far_src.at[g], dst_ref=recv_out.at[g - n_q], send_sem=far_send.at[g - n_q],
-            recv_sem=far_recv.at[g - n_q], **to_across)
-
-    def far_copy_q(g, step):
-        rows = slice(32 * step, 32 * step + 32)
-        return pltpu.make_async_remote_copy(
-            src_ref=far_src.at[g, rows], dst_ref=far_q.at[g, rows], send_sem=qf_send.at[g, step],
-            recv_sem=qf_recv.at[g, step], **to_across)
-
-    def far_copy_kv(step):
-        rows = slice(32 * step, 32 * step + 32)
-        return pltpu.make_async_remote_copy(
-            src_ref=far_src_kv.at[rows], dst_ref=far_kv.at[rows], send_sem=kf_send.at[step],
-            recv_sem=kf_recv.at[step], **to_across)
+            src_ref=far_src.at[g], dst_ref=far.at[g], send_sem=far_send.at[g], recv_sem=far_recv.at[g], **to_across)
+
+    def far_copy_kv():
+        return pltpu.make_async_remote_copy(
+            src_ref=far_src_kv, dst_ref=far_kv, send_sem=kf_sems.at[0], recv_sem=kf_sems.at[1], **to_across)
 
     def keep_copy(g):
         return pltpu.make_async_copy(keep.at[g], keep_out.at[g - n_q], out_sem.at[g - n_q, 0])
@@ -164,6 +151,9 @@
     def send_copy(g):
         k = g - n_q
         return pltpu.make_async_copy(far_src.at[g], send_out.at[k - EARLY], out_sem.at[k, 1])
+
+    def recv_copy(g):
+        return pltpu.make_async_copy(far.at[g], recv_out.at[g - n_q], recv_sem.at[g - n_q])
 
     def add(a, b):
         return (a.astype(F32) + b.astype(F32)).astype(BF16)
@@ -172,8 +162,8 @@
         slot = lax.rem(g, NBUF1)
         for k in range(2):
             wait_weights(slot, k)
-            res = jnp.dot(u[...].reshape(256, u.shape[-1]), wbuf[slot, k], preferred_element_type=F32).astype(BF16)
-            part[g, :, :, :, :, k * W:(k + 1) * W] = res.reshape(2, 2, 2, 32, W)
+            res = jnp.dot(u[...], wbuf[slot, k], preferred_element_type=F32).astype(BF16)
+            part[g, :, :, :, k * W:(k + 1) * W] = res.reshape(2, 2, 64, W)
         near_copy(g).start()
 
         @pl.when(g + NBUF1 < n_all)
@@ -182,7 +172,7 @@
 
     def reduce_near(g):
         near_copy(g).wait_recv()
-        far_src[g] = add(part[g, 1 - chip, :, core], near[g, 1 - chip]).reshape(64, 2 * W)
+        far_src[g] = add(part[g, 1 - chip, core], near[g, 1 - chip])
 
         @pl.when(g < n_far)
         def _():
@@ -192,60 +182,57 @@
         def _():
             send_copy(g).start()
 
-        keep[g] = add(part[g, chip, :, core], near[g, chip]).reshape(64, 2 * W)
+        keep[g] = add(part[g, chip, core], near[g, chip])
         keep_copy(g).start()
 
-    def multiply_q(step, g):
-        side, piece = side_of(step), step % 2
-        if g == n_q:
+    def multiply_q(step):
+        side = side_of(step)
+        for g in range(n_q):
             if step == 0:
-                kv_copy.wait()
-            res = jnp.dot(u[side, piece], wkv_buf[...], preferred_element_type=F32).astype(BF16)
-            part_kv[side, piece] = res.reshape(2, 32, res.shape[1])
-            near_copy_kv(step).start()
-            return
-        for k in range(2):
-            if step == 0:
-                wait_weights(g, k)
-            res = jnp.dot(u[side, piece], wbuf[g, k], preferred_element_type=F32).astype(BF16)
-            part[g, side, piece, :, :, k * W:(k + 1) * W] = res.reshape(2, 32, W)
-        near_copy_q(g, step).start()
-        if step == 3:
-            start_weights(jnp.int32(g + NBUF1))
-
-    def reduce_q(step, g):
-        side, piece = side_of(step), step % 2
-        rows = slice(32 * piece, 32 * piece + 32)
-        if g == n_q:
-            near_copy_kv(step).wait_recv()
-            total_q = add(part_kv[side, piece, core], near_kv[side, piece])
-            if step < 2:
-                far_src_kv[rows] = total_q
-                far_copy_kv(step).start()
-            else:
-                keep_kv[rows] = total_q
-            return
-        near_copy_q(g, step).wait_recv()
-        total_q = add(part[g, side, piece, core], near[g, side, piece])
-        if step < 2:
-            far_src[g, rows] = total_q
-            far_copy_q(g, step).start()
-        else:
-            keep[g, rows] = total_q
-
-    for step in range(4):
-        normalize(h_own, step, yj)
-        h_copy(step).wait_recv()
-        normalize(h_other, step, other_y)
-        for g in range(n_q + 1):
-            multiply_q(step, g)
+                wq_copy(g).wait()
+            for k in range(2):
+                res = jnp.dot(
+                    u[side_rows(step)], wq_buf[g, :, k * W:(k + 1) * W], preferred_element_type=F32).astype(BF16)
+                part[g, side, :, :, k * W:(k + 1) * W] = res.reshape(2, 64, W)
+            near_copy_q(g, step).start()
             if step == 0 and g >= 2:
                 reduce_q(0, g - 2)
-            if step == 2:
-                reduce_q(1, g)
         if step == 0:
-            reduce_q(0, n_q - 1)
-            reduce_q(0, n_q)
+            kv_copy.wait()
+        res = jnp.dot(u[side_rows(step)], wkv_buf[...], preferred_element_type=F32).astype(BF16)
+        part_kv[side] = res.reshape(2, 64, res.shape[1])
+        near_copy_kv(step).start()
+
+    def reduce_q(step, g):
+        side = side_of(step)
+        near_copy_q(g, step).wait_recv()
+        total_q = add(part[g, side, core], near[g, side])
+        if step == 0:
+            far_src[g] = total_q
+            far_copy(g).start()
+        else:
+            keep[g] = total_q
+
+    def reduce_kv(step):
+        side = side_of(step)
+        near_copy_kv(step).wait_recv()
+        total_kv = add(part_kv[side, core], near_kv[side])
+        if step == 0:
+            far_src_kv[...] = total_kv
+            far_copy_kv().start()
+        else:
+            keep_kv[...] = total_kv
+
+    normalize(h_own, 0, yj)
+    h_copy(0).wait_recv()
+    normalize(h_other, 0, other_y)
+    multiply_q(0)
+    for g in range(n_q - 2, n_q):
+        reduce_q(0, g)
+    reduce_kv(0)
+    normalize(h_own, 1, yj)
+    h_copy(1).wait_recv()
+    normalize(h_other, 1, other_y)
 
     @pl.loop(n_q, n_far)
     def _(g):
@@ -256,15 +243,13 @@
             reduce_near(g - 2)
 
     q_cols = n_q * 2 * W
-    for g in range(n_q + 1):
-        reduce_q(2, g)
-        reduce_q(3, g)
+    multiply_q(1)
     for g in range(n_q):
-        for step in range(2):
-            far_copy_q(g, step).wait_recv()
-        z_rows[:, :, g * 2 * W:(g + 1) * 2 * W] = add(keep[g], far_q[g]).reshape(2, 32, 2 * W)
-    for step in range(2):
-        far_copy_kv(step).wait_recv()
+        reduce_q(1, g)
+        far_copy(g).wait_recv()
+        z_rows[:, :, g * 2 * W:(g + 1) * 2 * W] = add(keep[g], far[g]).reshape(2, 32, 2 * W)
+    reduce_kv(1)
+    far_copy_kv().wait_recv()
     z_kv = add(keep_kv[...], far_kv[...])
     z_rows[:, :, q_cols:] = z_kv.reshape(2, 32, z_kv.shape[1])
     y_copy = pltpu.make_async_remote_copy(
@@ -285,15 +270,17 @@
     qkv_other = pltpu.make_async_copy(z_other, qkv_out.at[other_y], qkv_sem.at[1])
     qkv_other.start()
 
-    for step in range(4):
+    @pl.loop(n_q, n_far)
+    def _(g):
+        far_copy(g).wait_recv()
+        recv_copy(g).start()
+
+    for step in range(2):
         h_copy(step).wait_send()
         near_copy_kv(step).wait_send()
         for g in range(n_q):
             near_copy_q(g, step).wait_send()
-    for step in range(2):
-        far_copy_kv(step).wait_send()
-        for g in range(n_q):
-            far_copy_q(g, step).wait_send()
+    far_copy_kv().wait_send()
     for k in range(1, 8):
         sq_copy(lax.rem(me + k, 8), me).wait_send()
     y_copy.wait_send()
@@ -307,13 +294,16 @@
     def _(g):
         send_copy(g).wait()
 
+    @pl.loop(0, n_far)
+    def _(g):
+        far_copy(g).wait_send()
+
     qkv_own.wait()
     qkv_other.wait()
 
     @pl.loop(n_q, n_far)
     def _(g):
-        far_copy(g).wait_send()
-        far_copy(g).wait_recv()
+        recv_copy(g).wait()
 
 
 def project(hidden, gain, w_q, w_kv, w_gate, w_up, d_model):
@@ -329,7 +319,6 @@
     vmem = pl.BlockSpec(memory_space=pltpu.VMEM)
     cols = w_q.shape[2] + kv
     flops = 2 * rows * feats * (w_q.shape[2] + kv + 2 * w_gate.shape[2])
-    h_shape = (2, 2, 2, 32, half)
     return pl.pallas_call(
         functools.partial(project_kernel, n_q, n_ff, d_model),
         name="project",
@@ -342,50 +331,50 @@
         in_specs=[any_spec, vmem, any_spec, any_spec, any_spec, any_spec],
         out_specs=(any_spec, any_spec, any_spec, any_spec),
         scratch_shapes=[
-            pltpu.VMEM(h_shape, BF16),
-            pltpu.VMEM(h_shape, BF16),
-            pltpu.VMEM((2, 2, 64, feats), BF16),
-            pltpu.VMEM((2, 2, 2, 32, 128), F32),
+            pltpu.VMEM((rows, half), BF16),
+            pltpu.VMEM((rows, half), BF16),
+            pltpu.VMEM((rows, feats), BF16),
+            pltpu.VMEM((rows, 128), F32),
             pltpu.VMEM((8, 8, rows), F32),
+            pltpu.VMEM((n_q, feats, 2 * W), BF16),
             pltpu.VMEM((NBUF1, 2, feats, W), BF16),
             pltpu.VMEM((feats, kv), BF16),
-            pltpu.VMEM((n_all, 2, 2, 2, 32, 2 * W), BF16),
-            pltpu.VMEM((2, 2, 2, 32, kv), BF16),
-            pltpu.VMEM((n_all, 2, 2, 32, 2 * W), BF16),
-            pltpu.VMEM((2, 2, 32, kv), BF16),
+            pltpu.VMEM((n_all, 2, 2, 64, 2 * W), BF16),
+            pltpu.VMEM((2, 2, 64, kv), BF16),
+            pltpu.VMEM((n_all, 2, 64, 2 * W), BF16),
+            pltpu.VMEM((2, 64, kv), BF16),
             pltpu.VMEM((n_all, 64, 2 * W), BF16),
             pltpu.VMEM((64, kv), BF16),
             pltpu.VMEM((n_all, 64, 2 * W), BF16),
             pltpu.VMEM((64, kv), BF16),
-            pltpu.VMEM((n_q, 64, 2 * W), BF16),
+            pltpu.VMEM((n_q + EARLY, 64, 2 * W), BF16),
             pltpu.VMEM((64, kv), BF16),
             pltpu.VMEM((2, 32, cols), BF16),
             pltpu.VMEM((32, cols), BF16),
+            dma((n_q,)),
             dma((NBUF1, 2)),
             dma,
             dma,
-            dma((4, 2)),
+            dma((2, 2)),
             dma((8,)),
             dma((8,)),
             dma((n_all,)),
             dma((n_all,)),
-            dma((n_q, 4)),
-            dma((n_q, 4)),
-            dma((4,)),
-            dma((4,)),
-            dma((EARLY,)),
-            dma((EARLY,)),
             dma((n_q, 2)),
             dma((n_q, 2)),
             dma((2,)),
             dma((2,)),
+            dma((n_q + EARLY,)),
+            dma((n_q + EARLY,)),
+            dma((2,)),
             dma((2,)),
             dma((n_ff, 2)),
+            dma((EARLY,)),
             dma((2,)),
         ],
         compiler_params=pltpu.CompilerParams(collective_id=0, has_side_effects=True, vmem_limit_bytes=VMEM_LIMIT),
         cost_estimate=pl.CostEstimate(flops=flops, bytes_accessed=feats * (flops // (rows * feats)), transcendentals=0),
-    )(hidden.reshape(h_shape), gain, w_q, w_kv, w_gate, w_up)
+    )(hidden, gain, w_q, w_kv, w_gate, w_up)
 
 
 def attend_kernel(lens, q_ref, kv_ref, k_ref, v_ref, k_out, v_out, o_ref):

time: 160 us -> 158 us (0.988)
  no operation moved by 1% of the time
where the time goes in v5:
time: 158 us
  Pallas kernels  148 us (94%)
  local copies, waits for them, and re-layouts  6.74 us (4%)
    pallas_call x1, Pallas kernels, project(): pl.pallas_call(functools.partial(project_kernel, n_q, n_ff, d_model), nam...  67.5 us
    pallas_call x1, Pallas kernels, finish(): pl.pallas_call(functools.partial(output_kernel, n_ff, n_o), name='finish'...  53.1 us
    pallas_call x1, Pallas kernels, attend(): pl.pallas_call(attend_kernel, name='attend', out_shape=(jax.ShapeDtypeStr...  27.5 us
  transfers between devices with their start and end apart: 1, of which 1 were waited for; matrix products, arithmetic and copies ran while one was open for 4% of the time, Pallas kernels for 17%

profile of v5, /device:TPU:0, one launch (start us, length us, event | category | flops | bytes accessed | tf_op | source)
XLA Modules:
  0.0 157.7 jit_solution(15544366811352456614)
XLA Ops:
  0.6 67.5 %project.1 = (bf16[2,32,3200]{2,1,0:T(8,128)(2,1)}, bf16[24,64,1024]{2,1,0:T(8,128)(2,1)}, bf16[12,64,1024]{2,1,0:T(8,128)(2,1)}, bf16[12,64,1024]{2,1,0:T(8,128)(2,1)}) custom-call(bf16[256,768]{1,0:T(8,128)(2,1)} %hidden.1, bf16[1,1536]{1,0:T(2,128)(2,1)} %gain.1, bf16[1,1536,3072]{2,1,0:T(8,128)(2,1)} %wq.1, bf16[1,1536,128]{2,1,0:T(8,128)(2,1)} %wkv.1, ...), custom_call_target="tpu_custom_call" | custom-call | flops 21843935232 | bytes 85327872 | tf_op jit(solution)/shard_map/project/pallas_call | solution.py:322
  68.1 0.8 collective-permute-start
  68.9 1.0 slice.6
  69.9 1.3 copy.17
  71.2 0.1 copy.19
  71.3 0.8 copy.16
  72.1 0.6 slice_bitcast_fusion.kv_ref
  72.7 27.5 %attend.1 = (bf16[1,32,2048,128]{3,2,1,0:T(8,128)(2,1)}, bf16[1,32,2048,128]{3,2,1,0:T(8,128)(2,1)}, bf16[32,48,128]{2,1,0:T(8,128)(2,1)}) custom-call(s32[32]{0:T(128)} %lens.1, bf16[32,48,128]{2,1,0:T(8,128)(2,1)} %bitcast.19, bf16[32,2,128]{2,1,0:T(2,128)(2,1)} %slice_bitcast_fusion.kv_ref, bf16[1,32,2048,128]{3,2,1,0:T(8,128)(2,1)} %k_ref.1, ...), custom_call_target="tpu_custom_call" | custom-call | flops 10000000000 | bytes 67108864 | tf_op jit(solution)/shard_map/attend/pallas_call | solution.py:407
  100.2 1.2 reshape.23
  101.4 1.0 copy.21
  102.4 1.4 collective-permute-done.recv_l
  103.8 53.1 %finish.1 = bf16[4,64,768]{2,1,0:T(8,128)(2,1)S(1)} custom-call(bf16[2,6,32,512]{3,2,1,0:T(8,128)(2,1)} %bitcast.18, bf16[24,64,1024]{2,1,0:T(8,128)(2,1)} %get-tuple-element.12.keep, bf16[12,64,1024]{2,1,0:T(8,128)(2,1)} %get-tuple-element.13.recv_e, bf16[12,64,1024]{2,1,0:T(8,128)(2,1)} %collective-permute-done.recv_l, bf16[4,64,768]{2,1,0:T(8,128)(2,1)} %bitcast.17, ...), custom_call_target="tpu_custom_call" | custom-call | flops 12079595520 | bytes 47185920 | tf_op jit(solution)/shard_map/finish/pallas_call | solution.py:648
  157.0 0.7 copy.23
Async XLA Ops:
  68.1 35.7 %collective-permute-start = (bf16[12,64,1024]{2,1,0:T(8,128)(2,1)}, bf16[12,64,1024]{2,1,0:T(8,128)(2,1)}, u32[]{:S(2)}, u32[]{:S(2)}) collective-permute-start(bf16[12,64,1024]{2,1,0:T(8,128)(2,1)} %get-tuple-element.14), channel_id=1, source_target_pairs={{0,2},{1,3},{2,0},{3,1},{4,6},{5,7},{6,4},{7,5}} | collective-permute-start | bytes 4718600 | tf_op jit(solution)/shard_map/ppermute | solution.py:698

commit v6 on v5

--- a/solution.py
+++ b/solution.py
@@ -38,7 +38,7 @@
     h_own, h_other, u, inv_all, sq_all, wq_buf, wbuf, wkv_buf, part, part_kv, near, near_kv, keep, keep_kv, far_src,
     far_src_kv, far, far_kv, z_rows, z_other,
     wq_sem, w_sem, wkv_sem, h_in, h_sems, sq_send, sq_recv, near_send, near_recv, qn_send, qn_recv, kn_send, kn_recv,
-    far_send, far_recv, kf_sems, y_sems, out_sem, recv_sem, qkv_sem,
+    far_send, far_recv, qf_send, qf_recv, kf_send, kf_recv, y_sems, out_sem, recv_sem, qkv_sem,
 ):
     xi = lax.axis_index("x")
     yj = lax.axis_index("yz")
@@ -73,6 +73,7 @@
     def wq_copy(g):
         return pltpu.make_async_copy(wq.at[0, :, g * 2 * W:(g + 1) * 2 * W], wq_buf.at[g], wq_sem.at[g])
 
+    h_load.wait()
     for g in range(n_q):
         wq_copy(g).start()
     kv_copy = pltpu.make_async_copy(wkv.at[0], wkv_buf, wkv_sem)
@@ -80,8 +81,7 @@
     for g in range(n_q, n_q + NBUF1):
         start_weights(jnp.int32(g))
 
-    h_load.wait()
-    h_f32 = h_own[...].astype(F32)
+    h_f32 = h_own[...].reshape(256, half).astype(F32)
     sq_all[me] = lax.dot_general(
         jnp.ones((8, half), F32), h_f32 * h_f32, (((1,), (1,)), ((), ())),
         precision=lax.Precision.HIGHEST, preferred_element_type=F32)
@@ -93,32 +93,33 @@
             **dev(x=peer // 2, yz=lax.rem(peer, 2)))
 
     def side_of(step):
-        return 1 - chip if step == 0 else chip
-
-    def side_rows(step):
-        return pl.ds(pl.multiple_of(side_of(step) * 128, 128), 128)
+        return 1 - chip if step < 2 else chip
+
+    def piece(step):
+        return pl.ds(32 * step, 32) if step < 2 else pl.ds(0, 64)
 
     def h_copy(step):
-        return pltpu.make_async_remote_copy(
-            src_ref=h_own.at[side_rows(step)], dst_ref=h_other.at[side_rows(step)],
+        block = (side_of(step), slice(None), piece(step))
+        return pltpu.make_async_remote_copy(
+            src_ref=h_own.at[block], dst_ref=h_other.at[block],
             send_sem=h_sems.at[step, 0], recv_sem=h_sems.at[step, 1], **dev(x=xi, yz=other_y))
 
     for k in range(1, 8):
         sq_copy(lax.rem(me + k, 8), me).start()
-    for step in range(2):
+    for step in range(3):
         h_copy(step).start()
     for k in range(1, 8):
         peer = lax.rem(me + k, 8)
         sq_copy(peer, peer).wait_recv()
     total = jnp.sum(sq_all[...], axis=0)
     inv = lax.rsqrt(total / d_model + NORM_EPS)
-    inv_all[...] = jnp.transpose(jnp.concatenate([inv] * 16, axis=0))
+    inv_all[...] = jnp.transpose(jnp.concatenate([inv] * 16, axis=0)).reshape(inv_all.shape)
 
     def normalize(values, step, which):
         cols = pl.ds(pl.multiple_of(which * half, 128), half)
-        rows = side_rows(step)
-        u[rows, cols] = (
-            values[rows].astype(F32) * inv_all[rows, :1] * gain[:, cols].astype(F32)).astype(BF16)
+        side, rows = side_of(step), piece(step)
+        u[side, :, rows, cols] = (
+            values[side, :, rows].astype(F32) * inv_all[side, :, rows, :1] * gain[:, cols].astype(F32)).astype(BF16)
 
     def near_copy(g):
         return pltpu.make_async_remote_copy(
@@ -126,24 +127,33 @@
             recv_sem=near_recv.at[g], **to_mate)
 
     def near_copy_q(g, step):
-        side = side_of(step)
-        return pltpu.make_async_remote_copy(
-            src_ref=part.at[g, side, 1 - core], dst_ref=near.at[g, side],
+        side, rows = side_of(step), piece(step)
+        return pltpu.make_async_remote_copy(
+            src_ref=part.at[g, side, 1 - core, rows], dst_ref=near.at[g, side, rows],
             send_sem=qn_send.at[g, step], recv_sem=qn_recv.at[g, step], **to_mate)
 
     def near_copy_kv(step):
-        side = side_of(step)
-        return pltpu.make_async_remote_copy(
-            src_ref=part_kv.at[side, 1 - core], dst_ref=near_kv.at[side],
+        side, rows = side_of(step), piece(step)
+        return pltpu.make_async_remote_copy(
+            src_ref=part_kv.at[side, 1 - core, rows], dst_ref=near_kv.at[side, rows],
             send_sem=kn_send.at[step], recv_sem=kn_recv.at[step], **to_mate)
 
     def far_copy(g):
         return pltpu.make_async_remote_copy(
-            src_ref=far_src.at[g], dst_ref=far.at[g], send_sem=far_send.at[g], recv_sem=far_recv.at[g], **to_across)
-
-    def far_copy_kv():
-        return pltpu.make_async_remote_copy(
-            src_ref=far_src_kv, dst_ref=far_kv, send_sem=kf_sems.at[0], recv_sem=kf_sems.at[1], **to_across)
+            src_ref=far_src.at[g], dst_ref=far.at[g], send_sem=far_send.at[g - n_q], recv_sem=far_recv.at[g - n_q],
+            **to_across)
+
+    def far_copy_q(g, step):
+        rows = piece(step)
+        return pltpu.make_async_remote_copy(
+            src_ref=far_src.at[g, rows], dst_ref=far.at[g, rows], send_sem=qf_send.at[g, step],
+            recv_sem=qf_recv.at[g, step], **to_across)
+
+    def far_copy_kv(step):
+        rows = piece(step)
+        return pltpu.make_async_remote_copy(
+            src_ref=far_src_kv.at[rows], dst_ref=far_kv.at[rows], send_sem=kf_send.at[step], recv_sem=kf_recv.at[step],
+            **to_across)
 
     def keep_copy(g):
         return pltpu.make_async_copy(keep.at[g], keep_out.at[g - n_q], out_sem.at[g - n_q, 0])
@@ -162,7 +172,7 @@
         slot = lax.rem(g, NBUF1)
         for k in range(2):
             wait_weights(slot, k)
-            res = jnp.dot(u[...], wbuf[slot, k], preferred_element_type=F32).astype(BF16)
+            res = jnp.dot(u[...].reshape(256, u.shape[-1]), wbuf[slot, k], preferred_element_type=F32).astype(BF16)
             part[g, :, :, :, k * W:(k + 1) * W] = res.reshape(2, 2, 64, W)
         near_copy(g).start()
 
@@ -186,53 +196,52 @@
         keep_copy(g).start()
 
     def multiply_q(step):
-        side = side_of(step)
+        side, rows = side_of(step), piece(step)
+        lhs = u[side, :, rows].reshape(2 * rows.size, u.shape[-1])
         for g in range(n_q):
             if step == 0:
                 wq_copy(g).wait()
             for k in range(2):
-                res = jnp.dot(
-                    u[side_rows(step)], wq_buf[g, :, k * W:(k + 1) * W], preferred_element_type=F32).astype(BF16)
-                part[g, side, :, :, k * W:(k + 1) * W] = res.reshape(2, 64, W)
+                res = jnp.dot(lhs, wq_buf[g, :, k * W:(k + 1) * W], preferred_element_type=F32).astype(BF16)
+                part[g, side, :, rows, k * W:(k + 1) * W] = res.reshape(2, rows.size, W)
             near_copy_q(g, step).start()
             if step == 0 and g >= 2:
                 reduce_q(0, g - 2)
         if step == 0:
             kv_copy.wait()
-        res = jnp.dot(u[side_rows(step)], wkv_buf[...], preferred_element_type=F32).astype(BF16)
-        part_kv[side] = res.reshape(2, 64, res.shape[1])
+        res = jnp.dot(lhs, wkv_buf[...], preferred_element_type=F32).astype(BF16)
+        part_kv[side, :, rows] = res.reshape(2, rows.size, res.shape[1])
         near_copy_kv(step).start()
 
     def reduce_q(step, g):
-        side = side_of(step)
+        side, rows = side_of(step), piece(step)
         near_copy_q(g, step).wait_recv()
-        total_q = add(part[g, side, core], near[g, side])
-        if step == 0:
-            far_src[g] = total_q
-            far_copy(g).start()
+        total_q = add(part[g, side, core, rows], near[g, side, rows])
+        if step < 2:
+            far_src[g, rows] = total_q
+            far_copy_q(g, step).start()
         else:
             keep[g] = total_q
 
     def reduce_kv(step):
-        side = side_of(step)
+        side, rows = side_of(step), piece(step)
         near_copy_kv(step).wait_recv()
-        total_kv = add(part_kv[side, core], near_kv[side])
-        if step == 0:
-            far_src_kv[...] = total_kv
-            far_copy_kv().start()
+        total_kv = add(part_kv[side, core, rows], near_kv[side, rows])
+        if step < 2:
+            far_src_kv[rows] = total_kv
+            far_copy_kv(step).start()
         else:
             keep_kv[...] = total_kv
 
-    normalize(h_own, 0, yj)
-    h_copy(0).wait_recv()
-    normalize(h_other, 0, other_y)
-    multiply_q(0)
-    for g in range(n_q - 2, n_q):
-        reduce_q(0, g)
-    reduce_kv(0)
-    normalize(h_own, 1, yj)
-    h_copy(1).wait_recv()
-    normalize(h_other, 1, other_y)
+    for step in range(3):
+        normalize(h_own, step, yj)
+        h_copy(step).wait_recv()
+        normalize(h_other, step, other_y)
+        if step < 2:
+            multiply_q(step)
+            for g in range(n_q - 2 if step == 0 else 0, n_q):
+                reduce_q(step, g)
+            reduce_kv(step)
 
     @pl.loop(n_q, n_far)
     def _(g):
@@ -243,13 +252,15 @@
             reduce_near(g - 2)
 
     q_cols = n_q * 2 * W
-    multiply_q(1)
+    multiply_q(2)
     for g in range(n_q):
-        reduce_q(1, g)
-        far_copy(g).wait_recv()
+        reduce_q(2, g)
+        for step in range(2):
+            far_copy_q(g, step).wait_recv()
         z_rows[:, :, g * 2 * W:(g + 1) * 2 * W] = add(keep[g], far[g]).reshape(2, 32, 2 * W)
-    reduce_kv(1)
-    far_copy_kv().wait_recv()
+    reduce_kv(2)
+    for step in range(2):
+        far_copy_kv(step).wait_recv()
     z_kv = add(keep_kv[...], far_kv[...])
     z_rows[:, :, q_cols:] = z_kv.reshape(2, 32, z_kv.shape[1])
     y_copy = pltpu.make_async_remote_copy(
@@ -275,12 +286,15 @@
         far_copy(g).wait_recv()
         recv_copy(g).start()
 
-    for step in range(2):
+    for step in range(3):
         h_copy(step).wait_send()
         near_copy_kv(step).wait_send()
         for g in range(n_q):
             near_copy_q(g, step).wait_send()
-    far_copy_kv().wait_send()
+    for step in range(2):
+        far_copy_kv(step).wait_send()
+        for g in range(n_q):
+            far_copy_q(g, step).wait_send()
     for k in range(1, 8):
         sq_copy(lax.rem(me + k, 8), me).wait_send()
     y_copy.wait_send()
@@ -294,7 +308,7 @@
     def _(g):
         send_copy(g).wait()
 
-    @pl.loop(0, n_far)
+    @pl.loop(n_q, n_far)
     def _(g):
         far_copy(g).wait_send()
 
@@ -331,10 +345,10 @@
         in_specs=[any_spec, vmem, any_spec, any_spec, any_spec, any_spec],
         out_specs=(any_spec, any_spec, any_spec, any_spec),
         scratch_shapes=[
-            pltpu.VMEM((rows, half), BF16),
-            pltpu.VMEM((rows, half), BF16),
-            pltpu.VMEM((rows, feats), BF16),
-            pltpu.VMEM((rows, 128), F32),
+            pltpu.VMEM((2, 2, 64, half), BF16),
+            pltpu.VMEM((2, 2, 64, half), BF16),
+            pltpu.VMEM((2, 2, 64, feats), BF16),
+            pltpu.VMEM((2, 2, 64, 128), F32),
             pltpu.VMEM((8, 8, rows), F32),
             pltpu.VMEM((n_q, feats, 2 * W), BF16),
             pltpu.VMEM((NBUF1, 2, feats, W), BF16),
@@ -355,17 +369,20 @@
             dma((NBUF1, 2)),
             dma,
             dma,
-            dma((2, 2)),
+            dma((3, 2)),
             dma((8,)),
             dma((8,)),
             dma((n_all,)),
             dma((n_all,)),
+            dma((n_q, 3)),
+            dma((n_q, 3)),
+            dma((3,)),
+            dma((3,)),
+            dma((EARLY,)),
+            dma((EARLY,)),
             dma((n_q, 2)),
             dma((n_q, 2)),
             dma((2,)),
-            dma((2,)),
-            dma((n_q + EARLY,)),
-            dma((n_q + EARLY,)),
             dma((2,)),
             dma((2,)),
             dma((n_ff, 2)),
@@ -374,7 +391,7 @@
         ],
         compiler_params=pltpu.CompilerParams(collective_id=0, has_side_effects=True, vmem_limit_bytes=VMEM_LIMIT),
         cost_estimate=pl.CostEstimate(flops=flops, bytes_accessed=feats * (flops // (rows * feats)), transcendentals=0),
-    )(hidden, gain, w_q, w_kv, w_gate, w_up)
+    )(hidden.reshape(2, 2, 64, half), gain, w_q, w_kv, w_gate, w_up)
 
 
 def attend_kernel(lens, q_ref, kv_ref, k_ref, v_ref, k_out, v_out, o_ref):

time: 158 us -> 152 us (0.962)
  Pallas kernels: 148 us -> 141 us
    pallas_call x1, Pallas kernels: 67.5 us -> 60.5 us  [project(): pl.pallas_call(functools.partial(project_kernel, n_q, n_ff, d_model), nam...]
  transfers between devices with their start and end apart: 1 -> 1, of which waited for: 1 -> 1; matrix products, arithmetic and copies ran while one was open for 4% -> 4% of each run, Pallas kernels for 17% -> 18%
where the time goes in v6:
time: 152 us; the launch traced here: 151 us
  Pallas kernels  141 us (93%)
  local copies, waits for them, and re-layouts  6.74 us (4%)
  waiting for transfers between devices  1.62 us (1%)
    pallas_call x1, Pallas kernels, project(): pl.pallas_call(functools.partial(project_kernel, n_q, n_ff, d_model), nam...  60.5 us
    pallas_call x1, Pallas kernels, finish(): pl.pallas_call(functools.partial(output_kernel, n_ff, n_o), name='finish'...  53.3 us
    pallas_call x1, Pallas kernels, attend(): pl.pallas_call(attend_kernel, name='attend', out_shape=(jax.ShapeDtypeStr...  27.5 us
  transfers between devices with their start and end apart: 1, of which 1 were waited for; matrix products, arithmetic and copies ran while one was open for 4% of the time, Pallas kernels for 18%

profile of v6, /device:TPU:0, one launch (start us, length us, event | category | flops | bytes accessed | tf_op | source)
XLA Modules:
  0.0 151.1 jit_solution(9713692775364817121)
XLA Ops:
  0.6 60.5 %project.1 = (bf16[2,32,3200]{2,1,0:T(8,128)(2,1)}, bf16[24,64,1024]{2,1,0:T(8,128)(2,1)}, bf16[12,64,1024]{2,1,0:T(8,128)(2,1)}, bf16[12,64,1024]{2,1,0:T(8,128)(2,1)}) custom-call(bf16[2,2,64,768]{3,2,1,0:T(8,128)(2,1)} %bitcast.18, bf16[1,1536]{1,0:T(2,128)(2,1)} %gain.1, bf16[1,1536,3072]{2,1,0:T(8,128)(2,1)} %wq.1, bf16[1,1536,128]{2,1,0:T(8,128)(2,1)} %wkv.1, ...), custom_call_target="tpu_custom_call" | custom-call | flops 21843935232 | bytes 85327872 | tf_op jit(solution)/shard_map/project/pallas_call | solution.py:336
  61.1 0.8 collective-permute-start
  61.9 1.0 slice.6
  62.9 1.3 copy.17
  64.2 0.1 copy.19
  64.3 0.8 copy.16
  65.1 0.6 slice_bitcast_fusion.kv_ref
  65.7 27.5 %attend.1 = (bf16[1,32,2048,128]{3,2,1,0:T(8,128)(2,1)}, bf16[1,32,2048,128]{3,2,1,0:T(8,128)(2,1)}, bf16[32,48,128]{2,1,0:T(8,128)(2,1)}) custom-call(s32[32]{0:T(128)} %lens.1, bf16[32,48,128]{2,1,0:T(8,128)(2,1)} %bitcast.21, bf16[32,2,128]{2,1,0:T(2,128)(2,1)} %slice_bitcast_fusion.kv_ref, bf16[1,32,2048,128]{3,2,1,0:T(8,128)(2,1)} %k_ref.1, ...), custom_call_target="tpu_custom_call" | custom-call | flops 10000000000 | bytes 67108864 | tf_op jit(solution)/shard_map/attend/pallas_call | solution.py:424
  93.2 1.2 reshape.27
  94.5 1.0 copy.21
  95.4 1.6 %collective-permute-done.recv_l = bf16[12,64,1024]{2,1,0:T(8,128)(2,1)} collective-permute-done((bf16[12,64,1024]{2,1,0:T(8,128)(2,1)}, bf16[12,64,1024]{2,1,0:T(8,128)(2,1)}, u32[]{:S(2)}, u32[]{:S(2)}) %collective-permute-start) | collective-permute-done | bytes 1572896 | tf_op jit(solution)/shard_map/ppermute | solution.py:715
  97.1 53.3 %finish.1 = bf16[4,64,768]{2,1,0:T(8,128)(2,1)S(1)} custom-call(bf16[2,6,32,512]{3,2,1,0:T(8,128)(2,1)} %bitcast.20, bf16[24,64,1024]{2,1,0:T(8,128)(2,1)} %get-tuple-element.12.keep, bf16[12,64,1024]{2,1,0:T(8,128)(2,1)} %get-tuple-element.13.recv_e, bf16[12,64,1024]{2,1,0:T(8,128)(2,1)} %collective-permute-done.recv_l, bf16[4,64,768]{2,1,0:T(8,128)(2,1)} %bitcast.19, ...), custom_call_target="tpu_custom_call" | custom-call | flops 12079595520 | bytes 47185920 | tf_op jit(solution)/shard_map/finish/pallas_call | solution.py:665
  150.4 0.7 copy.23
Async XLA Ops:
  61.1 35.9 %collective-permute-start = (bf16[12,64,1024]{2,1,0:T(8,128)(2,1)}, bf16[12,64,1024]{2,1,0:T(8,128)(2,1)}, u32[]{:S(2)}, u32[]{:S(2)}) collective-permute-start(bf16[12,64,1024]{2,1,0:T(8,128)(2,1)} %get-tuple-element.14), channel_id=1, source_target_pairs={{0,2},{1,3},{2,0},{3,1},{4,6},{5,7},{6,4},{7,5}} | collective-permute-start | bytes 4718600 | tf_op jit(solution)/shard_map/ppermute | solution.py:715

commit v7 on v6

--- a/solution.py
+++ b/solution.py
@@ -38,7 +38,7 @@
     h_own, h_other, u, inv_all, sq_all, wq_buf, wbuf, wkv_buf, part, part_kv, near, near_kv, keep, keep_kv, far_src,
     far_src_kv, far, far_kv, z_rows, z_other,
     wq_sem, w_sem, wkv_sem, h_in, h_sems, sq_send, sq_recv, near_send, near_recv, qn_send, qn_recv, kn_send, kn_recv,
-    far_send, far_recv, qf_send, qf_recv, kf_send, kf_recv, y_sems, out_sem, recv_sem, qkv_sem,
+    far_send, far_recv, qf_send, qf_recv, kf_send, kf_recv, y_sems, out_sem, qkv_sem,
 ):
     xi = lax.axis_index("x")
     yj = lax.axis_index("yz")
@@ -78,8 +78,6 @@
         wq_copy(g).start()
     kv_copy = pltpu.make_async_copy(wkv.at[0], wkv_buf, wkv_sem)
     kv_copy.start()
-    for g in range(n_q, n_q + NBUF1):
-        start_weights(jnp.int32(g))
 
     h_f32 = h_own[...].reshape(256, half).astype(F32)
     sq_all[me] = lax.dot_general(
@@ -140,8 +138,8 @@
 
     def far_copy(g):
         return pltpu.make_async_remote_copy(
-            src_ref=far_src.at[g], dst_ref=far.at[g], send_sem=far_send.at[g - n_q], recv_sem=far_recv.at[g - n_q],
-            **to_across)
+            src_ref=far_src.at[g], dst_ref=recv_out.at[g - n_q], send_sem=far_send.at[g - n_q],
+            recv_sem=far_recv.at[g - n_q], **to_across)
 
     def far_copy_q(g, step):
         rows = piece(step)
@@ -161,9 +159,6 @@
     def send_copy(g):
         k = g - n_q
         return pltpu.make_async_copy(far_src.at[g], send_out.at[k - EARLY], out_sem.at[k, 1])
-
-    def recv_copy(g):
-        return pltpu.make_async_copy(far.at[g], recv_out.at[g - n_q], recv_sem.at[g - n_q])
 
     def add(a, b):
         return (a.astype(F32) + b.astype(F32)).astype(BF16)
@@ -242,6 +237,9 @@
             for g in range(n_q - 2 if step == 0 else 0, n_q):
                 reduce_q(step, g)
             reduce_kv(step)
+        if step == 0:
+            for g in range(n_q, n_q + NBUF1):
+                start_weights(jnp.int32(g))
 
     @pl.loop(n_q, n_far)
     def _(g):
@@ -281,11 +279,6 @@
     qkv_other = pltpu.make_async_copy(z_other, qkv_out.at[other_y], qkv_sem.at[1])
     qkv_other.start()
 
-    @pl.loop(n_q, n_far)
-    def _(g):
-        far_copy(g).wait_recv()
-        recv_copy(g).start()
-
     for step in range(3):
         h_copy(step).wait_send()
         near_copy_kv(step).wait_send()
@@ -308,16 +301,13 @@
     def _(g):
         send_copy(g).wait()
 
+    qkv_own.wait()
+    qkv_other.wait()
+
     @pl.loop(n_q, n_far)
     def _(g):
         far_copy(g).wait_send()
-
-    qkv_own.wait()
-    qkv_other.wait()
-
-    @pl.loop(n_q, n_far)
-    def _(g):
-        recv_copy(g).wait()
+        far_copy(g).wait_recv()
 
 
 def project(hidden, gain, w_q, w_kv, w_gate, w_up, d_model):
@@ -361,7 +351,7 @@
             pltpu.VMEM((64, kv), BF16),
             pltpu.VMEM((n_all, 64, 2 * W), BF16),
             pltpu.VMEM((64, kv), BF16),
-            pltpu.VMEM((n_q + EARLY, 64, 2 * W), BF16),
+            pltpu.VMEM((n_q, 64, 2 * W), BF16),
             pltpu.VMEM((64, kv), BF16),
             pltpu.VMEM((2, 32, cols), BF16),
             pltpu.VMEM((32, cols), BF16),
@@ -386,7 +376,6 @@
             dma((2,)),
             dma((2,)),
             dma((n_ff, 2)),
-            dma((EARLY,)),
             dma((2,)),
         ],
         compiler_params=pltpu.CompilerParams(collective_id=0, has_side_effects=True, vmem_limit_bytes=VMEM_LIMIT),
@@ -471,9 +460,8 @@
         src = recv_e.at[pl.ds(GROUP * g, GROUP)] if g < n_early else recv_l.at[pl.ds(GROUP * (g - n_early), GROUP)]
         return pltpu.make_async_copy(src, recv_v.at[pl.ds(GROUP * g, GROUP)], recv_sem.at[g])
 
-    for g in range(n_m):
-        keep_copy(g).start()
-        recv_copy(g).start()
+    keep_copy(0).start()
+    recv_copy(0).start()
 
     def rows_of(p, owner):
         off, size = PARTS[p]
@@ -541,9 +529,12 @@
             for s in range(2):
                 o_copy(s).start()
                 o_own(s).start()
-            for s in range(NBUF3):
-                load_weights(jnp.int32(s))
-            h_load.start()
+            for k in range(1, n_m):
+                keep_copy(k).start()
+                recv_copy(k).start()
+    for s in range(NBUF3):
+        load_weights(jnp.int32(s))
+    h_load.start()
     acc[...] = jnp.zeros_like(acc)
     for s in range(2):
         o_own(s).wait()

time: 152 us -> 151 us (level)
  no operation moved by 1% of the time
where the time goes in v7:
time: 151 us; the launch traced here: 150 us
  Pallas kernels  141 us (93%)
  local copies, waits for them, and re-layouts  6.74 us (4%)
  waiting for transfers between devices  1.73 us (1%)
    pallas_call x1, Pallas kernels, project(): pl.pallas_call(functools.partial(project_kernel, n_q, n_ff, d_model), nam...  59.7 us
    pallas_call x1, Pallas kernels, finish(): pl.pallas_call(functools.partial(output_kernel, n_ff, n_o), name='finish'...  53.3 us
    pallas_call x1, Pallas kernels, attend(): pl.pallas_call(attend_kernel, name='attend', out_shape=(jax.ShapeDtypeStr...  27.5 us
  transfers between devices with their start and end apart: 1, of which 1 were waited for; matrix products, arithmetic and copies ran while one was open for 4% of the time, Pallas kernels for 18%

profile of v7, /device:TPU:0, one launch (start us, length us, event | category | flops | bytes accessed | tf_op | source)
XLA Modules:
  0.0 150.5 jit_solution(10762098229248962801)
XLA Ops:
  0.6 59.7 %project.1 = (bf16[2,32,3200]{2,1,0:T(8,128)(2,1)}, bf16[24,64,1024]{2,1,0:T(8,128)(2,1)}, bf16[12,64,1024]{2,1,0:T(8,128)(2,1)}, bf16[12,64,1024]{2,1,0:T(8,128)(2,1)}) custom-call(bf16[2,2,64,768]{3,2,1,0:T(8,128)(2,1)} %bitcast.18, bf16[1,1536]{1,0:T(2,128)(2,1)} %gain.1, bf16[1,1536,3072]{2,1,0:T(8,128)(2,1)} %wq.1, bf16[1,1536,128]{2,1,0:T(8,128)(2,1)} %wkv.1, ...), custom_call_target="tpu_custom_call" | custom-call | flops 21843935232 | bytes 85327872 | tf_op jit(solution)/shard_map/project/pallas_call | solution.py:326
  60.4 0.8 collective-permute-start
  61.1 1.0 slice.6
  62.1 1.3 copy.17
  63.5 0.1 copy.19
  63.5 0.8 copy.16
  64.3 0.6 slice_bitcast_fusion.kv_ref
  64.9 27.5 %attend.1 = (bf16[1,32,2048,128]{3,2,1,0:T(8,128)(2,1)}, bf16[1,32,2048,128]{3,2,1,0:T(8,128)(2,1)}, bf16[32,48,128]{2,1,0:T(8,128)(2,1)}) custom-call(s32[32]{0:T(128)} %lens.1, bf16[32,48,128]{2,1,0:T(8,128)(2,1)} %bitcast.21, bf16[32,2,128]{2,1,0:T(2,128)(2,1)} %slice_bitcast_fusion.kv_ref, bf16[1,32,2048,128]{3,2,1,0:T(8,128)(2,1)} %k_ref.1, ...), custom_call_target="tpu_custom_call" | custom-call | flops 10000000000 | bytes 67108864 | tf_op jit(solution)/shard_map/attend/pallas_call | solution.py:413
  92.5 1.2 reshape.27
  93.7 1.0 copy.21
  94.7 1.7 %collective-permute-done.recv_l = bf16[12,64,1024]{2,1,0:T(8,128)(2,1)} collective-permute-done((bf16[12,64,1024]{2,1,0:T(8,128)(2,1)}, bf16[12,64,1024]{2,1,0:T(8,128)(2,1)}, u32[]{:S(2)}, u32[]{:S(2)}) %collective-permute-start) | collective-permute-done | bytes 1572896 | tf_op jit(solution)/shard_map/ppermute | solution.py:706
  96.4 53.3 %finish.1 = bf16[4,64,768]{2,1,0:T(8,128)(2,1)S(1)} custom-call(bf16[2,6,32,512]{3,2,1,0:T(8,128)(2,1)} %bitcast.20, bf16[24,64,1024]{2,1,0:T(8,128)(2,1)} %get-tuple-element.12.keep, bf16[12,64,1024]{2,1,0:T(8,128)(2,1)} %get-tuple-element.13.recv_e, bf16[12,64,1024]{2,1,0:T(8,128)(2,1)} %collective-permute-done.recv_l, bf16[4,64,768]{2,1,0:T(8,128)(2,1)} %bitcast.19, ...), custom_call_target="tpu_custom_call" | custom-call | flops 12079595520 | bytes 47185920 | tf_op jit(solution)/shard_map/finish/pallas_call | solution.py:656
  149.8 0.7 copy.23
Async XLA Ops:
  60.4 36.0 %collective-permute-start = (bf16[12,64,1024]{2,1,0:T(8,128)(2,1)}, bf16[12,64,1024]{2,1,0:T(8,128)(2,1)}, u32[]{:S(2)}, u32[]{:S(2)}) collective-permute-start(bf16[12,64,1024]{2,1,0:T(8,128)(2,1)} %get-tuple-element.14), channel_id=1, source_target_pairs={{0,2},{1,3},{2,0},{3,1},{4,6},{5,7},{6,4},{7,5}} | collective-permute-start | bytes 4718600 | tf_op jit(solution)/shard_map/ppermute | solution.py:706

commit v8 on v7

--- a/solution.py
+++ b/solution.py
@@ -13,7 +13,7 @@
 NBUF3 = 6
 GROUP = 3
 PARTS = ((0, 32), (32, 16), (48, 16))
-EARLY = 12
+EARLY = 9
 SEQ_STEP = 2
 VMEM_LIMIT = 64_000_000
 F32 = jnp.float32

time: 151 us -> 155 us (1.026)
  waiting for transfers between devices: 1.73 us -> 9.64 us
  Pallas kernels: 141 us -> 136 us
    ppermute x1, waiting for transfers between devices: 1.73 us -> 9.64 us  [device_step(): lax.ppermute(send, 'x', [(i, (i + x_size // 2) % x_size) for i in range(x...]
    pallas_call x1, Pallas kernels: 59.7 us -> 54.2 us  [project(): pl.pallas_call(functools.partial(project_kernel, n_q, n_ff, d_model), nam...]
where the time goes in v8:
time: 155 us; the launch traced here: 154 us
  Pallas kernels  136 us (88%)
  waiting for transfers between devices  9.64 us (6%)
  local copies, waits for them, and re-layouts  6.73 us (4%)
    pallas_call x1, Pallas kernels, project(): pl.pallas_call(functools.partial(project_kernel, n_q, n_ff, d_model), nam...  54.2 us
    pallas_call x1, Pallas kernels, finish(): pl.pallas_call(functools.partial(output_kernel, n_ff, n_o), name='finish'...  53.9 us
    pallas_call x1, Pallas kernels, attend(): pl.pallas_call(attend_kernel, name='attend', out_shape=(jax.ShapeDtypeStr...  27.5 us
    ppermute x1, waiting for transfers between devices, device_step(): lax.ppermute(send, 'x', [(i, (i + x_size // 2) % x_size) for i in range(x...  9.64 us
  transfers between devices with their start and end apart: 1, of which 1 were waited for; matrix products, arithmetic and copies ran while one was open for 4% of the time, Pallas kernels for 18%

profile of v8, /device:TPU:0, one launch (start us, length us, event | category | flops | bytes accessed | tf_op | source)
XLA Modules:
  0.0 154.0 jit_solution(937027369951102795)
XLA Ops:
  0.6 54.2 %project.1 = (bf16[2,32,3200]{2,1,0:T(8,128)(2,1)}, bf16[24,64,1024]{2,1,0:T(8,128)(2,1)}, bf16[9,64,1024]{2,1,0:T(8,128)(2,1)}, bf16[15,64,1024]{2,1,0:T(8,128)(2,1)}) custom-call(bf16[2,2,64,768]{3,2,1,0:T(8,128)(2,1)} %bitcast.18, bf16[1,1536]{1,0:T(2,128)(2,1)} %gain.1, bf16[1,1536,3072]{2,1,0:T(8,128)(2,1)} %wq.1, bf16[1,1536,128]{2,1,0:T(8,128)(2,1)} %wkv.1, ...), custom_call_target="tpu_custom_call" | custom-call | flops 21843935232 | bytes 85327872 | tf_op jit(solution)/shard_map/project/pallas_call | solution.py:326
  54.8 1.3 collective-permute-start
  56.2 1.0 slice.6
  57.2 1.3 copy.17
  58.5 0.1 copy.19
  58.6 0.8 copy.16
  59.4 0.6 slice_bitcast_fusion.kv_ref
  60.0 27.5 %attend.1 = (bf16[1,32,2048,128]{3,2,1,0:T(8,128)(2,1)}, bf16[1,32,2048,128]{3,2,1,0:T(8,128)(2,1)}, bf16[32,48,128]{2,1,0:T(8,128)(2,1)}) custom-call(s32[32]{0:T(128)} %lens.1, bf16[32,48,128]{2,1,0:T(8,128)(2,1)} %bitcast.21, bf16[32,2,128]{2,1,0:T(2,128)(2,1)} %slice_bitcast_fusion.kv_ref, bf16[1,32,2048,128]{3,2,1,0:T(8,128)(2,1)} %k_ref.1, ...), custom_call_target="tpu_custom_call" | custom-call | flops 10000000000 | bytes 67108864 | tf_op jit(solution)/shard_map/attend/pallas_call | solution.py:413
  87.5 1.2 reshape.27
  88.7 1.0 copy.21
  89.7 9.6 %collective-permute-done.recv_l = bf16[15,64,1024]{2,1,0:T(8,128)(2,1)} collective-permute-done((bf16[15,64,1024]{2,1,0:T(8,128)(2,1)}, bf16[15,64,1024]{2,1,0:T(8,128)(2,1)}, u32[]{:S(2)}, u32[]{:S(2)}) %collective-permute-start) | collective-permute-done | bytes 1966112 | tf_op jit(solution)/shard_map/ppermute | solution.py:706
  99.3 53.9 %finish.1 = bf16[4,64,768]{2,1,0:T(8,128)(2,1)S(1)} custom-call(bf16[2,6,32,512]{3,2,1,0:T(8,128)(2,1)} %bitcast.20, bf16[24,64,1024]{2,1,0:T(8,128)(2,1)} %get-tuple-element.12.keep, bf16[9,64,1024]{2,1,0:T(8,128)(2,1)} %get-tuple-element.13.recv_e, bf16[15,64,1024]{2,1,0:T(8,128)(2,1)} %collective-permute-done.recv_l, bf16[4,64,768]{2,1,0:T(8,128)(2,1)} %bitcast.19, ...), custom_call_target="tpu_custom_call" | custom-call | flops 12079595520 | bytes 47185920 | tf_op jit(solution)/shard_map/finish/pallas_call | solution.py:656
  153.2 0.7 copy.23
Async XLA Ops:
  54.8 44.5 %collective-permute-start = (bf16[15,64,1024]{2,1,0:T(8,128)(2,1)}, bf16[15,64,1024]{2,1,0:T(8,128)(2,1)}, u32[]{:S(2)}, u32[]{:S(2)}) collective-permute-start(bf16[15,64,1024]{2,1,0:T(8,128)(2,1)} %get-tuple-element.14), channel_id=1, source_target_pairs={{0,2},{1,3},{2,0},{3,1},{4,6},{5,7},{6,4},{7,5}} | collective-permute-start | bytes 5898248 | tf_op jit(solution)/shard_map/ppermute | solution.py:706

commit v9 on v7

--- a/solution.py
+++ b/solution.py
@@ -10,8 +10,9 @@
 NORM_EPS = 1e-6
 W = 512
 NBUF1 = 4
-NBUF3 = 6
-GROUP = 3
+FAR = 2
+NBUF3 = 3
+GROUP = 6
 PARTS = ((0, 32), (32, 16), (48, 16))
 EARLY = 12
 SEQ_STEP = 2
@@ -136,10 +137,10 @@
             src_ref=part_kv.at[side, 1 - core, rows], dst_ref=near_kv.at[side, rows],
             send_sem=kn_send.at[step], recv_sem=kn_recv.at[step], **to_mate)
 
-    def far_copy(g):
-        return pltpu.make_async_remote_copy(
-            src_ref=far_src.at[g], dst_ref=recv_out.at[g - n_q], send_sem=far_send.at[g - n_q],
-            recv_sem=far_recv.at[g - n_q], **to_across)
+    def far_copy(k):
+        return pltpu.make_async_remote_copy(
+            src_ref=far_src.at[pl.ds(n_q + FAR * k, FAR)], dst_ref=recv_out.at[pl.ds(FAR * k, FAR)],
+            send_sem=far_send.at[k], recv_sem=far_recv.at[k], **to_across)
 
     def far_copy_q(g, step):
         rows = piece(step)
@@ -179,9 +180,9 @@
         near_copy(g).wait_recv()
         far_src[g] = add(part[g, 1 - chip, core], near[g, 1 - chip])
 
-        @pl.when(g < n_far)
+        @pl.when((g < n_far) & (lax.rem(g - n_q, FAR) == FAR - 1))
         def _():
-            far_copy(g).start()
+            far_copy((g - n_q) // FAR).start()
 
         @pl.when(g >= n_far)
         def _():
@@ -245,9 +246,9 @@
     def _(g):
         multiply(g)
 
-        @pl.when(g >= n_q + 2)
+        @pl.when(g >= n_q + 1)
         def _():
-            reduce_near(g - 2)
+            reduce_near(g - 1)
 
     q_cols = n_q * 2 * W
     multiply_q(2)
@@ -271,9 +272,8 @@
     @pl.loop(n_far, n_all)
     def _(g):
         multiply(g)
-        reduce_near(g - 2)
-
-    reduce_near(jnp.int32(n_all - 2))
+        reduce_near(g - 1)
+
     reduce_near(jnp.int32(n_all - 1))
     y_copy.wait_recv()
     qkv_other = pltpu.make_async_copy(z_other, qkv_out.at[other_y], qkv_sem.at[1])
@@ -304,10 +304,10 @@
     qkv_own.wait()
     qkv_other.wait()
 
-    @pl.loop(n_q, n_far)
-    def _(g):
-        far_copy(g).wait_send()
-        far_copy(g).wait_recv()
+    @pl.loop(0, EARLY // FAR)
+    def _(k):
+        far_copy(k).wait_send()
+        far_copy(k).wait_recv()
 
 
 def project(hidden, gain, w_q, w_kv, w_gate, w_up, d_model):
@@ -368,8 +368,8 @@
             dma((n_q, 3)),
             dma((3,)),
             dma((3,)),
-            dma((EARLY,)),
-            dma((EARLY,)),
+            dma((EARLY // FAR,)),
+            dma((EARLY // FAR,)),
             dma((n_q, 2)),
             dma((n_q, 2)),
             dma((2,)),

time: 151 us -> 152 us (level)
  no operation moved by 1% of the time
where the time goes in v9:
time: 152 us; the launch traced here: 151 us
  Pallas kernels  141 us (93%)
  local copies, waits for them, and re-layouts  6.74 us (4%)
  waiting for transfers between devices  1.92 us (1%)
    pallas_call x1, Pallas kernels, project(): pl.pallas_call(functools.partial(project_kernel, n_q, n_ff, d_model), nam...  59.7 us
    pallas_call x1, Pallas kernels, finish(): pl.pallas_call(functools.partial(output_kernel, n_ff, n_o), name='finish'...  53.9 us
    pallas_call x1, Pallas kernels, attend(): pl.pallas_call(attend_kernel, name='attend', out_shape=(jax.ShapeDtypeStr...  27.5 us
  transfers between devices with their start and end apart: 1, of which 1 were waited for; matrix products, arithmetic and copies ran while one was open for 4% of the time, Pallas kernels for 18%

profile of v9, /device:TPU:0, one launch (start us, length us, event | category | flops | bytes accessed | tf_op | source)
XLA Modules:
  0.0 151.2 jit_solution(6017134057543328349)
XLA Ops:
  0.6 59.7 %project.1 = (bf16[2,32,3200]{2,1,0:T(8,128)(2,1)}, bf16[24,64,1024]{2,1,0:T(8,128)(2,1)}, bf16[12,64,1024]{2,1,0:T(8,128)(2,1)}, bf16[12,64,1024]{2,1,0:T(8,128)(2,1)}) custom-call(bf16[2,2,64,768]{3,2,1,0:T(8,128)(2,1)} %bitcast.18, bf16[1,1536]{1,0:T(2,128)(2,1)} %gain.1, bf16[1,1536,3072]{2,1,0:T(8,128)(2,1)} %wq.1, bf16[1,1536,128]{2,1,0:T(8,128)(2,1)} %wkv.1, ...), custom_call_target="tpu_custom_call" | custom-call | flops 21843935232 | bytes 85327872 | tf_op jit(solution)/shard_map/project/pallas_call | solution.py:326
  60.3 0.8 collective-permute-start
  61.1 1.0 slice.6
  62.1 1.3 copy.17
  63.4 0.1 copy.19
  63.5 0.8 copy.16
  64.3 0.6 slice_bitcast_fusion.kv_ref
  64.9 27.5 %attend.1 = (bf16[1,32,2048,128]{3,2,1,0:T(8,128)(2,1)}, bf16[1,32,2048,128]{3,2,1,0:T(8,128)(2,1)}, bf16[32,48,128]{2,1,0:T(8,128)(2,1)}) custom-call(s32[32]{0:T(128)} %lens.1, bf16[32,48,128]{2,1,0:T(8,128)(2,1)} %bitcast.21, bf16[32,2,128]{2,1,0:T(2,128)(2,1)} %slice_bitcast_fusion.kv_ref, bf16[1,32,2048,128]{3,2,1,0:T(8,128)(2,1)} %k_ref.1, ...), custom_call_target="tpu_custom_call" | custom-call | flops 10000000000 | bytes 67108864 | tf_op jit(solution)/shard_map/attend/pallas_call | solution.py:413
  92.4 1.2 reshape.27
  93.7 1.0 copy.21
  94.6 1.9 %collective-permute-done.recv_l = bf16[12,64,1024]{2,1,0:T(8,128)(2,1)} collective-permute-done((bf16[12,64,1024]{2,1,0:T(8,128)(2,1)}, bf16[12,64,1024]{2,1,0:T(8,128)(2,1)}, u32[]{:S(2)}, u32[]{:S(2)}) %collective-permute-start) | collective-permute-done | bytes 1572896 | tf_op jit(solution)/shard_map/ppermute | solution.py:706
  96.6 53.9 %finish.1 = bf16[4,64,768]{2,1,0:T(8,128)(2,1)S(1)} custom-call(bf16[2,6,32,512]{3,2,1,0:T(8,128)(2,1)} %bitcast.20, bf16[24,64,1024]{2,1,0:T(8,128)(2,1)} %get-tuple-element.12.keep, bf16[12,64,1024]{2,1,0:T(8,128)(2,1)} %get-tuple-element.13.recv_e, bf16[12,64,1024]{2,1,0:T(8,128)(2,1)} %collective-permute-done.recv_l, bf16[4,64,768]{2,1,0:T(8,128)(2,1)} %bitcast.19, ...), custom_call_target="tpu_custom_call" | custom-call | flops 12079595520 | bytes 47185920 | tf_op jit(solution)/shard_map/finish/pallas_call | solution.py:656
  150.4 0.7 copy.23
Async XLA Ops:
  60.3 36.2 %collective-permute-start = (bf16[12,64,1024]{2,1,0:T(8,128)(2,1)}, bf16[12,64,1024]{2,1,0:T(8,128)(2,1)}, u32[]{:S(2)}, u32[]{:S(2)}) collective-permute-start(bf16[12,64,1024]{2,1,0:T(8,128)(2,1)} %get-tuple-element.14), channel_id=1, source_target_pairs={{0,2},{1,3},{2,0},{3,1},{4,6},{5,7},{6,4},{7,5}} | collective-permute-start | bytes 4718600 | tf_op jit(solution)/shard_map/ppermute | solution.py:706

commit v10 on v7

--- a/solution.py
+++ b/solution.py
@@ -19,7 +19,7 @@
 F32 = jnp.float32
 BF16 = jnp.bfloat16
 LOG2E = 1.4426950408889634
-MASKED = -1e30
+MASKED = -1e30 * LOG2E
 
 
 def dev(**axes):
@@ -33,11 +33,11 @@
 
 
 def project_kernel(
-    n_q, n_ff, d_model, hidden, gain, wq, wkv, wg, wu,
+    n_q, n_ff, d_model, hidden, gain_in, wq, wkv, wg, wu,
     qkv_out, keep_out, recv_out, send_out,
-    h_own, h_other, u, inv_all, sq_all, wq_buf, wbuf, wkv_buf, part, part_kv, near, near_kv, keep, keep_kv, far_src,
+    gain, h_own, h_other, u, inv_all, sq_all, wq_buf, wbuf, wkv_buf, part, part_kv, near, near_kv, keep, keep_kv, far_src,
     far_src_kv, far, far_kv, z_rows, z_other,
-    wq_sem, w_sem, wkv_sem, h_in, h_sems, sq_send, sq_recv, near_send, near_recv, qn_send, qn_recv, kn_send, kn_recv,
+    wq_sem, w_sem, wkv_sem, h_in, gain_sem, h_sems, sq_send, sq_recv, near_send, near_recv, qn_send, qn_recv, kn_send, kn_recv,
     far_send, far_recv, qf_send, qf_recv, kf_send, kf_recv, y_sems, out_sem, qkv_sem,
 ):
     xi = lax.axis_index("x")
@@ -60,6 +60,8 @@
         pl.semaphore_signal(barrier, inc=1, **dev(x=peer // 2, yz=lax.rem(peer, 2)))
     h_load = pltpu.make_async_copy(hidden, h_own, h_in)
     h_load.start()
+    gain_load = pltpu.make_async_copy(gain_in, gain, gain_sem)
+    gain_load.start()
 
     def start_weights(g):
         slot = lax.rem(g, NBUF1)
@@ -74,15 +76,17 @@
         return pltpu.make_async_copy(wq.at[0, :, g * 2 * W:(g + 1) * 2 * W], wq_buf.at[g], wq_sem.at[g])
 
     h_load.wait()
+    gain_load.wait()
     for g in range(n_q):
         wq_copy(g).start()
     kv_copy = pltpu.make_async_copy(wkv.at[0], wkv_buf, wkv_sem)
     kv_copy.start()
 
-    h_f32 = h_own[...].reshape(256, half).astype(F32)
-    sq_all[me] = lax.dot_general(
-        jnp.ones((8, half), F32), h_f32 * h_f32, (((1,), (1,)), ((), ())),
-        precision=lax.Precision.HIGHEST, preferred_element_type=F32)
+    folded = jnp.zeros((256, 128), F32)
+    for k in range(half // 128):
+        block = h_own[:, :, :, k * 128:(k + 1) * 128].reshape(256, 128).astype(F32)
+        folded += block * block
+    sq_all[me] = jnp.broadcast_to(jnp.sum(jnp.transpose(folded), axis=0, keepdims=True), (8, 256))
     pl.semaphore_wait(barrier, 7)
 
     def sq_copy(peer, src):
@@ -200,8 +204,8 @@
                 res = jnp.dot(lhs, wq_buf[g, :, k * W:(k + 1) * W], preferred_element_type=F32).astype(BF16)
                 part[g, side, :, rows, k * W:(k + 1) * W] = res.reshape(2, rows.size, W)
             near_copy_q(g, step).start()
-            if step == 0 and g >= 2:
-                reduce_q(0, g - 2)
+            if step == 0 and g >= 1:
+                reduce_q(0, g - 1)
         if step == 0:
             kv_copy.wait()
         res = jnp.dot(lhs, wkv_buf[...], preferred_element_type=F32).astype(BF16)
@@ -234,7 +238,7 @@
         normalize(h_other, step, other_y)
         if step < 2:
             multiply_q(step)
-            for g in range(n_q - 2 if step == 0 else 0, n_q):
+            for g in range(n_q - 1 if step == 0 else 0, n_q):
                 reduce_q(step, g)
             reduce_kv(step)
         if step == 0:
@@ -320,7 +324,6 @@
     late = n_ff - EARLY
     dma = pltpu.SemaphoreType.DMA
     any_spec = pl.BlockSpec(memory_space=pl.ANY)
-    vmem = pl.BlockSpec(memory_space=pltpu.VMEM)
     cols = w_q.shape[2] + kv
     flops = 2 * rows * feats * (w_q.shape[2] + kv + 2 * w_gate.shape[2])
     return pl.pallas_call(
@@ -332,9 +335,10 @@
             jax.ShapeDtypeStruct((EARLY, 64, 2 * W), BF16),
             jax.ShapeDtypeStruct((late, 64, 2 * W), BF16),
         ),
-        in_specs=[any_spec, vmem, any_spec, any_spec, any_spec, any_spec],
+        in_specs=[any_spec] * 6,
         out_specs=(any_spec, any_spec, any_spec, any_spec),
         scratch_shapes=[
+            pltpu.VMEM((1, feats), BF16),
             pltpu.VMEM((2, 2, 64, half), BF16),
             pltpu.VMEM((2, 2, 64, half), BF16),
             pltpu.VMEM((2, 2, 64, feats), BF16),
@@ -359,6 +363,7 @@
             dma((NBUF1, 2)),
             dma,
             dma,
+            dma,
             dma((3, 2)),
             dma((8,)),
             dma((8,)),
@@ -625,8 +630,22 @@
             finalize(p - 1)
 
     last = len(PARTS) - 1
-    multiply(last, jnp.int32(n_g - 1))
-    exchange(last)
+    g = chunk(last, n_g - 1)
+    if n_g > NBUF3:
+        pltpu.make_async_copy(w_down.at[0, pl.ds(0, depth)], wbuf.at[g % NBUF3], w_sem.at[g % NBUF3]).wait()
+    near_copy(last, g, 0).wait_recv()
+    near_copy(last, g, 1).wait_recv()
+    rows = slice(4 * PARTS[last][0], 4 * sum(PARTS[last]))
+    for j in (other_y, yj):
+        for n in range(half // 256):
+            cols = pl.ds(pl.multiple_of(j * half + n * 256, 256), 256)
+            total = acc[rows, cols]
+            for k in range(GROUP):
+                total += jnp.dot(
+                    acts[GROUP * g + k, rows], wbuf[g % NBUF3, k * W:(k + 1) * W, cols], preferred_element_type=F32)
+            acc[rows, cols] = total
+        if j is other_y:
+            exchange(last)
     for s in range(2):
         o_copy(s).wait_send()
     for p in range(len(PARTS)):

time: 151 us -> 150 us (level)
  Pallas kernels: 141 us -> 139 us
    pallas_call x1, Pallas kernels: 59.7 us -> 57.7 us  [project(): pl.pallas_call(functools.partial(project_kernel, n_q, n_ff, d_model), nam...]
where the time goes in v10:
time: 150 us; the launch traced here: 149 us
  Pallas kernels  139 us (93%)
  local copies, waits for them, and re-layouts  6.74 us (4%)
  waiting for transfers between devices  2 us (1%)
    pallas_call x1, Pallas kernels, project(): pl.pallas_call(functools.partial(project_kernel, n_q, n_ff, d_model), nam...  57.7 us
    pallas_call x1, Pallas kernels, finish(): pl.pallas_call(functools.partial(output_kernel, n_ff, n_o), name='finish'...  53.6 us
    pallas_call x1, Pallas kernels, attend(): pl.pallas_call(attend_kernel, name='attend', out_shape=(jax.ShapeDtypeStr...  27.5 us
  transfers between devices with their start and end apart: 1, of which 1 were waited for; matrix products, arithmetic and copies ran while one was open for 4% of the time, Pallas kernels for 18%

profile of v10, /device:TPU:0, one launch (start us, length us, event | category | flops | bytes accessed | tf_op | source)
XLA Modules:
  0.0 149.1 jit_solution(6107686943485186128)
XLA Ops:
  0.6 57.7 %project.1 = (bf16[2,32,3200]{2,1,0:T(8,128)(2,1)}, bf16[24,64,1024]{2,1,0:T(8,128)(2,1)}, bf16[12,64,1024]{2,1,0:T(8,128)(2,1)}, bf16[12,64,1024]{2,1,0:T(8,128)(2,1)}) custom-call(bf16[2,2,64,768]{3,2,1,0:T(8,128)(2,1)} %bitcast.18, bf16[1,1536]{1,0:T(2,128)(2,1)} %gain_in.1, bf16[1,1536,3072]{2,1,0:T(8,128)(2,1)} %wq.1, bf16[1,1536,128]{2,1,0:T(8,128)(2,1)} %wkv.1, ...), custom_call_target="tpu_custom_call" | custom-call | flops 21843935232 | bytes 85327872 | tf_op jit(solution)/shard_map/project/pallas_call | solution.py:329
  58.4 0.9 collective-permute-start
  59.2 1.0 slice.6
  60.3 1.3 copy.17
  61.6 0.1 copy.19
  61.7 0.8 copy.16
  62.4 0.6 slice_bitcast_fusion.kv_ref
  63.1 27.5 %attend.1 = (bf16[1,32,2048,128]{3,2,1,0:T(8,128)(2,1)}, bf16[1,32,2048,128]{3,2,1,0:T(8,128)(2,1)}, bf16[32,48,128]{2,1,0:T(8,128)(2,1)}) custom-call(s32[32]{0:T(128)} %lens.1, bf16[32,48,128]{2,1,0:T(8,128)(2,1)} %bitcast.21, bf16[32,2,128]{2,1,0:T(2,128)(2,1)} %slice_bitcast_fusion.kv_ref, bf16[1,32,2048,128]{3,2,1,0:T(8,128)(2,1)} %k_ref.1, ...), custom_call_target="tpu_custom_call" | custom-call | flops 10000000000 | bytes 67108864 | tf_op jit(solution)/shard_map/attend/pallas_call | solution.py:418
  90.6 1.2 reshape.27
  91.8 1.0 copy.21
  92.8 2.0 %collective-permute-done.recv_l = bf16[12,64,1024]{2,1,0:T(8,128)(2,1)} collective-permute-done((bf16[12,64,1024]{2,1,0:T(8,128)(2,1)}, bf16[12,64,1024]{2,1,0:T(8,128)(2,1)}, u32[]{:S(2)}, u32[]{:S(2)}) %collective-permute-start) | collective-permute-done | bytes 1572896 | tf_op jit(solution)/shard_map/ppermute | solution.py:725
  94.8 53.6 %finish.1 = bf16[4,64,768]{2,1,0:T(8,128)(2,1)S(1)} custom-call(bf16[2,6,32,512]{3,2,1,0:T(8,128)(2,1)} %bitcast.20, bf16[24,64,1024]{2,1,0:T(8,128)(2,1)} %get-tuple-element.12.keep, bf16[12,64,1024]{2,1,0:T(8,128)(2,1)} %get-tuple-element.13.recv_e, bf16[12,64,1024]{2,1,0:T(8,128)(2,1)} %collective-permute-done.recv_l, bf16[4,64,768]{2,1,0:T(8,128)(2,1)} %bitcast.19, ...), custom_call_target="tpu_custom_call" | custom-call | flops 12079595520 | bytes 47185920 | tf_op jit(solution)/shard_map/finish/pallas_call | solution.py:675
  148.3 0.7 copy.23
Async XLA Ops:
  58.4 36.4 %collective-permute-start = (bf16[12,64,1024]{2,1,0:T(8,128)(2,1)}, bf16[12,64,1024]{2,1,0:T(8,128)(2,1)}, u32[]{:S(2)}, u32[]{:S(2)}) collective-permute-start(bf16[12,64,1024]{2,1,0:T(8,128)(2,1)} %get-tuple-element.14), channel_id=1, source_target_pairs={{0,2},{1,3},{2,0},{3,1},{4,6},{5,7},{6,4},{7,5}} | collective-permute-start | bytes 4718600 | tf_op jit(solution)/shard_map/ppermute | solution.py:725

commit v11 on v10

--- a/solution.py
+++ b/solution.py
@@ -14,7 +14,9 @@
 GROUP = 3
 PARTS = ((0, 32), (32, 16), (48, 16))
 EARLY = 12
-SEQ_STEP = 2
+SEQ_STEP = 4
+HELD = 6
+RELEASE = 3
 VMEM_LIMIT = 64_000_000
 F32 = jnp.float32
 BF16 = jnp.bfloat16
@@ -183,7 +185,7 @@
         near_copy(g).wait_recv()
         far_src[g] = add(part[g, 1 - chip, core], near[g, 1 - chip])
 
-        @pl.when(g < n_far)
+        @pl.when((g < n_far) & ((core == 1) | (g < n_far - HELD)))
         def _():
             far_copy(g).start()
 
@@ -249,9 +251,9 @@
     def _(g):
         multiply(g)
 
-        @pl.when(g >= n_q + 2)
-        def _():
-            reduce_near(g - 2)
+        @pl.when(g >= n_q + 1)
+        def _():
+            reduce_near(g - 1)
 
     q_cols = n_q * 2 * W
     multiply_q(2)
@@ -275,9 +277,14 @@
     @pl.loop(n_far, n_all)
     def _(g):
         multiply(g)
-        reduce_near(g - 2)
-
-    reduce_near(jnp.int32(n_all - 2))
+        reduce_near(g - 1)
+
+        @pl.when((g == n_far + RELEASE) & (core == 0))
+        def _():
+            @pl.loop(n_far - HELD, n_far)
+            def _(k):
+                far_copy(k).start()
+
     reduce_near(jnp.int32(n_all - 1))
     y_copy.wait_recv()
     qkv_other = pltpu.make_async_copy(z_other, qkv_out.at[other_y], qkv_sem.at[1])

time: 150 us -> 148 us (0.987)
  waiting for transfers between devices: 2 us -> 0.01 us
    ppermute x1, waiting for transfers between devices: 2 us -> 0.01 us  [device_step(): lax.ppermute(send, 'x', [(i, (i + x_size // 2) % x_size) for i in range(x...]
  transfers between devices with their start and end apart: 1 -> 1, of which waited for: 1 -> 0; matrix products, arithmetic and copies ran while one was open for 4% -> 4% of each run, Pallas kernels for 18% -> 19%
where the time goes in v11:
time: 148 us
  Pallas kernels  140 us (95%)
  local copies, waits for them, and re-layouts  6.74 us (5%)
    pallas_call x1, Pallas kernels, project(): pl.pallas_call(functools.partial(project_kernel, n_q, n_ff, d_model), nam...  57.5 us
    pallas_call x1, Pallas kernels, finish(): pl.pallas_call(functools.partial(output_kernel, n_ff, n_o), name='finish'...  53.8 us
    pallas_call x1, Pallas kernels, attend(): pl.pallas_call(attend_kernel, name='attend', out_shape=(jax.ShapeDtypeStr...  28.4 us
  transfers between devices with their start and end apart: 1, of which 0 were waited for; matrix products, arithmetic and copies ran while one was open for 4% of the time, Pallas kernels for 19%

profile of v11, /device:TPU:0, one launch (start us, length us, event | category | flops | bytes accessed | tf_op | source)
XLA Modules:
  0.0 147.9 jit_solution(1077383102323004179)
XLA Ops:
  0.6 57.5 %project.1 = (bf16[2,32,3200]{2,1,0:T(8,128)(2,1)}, bf16[24,64,1024]{2,1,0:T(8,128)(2,1)}, bf16[12,64,1024]{2,1,0:T(8,128)(2,1)}, bf16[12,64,1024]{2,1,0:T(8,128)(2,1)}) custom-call(bf16[2,2,64,768]{3,2,1,0:T(8,128)(2,1)} %bitcast.18, bf16[1,1536]{1,0:T(2,128)(2,1)} %gain_in.1, bf16[1,1536,3072]{2,1,0:T(8,128)(2,1)} %wq.1, bf16[1,1536,128]{2,1,0:T(8,128)(2,1)} %wkv.1, ...), custom_call_target="tpu_custom_call" | custom-call | flops 21843935232 | bytes 85327872 | tf_op jit(solution)/shard_map/project/pallas_call | solution.py:336
  58.1 0.9 collective-permute-start
  59.0 1.0 slice.6
  60.1 1.3 copy.17
  61.4 0.1 copy.19
  61.4 0.8 copy.16
  62.2 0.6 slice_bitcast_fusion.kv_ref
  62.8 28.4 %attend.1 = (bf16[1,32,2048,128]{3,2,1,0:T(8,128)(2,1)}, bf16[1,32,2048,128]{3,2,1,0:T(8,128)(2,1)}, bf16[32,48,128]{2,1,0:T(8,128)(2,1)}) custom-call(s32[32]{0:T(128)} %lens.1, bf16[32,48,128]{2,1,0:T(8,128)(2,1)} %bitcast.21, bf16[32,2,128]{2,1,0:T(2,128)(2,1)} %slice_bitcast_fusion.kv_ref, bf16[1,32,2048,128]{3,2,1,0:T(8,128)(2,1)} %k_ref.1, ...), custom_call_target="tpu_custom_call" | custom-call | flops 10000000000 | bytes 67108864 | tf_op jit(solution)/shard_map/attend/pallas_call | solution.py:425
  91.2 1.2 reshape.27
  92.4 1.0 copy.21
  93.4 0.0 collective-permute-done.recv_l
  93.4 53.8 %finish.1 = bf16[4,64,768]{2,1,0:T(8,128)(2,1)S(1)} custom-call(bf16[2,6,32,512]{3,2,1,0:T(8,128)(2,1)} %bitcast.20, bf16[24,64,1024]{2,1,0:T(8,128)(2,1)} %get-tuple-element.12.keep, bf16[12,64,1024]{2,1,0:T(8,128)(2,1)} %get-tuple-element.13.recv_e, bf16[12,64,1024]{2,1,0:T(8,128)(2,1)} %collective-permute-done.recv_l, bf16[4,64,768]{2,1,0:T(8,128)(2,1)} %bitcast.19, ...), custom_call_target="tpu_custom_call" | custom-call | flops 12079595520 | bytes 47185920 | tf_op jit(solution)/shard_map/finish/pallas_call | solution.py:682
  147.2 0.7 copy.23
Async XLA Ops:
  58.1 35.3 %collective-permute-start = (bf16[12,64,1024]{2,1,0:T(8,128)(2,1)}, bf16[12,64,1024]{2,1,0:T(8,128)(2,1)}, u32[]{:S(2)}, u32[]{:S(2)}) collective-permute-start(bf16[12,64,1024]{2,1,0:T(8,128)(2,1)} %get-tuple-element.14), channel_id=1, source_target_pairs={{0,2},{1,3},{2,0},{3,1},{4,6},{5,7},{6,4},{7,5}} | collective-permute-start | bytes 4718600 | tf_op jit(solution)/shard_map/ppermute | solution.py:732

commit v12 on v11

--- a/solution.py
+++ b/solution.py
@@ -14,7 +14,7 @@
 GROUP = 3
 PARTS = ((0, 32), (32, 16), (48, 16))
 EARLY = 12
-SEQ_STEP = 4
+SEQ_STEP = 2
 HELD = 6
 RELEASE = 3
 VMEM_LIMIT = 64_000_000
@@ -36,7 +36,7 @@
 
 def project_kernel(
     n_q, n_ff, d_model, hidden, gain_in, wq, wkv, wg, wu,
-    qkv_out, keep_out, recv_out, send_out,
+    q_out, kv_out, keep_out, recv_out, send_out,
     gain, h_own, h_other, u, inv_all, sq_all, wq_buf, wbuf, wkv_buf, part, part_kv, near, near_kv, keep, keep_kv, far_src,
     far_src_kv, far, far_kv, z_rows, z_other,
     wq_sem, w_sem, wkv_sem, h_in, gain_sem, h_sems, sq_send, sq_recv, near_send, near_recv, qn_send, qn_recv, kn_send, kn_recv,
@@ -271,8 +271,15 @@
         src_ref=z_rows.at[other_y], dst_ref=z_other, send_sem=y_sems.at[0], recv_sem=y_sems.at[1],
         **dev(x=xi, yz=other_y))
     y_copy.start()
-    qkv_own = pltpu.make_async_copy(z_rows.at[yj], qkv_out.at[yj], qkv_sem.at[0])
-    qkv_own.start()
+    def qkv_copies(src, which):
+        return (
+            pltpu.make_async_copy(src.at[:, :q_cols], q_out.at[which], qkv_sem.at[0, 0 if src is z_other else 1]),
+            pltpu.make_async_copy(src.at[:, q_cols:], kv_out.at[which], qkv_sem.at[1, 0 if src is z_other else 1]),
+        )
+
+    qkv_own = qkv_copies(z_rows.at[yj], yj)
+    for copy in qkv_own:
+        copy.start()
 
     @pl.loop(n_far, n_all)
     def _(g):
@@ -287,8 +294,9 @@
 
     reduce_near(jnp.int32(n_all - 1))
     y_copy.wait_recv()
-    qkv_other = pltpu.make_async_copy(z_other, qkv_out.at[other_y], qkv_sem.at[1])
-    qkv_other.start()
+    qkv_other = qkv_copies(z_other, other_y)
+    for copy in qkv_other:
+        copy.start()
 
     for step in range(3):
         h_copy(step).wait_send()
@@ -312,8 +320,8 @@
     def _(g):
         send_copy(g).wait()
 
-    qkv_own.wait()
-    qkv_other.wait()
+    for copy in qkv_own + qkv_other:
+        copy.wait()
 
     @pl.loop(n_q, n_far)
     def _(g):
@@ -337,13 +345,14 @@
         functools.partial(project_kernel, n_q, n_ff, d_model),
         name="project",
         out_shape=(
-            jax.ShapeDtypeStruct((2, 32, cols), BF16),
+            jax.ShapeDtypeStruct((2, 32, cols - kv), BF16),
+            jax.ShapeDtypeStruct((2, 32, kv), BF16),
             jax.ShapeDtypeStruct((n_ff, 64, 2 * W), BF16),
             jax.ShapeDtypeStruct((EARLY, 64, 2 * W), BF16),
             jax.ShapeDtypeStruct((late, 64, 2 * W), BF16),
         ),
         in_specs=[any_spec] * 6,
-        out_specs=(any_spec, any_spec, any_spec, any_spec),
+        out_specs=(any_spec,) * 5,
         scratch_shapes=[
             pltpu.VMEM((1, feats), BF16),
             pltpu.VMEM((2, 2, 64, half), BF16),
@@ -388,7 +397,7 @@
             dma((2,)),
             dma((2,)),
             dma((n_ff, 2)),
-            dma((2,)),
+            dma((2, 2)),
         ],
         compiler_params=pltpu.CompilerParams(collective_id=0, has_side_effects=True, vmem_limit_bytes=VMEM_LIMIT),
         cost_estimate=pl.CostEstimate(flops=flops, bytes_accessed=feats * (flops // (rows * feats)), transcendentals=0),
@@ -407,7 +416,9 @@
         hit = lax.broadcasted_iota(jnp.int32, (16, k_ref.shape[3]), 0) == length - base
         for src, dst, which in ((k_ref, k_out, 0), (v_ref, v_out, 1)):
             old = src[0, s, pl.ds(base, 16), :].astype(F32)
-            new = kv_ref[s, which:which + 1, :].astype(F32)
+            fresh = kv_ref[which].astype(F32)
+            mine = lax.broadcasted_iota(jnp.int32, fresh.shape, 0) == step * SEQ_STEP + s
+            new = jnp.sum(jnp.where(mine, fresh, 0.0), axis=0, keepdims=True)
             dst[0, s, pl.ds(base, 16), :] = jnp.where(hit, new, old).astype(BF16)
         scores = lax.dot_general(q_ref[s], k_out[0, s], (((1,), (1,)), ((), ())), preferred_element_type=F32) * scale
         visible = lax.broadcasted_iota(jnp.int32, scores.shape, 1) <= length
@@ -433,7 +444,7 @@
         grid_spec=pltpu.PrefetchScalarGridSpec(
             num_scalar_prefetch=1,
             grid=(seqs // SEQ_STEP,),
-            in_specs=[q_spec, pl.BlockSpec((SEQ_STEP, 2, dim), lambda b, lens: (b, 0, 0)), cache_spec, cache_spec],
+            in_specs=[q_spec, pl.BlockSpec((2, seqs, dim), lambda b, lens: (0, 0, 0)), cache_spec, cache_spec],
             out_specs=(cache_spec, cache_spec, q_spec),
         ),
         compiler_params=pltpu.CompilerParams(dimension_semantics=("arbitrary",), vmem_limit_bytes=66_000_000),
@@ -728,10 +739,9 @@
         dim = k_cache.shape[3]
         q_cols = w_q.shape[2]
         heads = q_cols // dim
-        qkv, keep, recv_e, send = project(hidden, norm_gain, w_q, w_kv, w_gate, w_up, d_model)
+        q, kv, keep, recv_e, send = project(hidden, norm_gain, w_q, w_kv, w_gate, w_up, d_model)
         recv_l = lax.ppermute(send, "x", [(i, (i + x_size // 2) % x_size) for i in range(x_size)])
-        q = qkv[:, :, :q_cols].reshape(y_size, seqs, heads, dim).transpose(1, 0, 2, 3).reshape(seqs, y_size * heads, dim)
-        kv = qkv[:, :, q_cols:].transpose(1, 0, 2)
+        q = q.reshape(y_size, seqs, heads, dim).transpose(1, 0, 2, 3).reshape(seqs, y_size * heads, dim)
         k_new, v_new, o = attend(seq_len, q, kv, k_cache, v_cache)
         o = o.reshape(seqs, y_size, q_cols // W, W).transpose(1, 2, 0, 3)
         hidden_out = finish(o, keep, recv_e, recv_l, hidden, w_o, w_down)

time: 148 us -> 148 us (level)
  local copies, waits for them, and re-layouts: 6.74 us -> 4.79 us
    pallas_call x1, Pallas kernels: 28.4 us -> 30.1 us  [attend(): pl.pallas_call(attend_kernel, name='attend', out_shape=(jax.ShapeDtypeStr...]
  transfers between devices with their start and end apart: 1 -> 1, of which waited for: 0 -> 0; matrix products, arithmetic and copies ran while one was open for 4% -> 3% of each run, Pallas kernels for 19% -> 20%
where the time goes in v12:
time: 148 us
  Pallas kernels  141 us (95%)
  local copies, waits for them, and re-layouts  4.79 us (3%)
    pallas_call x1, Pallas kernels, project(): pl.pallas_call(functools.partial(project_kernel, n_q, n_ff, d_model), nam...  57.5 us
    pallas_call x1, Pallas kernels, finish(): pl.pallas_call(functools.partial(output_kernel, n_ff, n_o), name='finish'...  53.7 us
    pallas_call x1, Pallas kernels, attend(): pl.pallas_call(attend_kernel, name='attend', out_shape=(jax.ShapeDtypeStr...  30.1 us
  transfers between devices with their start and end apart: 1, of which 0 were waited for; matrix products, arithmetic and copies ran while one was open for 3% of the time, Pallas kernels for 20%

profile of v12, /device:TPU:0, one launch (start us, length us, event | category | flops | bytes accessed | tf_op | source)
XLA Modules:
  0.0 147.7 jit_solution(9313451685870107346)
XLA Ops:
  0.6 57.5 %project.1 = (bf16[2,32,3072]{2,1,0:T(8,128)(2,1)}, bf16[2,32,128]{2,1,0:T(8,128)(2,1)}, bf16[24,64,1024]{2,1,0:T(8,128)(2,1)}, bf16[12,64,1024]{2,1,0:T(8,128)(2,1)}, bf16[12,64,1024]{2,1,0:T(8,128)(2,1)}) custom-call(bf16[2,2,64,768]{3,2,1,0:T(8,128)(2,1)} %bitcast.15, bf16[1,1536]{1,0:T(2,128)(2,1)} %gain_in.1, bf16[1,1536,3072]{2,1,0:T(8,128)(2,1)} %wq.1, ...), custom_call_target="tpu_custom_call" | custom-call | flops 21843935232 | bytes 85327872 | tf_op jit(solution)/shard_map/project/pallas_call | solution.py:344
  58.2 0.9 collective-permute-start
  59.0 1.1 copy.17
  60.1 0.8 copy.15
  60.9 30.1 %attend.1 = (bf16[1,32,2048,128]{3,2,1,0:T(8,128)(2,1)}, bf16[1,32,2048,128]{3,2,1,0:T(8,128)(2,1)}, bf16[32,48,128]{2,1,0:T(8,128)(2,1)}) custom-call(s32[32]{0:T(128)} %lens.1, bf16[32,48,128]{2,1,0:T(8,128)(2,1)} %bitcast.19, bf16[2,32,128]{2,1,0:T(8,128)(2,1)} %get-tuple-element.12.kv_ref, bf16[1,32,2048,128]{3,2,1,0:T(8,128)(2,1)} %k_ref.1, ...), custom_call_target="tpu_custom_call" | custom-call | flops 10000000000 | bytes 67108864 | tf_op jit(solution)/shard_map/attend/pallas_call | solution.py:436
  91.0 1.2 reshape.27
  92.2 1.0 copy.19
  93.2 0.0 collective-permute-done.recv_l
  93.2 53.7 %finish.1 = bf16[4,64,768]{2,1,0:T(8,128)(2,1)S(1)} custom-call(bf16[2,6,32,512]{3,2,1,0:T(8,128)(2,1)} %bitcast.17, bf16[24,64,1024]{2,1,0:T(8,128)(2,1)} %get-tuple-element.14.keep, bf16[12,64,1024]{2,1,0:T(8,128)(2,1)} %get-tuple-element.15.recv_e, bf16[12,64,1024]{2,1,0:T(8,128)(2,1)} %collective-permute-done.recv_l, bf16[4,64,768]{2,1,0:T(8,128)(2,1)} %bitcast.16, ...), custom_call_target="tpu_custom_call" | custom-call | flops 12079595520 | bytes 47185920 | tf_op jit(solution)/shard_map/finish/pallas_call | solution.py:693
  146.9 0.7 copy.21
Async XLA Ops:
  58.2 35.0 %collective-permute-start = (bf16[12,64,1024]{2,1,0:T(8,128)(2,1)}, bf16[12,64,1024]{2,1,0:T(8,128)(2,1)}, u32[]{:S(2)}, u32[]{:S(2)}) collective-permute-start(bf16[12,64,1024]{2,1,0:T(8,128)(2,1)} %get-tuple-element.16), channel_id=1, source_target_pairs={{0,2},{1,3},{2,0},{3,1},{4,6},{5,7},{6,4},{7,5}} | collective-permute-start | bytes 4718600 | tf_op jit(solution)/shard_map/ppermute | solution.py:743

commit v13 on v12

--- a/solution.py
+++ b/solution.py
@@ -404,8 +404,13 @@
     )(hidden.reshape(2, 2, 64, half), gain, w_q, w_kv, w_gate, w_up)
 
 
-def attend_kernel(lens, q_ref, kv_ref, k_ref, v_ref, k_out, v_out, o_ref):
+def attend_kernel(lens, q_ref, kv_ref, k_ref, v_ref, k_out, v_out, o_ref, fresh):
     step = pl.program_id(0)
+
+    @pl.when(step == 0)
+    def _():
+        fresh[...] = kv_ref[...].astype(F32)
+
     n_pos = k_ref.shape[2]
     scale = q_ref.shape[2] ** -0.5 * LOG2E
     for s in range(SEQ_STEP):
@@ -416,9 +421,7 @@
         hit = lax.broadcasted_iota(jnp.int32, (16, k_ref.shape[3]), 0) == length - base
         for src, dst, which in ((k_ref, k_out, 0), (v_ref, v_out, 1)):
             old = src[0, s, pl.ds(base, 16), :].astype(F32)
-            fresh = kv_ref[which].astype(F32)
-            mine = lax.broadcasted_iota(jnp.int32, fresh.shape, 0) == step * SEQ_STEP + s
-            new = jnp.sum(jnp.where(mine, fresh, 0.0), axis=0, keepdims=True)
+            new = fresh[which, pl.ds(step * SEQ_STEP + s, 1), :]
             dst[0, s, pl.ds(base, 16), :] = jnp.where(hit, new, old).astype(BF16)
         scores = lax.dot_general(q_ref[s], k_out[0, s], (((1,), (1,)), ((), ())), preferred_element_type=F32) * scale
         visible = lax.broadcasted_iota(jnp.int32, scores.shape, 1) <= length
@@ -446,6 +449,7 @@
             grid=(seqs // SEQ_STEP,),
             in_specs=[q_spec, pl.BlockSpec((2, seqs, dim), lambda b, lens: (0, 0, 0)), cache_spec, cache_spec],
             out_specs=(cache_spec, cache_spec, q_spec),
+            scratch_shapes=[pltpu.VMEM((2, seqs, dim), F32)],
         ),
         compiler_params=pltpu.CompilerParams(dimension_semantics=("arbitrary",), vmem_limit_bytes=66_000_000),
         cost_estimate=pl.CostEstimate(

time: 148 us -> 146 us (0.986)
  Pallas kernels: 141 us -> 139 us
    pallas_call x1, Pallas kernels: 30.1 us -> 28.2 us  [attend(): pl.pallas_call(attend_kernel, name='attend', out_shape=(jax.ShapeDtypeStr...]
  transfers between devices with their start and end apart: 1 -> 1, of which waited for: 0 -> 1; matrix products, arithmetic and copies ran while one was open for 3% -> 3% of each run, Pallas kernels for 20% -> 19%
where the time goes in v13:
time: 146 us
  Pallas kernels  139 us (95%)
  local copies, waits for them, and re-layouts  4.79 us (3%)
    pallas_call x1, Pallas kernels, project(): pl.pallas_call(functools.partial(project_kernel, n_q, n_ff, d_model), nam...  57.5 us
    pallas_call x1, Pallas kernels, finish(): pl.pallas_call(functools.partial(output_kernel, n_ff, n_o), name='finish'...  53.6 us
    pallas_call x1, Pallas kernels, attend(): pl.pallas_call(attend_kernel, name='attend', out_shape=(jax.ShapeDtypeStr...  28.2 us
  transfers between devices with their start and end apart: 1, of which 1 were waited for; matrix products, arithmetic and copies ran while one was open for 3% of the time, Pallas kernels for 19%

profile of v13, /device:TPU:0, one launch (start us, length us, event | category | flops | bytes accessed | tf_op | source)
XLA Modules:
  0.0 145.7 jit_solution(4750033806545591753)
XLA Ops:
  0.6 57.5 %project.1 = (bf16[2,32,3072]{2,1,0:T(8,128)(2,1)}, bf16[2,32,128]{2,1,0:T(8,128)(2,1)}, bf16[24,64,1024]{2,1,0:T(8,128)(2,1)}, bf16[12,64,1024]{2,1,0:T(8,128)(2,1)}, bf16[12,64,1024]{2,1,0:T(8,128)(2,1)}) custom-call(bf16[2,2,64,768]{3,2,1,0:T(8,128)(2,1)} %bitcast.15, bf16[1,1536]{1,0:T(2,128)(2,1)} %gain_in.1, bf16[1,1536,3072]{2,1,0:T(8,128)(2,1)} %wq.1, ...), custom_call_target="tpu_custom_call" | custom-call | flops 21843935232 | bytes 85327872 | tf_op jit(solution)/shard_map/project/pallas_call | solution.py:344
  58.2 0.9 collective-permute-start
  59.0 1.1 copy.17
  60.1 0.8 copy.15
  60.9 28.2 %attend.1 = (bf16[1,32,2048,128]{3,2,1,0:T(8,128)(2,1)}, bf16[1,32,2048,128]{3,2,1,0:T(8,128)(2,1)}, bf16[32,48,128]{2,1,0:T(8,128)(2,1)}) custom-call(s32[32]{0:T(128)} %lens.1, bf16[32,48,128]{2,1,0:T(8,128)(2,1)} %bitcast.19, bf16[2,32,128]{2,1,0:T(8,128)(2,1)} %get-tuple-element.12.kv_ref, bf16[1,32,2048,128]{3,2,1,0:T(8,128)(2,1)} %k_ref.1, ...), custom_call_target="tpu_custom_call" | custom-call | flops 10000000000 | bytes 67108864 | tf_op jit(solution)/shard_map/attend/pallas_call | solution.py:439
  89.1 1.2 reshape.27
  90.3 1.0 copy.19
  91.3 0.1 collective-permute-done.recv_l
  91.4 53.6 %finish.1 = bf16[4,64,768]{2,1,0:T(8,128)(2,1)S(1)} custom-call(bf16[2,6,32,512]{3,2,1,0:T(8,128)(2,1)} %bitcast.17, bf16[24,64,1024]{2,1,0:T(8,128)(2,1)} %get-tuple-element.14.keep, bf16[12,64,1024]{2,1,0:T(8,128)(2,1)} %get-tuple-element.15.recv_e, bf16[12,64,1024]{2,1,0:T(8,128)(2,1)} %collective-permute-done.recv_l, bf16[4,64,768]{2,1,0:T(8,128)(2,1)} %bitcast.16, ...), custom_call_target="tpu_custom_call" | custom-call | flops 12079595520 | bytes 47185920 | tf_op jit(solution)/shard_map/finish/pallas_call | solution.py:697
  145.0 0.7 copy.21
Async XLA Ops:
  58.2 33.2 %collective-permute-start = (bf16[12,64,1024]{2,1,0:T(8,128)(2,1)}, bf16[12,64,1024]{2,1,0:T(8,128)(2,1)}, u32[]{:S(2)}, u32[]{:S(2)}) collective-permute-start(bf16[12,64,1024]{2,1,0:T(8,128)(2,1)} %get-tuple-element.16), channel_id=1, source_target_pairs={{0,2},{1,3},{2,0},{3,1},{4,6},{5,7},{6,4},{7,5}} | collective-permute-start | bytes 4718600 | tf_op jit(solution)/shard_map/ppermute | solution.py:747

commit v14 on v13

--- a/solution.py
+++ b/solution.py
@@ -257,6 +257,8 @@
 
     q_cols = n_q * 2 * W
     multiply_q(2)
+    multiply(jnp.int32(n_far))
+    reduce_near(jnp.int32(n_far - 1))
     for g in range(n_q):
         reduce_q(2, g)
         for step in range(2):
@@ -281,7 +283,7 @@
     for copy in qkv_own:
         copy.start()
 
-    @pl.loop(n_far, n_all)
+    @pl.loop(n_far + 1, n_all)
     def _(g):
         multiply(g)
         reduce_near(g - 1)
@@ -423,9 +425,11 @@
             old = src[0, s, pl.ds(base, 16), :].astype(F32)
             new = fresh[which, pl.ds(step * SEQ_STEP + s, 1), :]
             dst[0, s, pl.ds(base, 16), :] = jnp.where(hit, new, old).astype(BF16)
-        scores = lax.dot_general(q_ref[s], k_out[0, s], (((1,), (1,)), ((), ())), preferred_element_type=F32) * scale
-        visible = lax.broadcasted_iota(jnp.int32, scores.shape, 1) <= length
-        scores = jnp.where(visible, scores, MASKED)
+        scores = lax.dot_general(q_ref[s], k_ref[0, s], (((1,), (1,)), ((), ())), preferred_element_type=F32) * scale
+        k_new = fresh[0, pl.ds(step * SEQ_STEP + s, 1), :]
+        own = jnp.sum(q_ref[s].astype(F32) * k_new, axis=1, keepdims=True) * scale
+        place = lax.broadcasted_iota(jnp.int32, scores.shape, 1)
+        scores = jnp.where(place < length, scores, jnp.where(place == length, own, MASKED))
         weights = jnp.exp2(scores - jnp.max(scores, axis=1, keepdims=True))
         probs = (weights * (1.0 / jnp.sum(weights, axis=1, keepdims=True))).astype(BF16)
         o_ref[s] = jnp.dot(probs, v_out[0, s], preferred_element_type=F32).astype(BF16)

time: 146 us -> 147 us (level)
  no operation moved by 1% of the time
where the time goes in v14:
time: 147 us; the launch traced here: 146 us
  Pallas kernels  139 us (95%)
  local copies, waits for them, and re-layouts  4.79 us (3%)
    pallas_call x1, Pallas kernels, project(): pl.pallas_call(functools.partial(project_kernel, n_q, n_ff, d_model), nam...  57.5 us
    pallas_call x1, Pallas kernels, finish(): pl.pallas_call(functools.partial(output_kernel, n_ff, n_o), name='finish'...  53.6 us
    pallas_call x1, Pallas kernels, attend(): pl.pallas_call(attend_kernel, name='attend', out_shape=(jax.ShapeDtypeStr...  27.9 us
  transfers between devices with their start and end apart: 1, of which 1 were waited for; matrix products, arithmetic and copies ran while one was open for 3% of the time, Pallas kernels for 19%

profile of v14, /device:TPU:0, one launch (start us, length us, event | category | flops | bytes accessed | tf_op | source)
XLA Modules:
  0.0 146.5 jit_solution(18395445561112080059)
XLA Ops:
  0.6 57.5 %project.1 = (bf16[2,32,3072]{2,1,0:T(8,128)(2,1)}, bf16[2,32,128]{2,1,0:T(8,128)(2,1)}, bf16[24,64,1024]{2,1,0:T(8,128)(2,1)}, bf16[12,64,1024]{2,1,0:T(8,128)(2,1)}, bf16[12,64,1024]{2,1,0:T(8,128)(2,1)}) custom-call(bf16[2,2,64,768]{3,2,1,0:T(8,128)(2,1)} %bitcast.15, bf16[1,1536]{1,0:T(2,128)(2,1)} %gain_in.1, bf16[1,1536,3072]{2,1,0:T(8,128)(2,1)} %wq.1, ...), custom_call_target="tpu_custom_call" | custom-call | flops 21843935232 | bytes 85327872 | tf_op jit(solution)/shard_map/project/pallas_call | solution.py:346
  58.2 0.9 collective-permute-start
  59.0 1.1 copy.17
  60.1 0.8 copy.15
  60.9 27.9 %attend.1 = (bf16[1,32,2048,128]{3,2,1,0:T(8,128)(2,1)}, bf16[1,32,2048,128]{3,2,1,0:T(8,128)(2,1)}, bf16[32,48,128]{2,1,0:T(8,128)(2,1)}) custom-call(s32[32]{0:T(128)} %lens.1, bf16[32,48,128]{2,1,0:T(8,128)(2,1)} %bitcast.19, bf16[2,32,128]{2,1,0:T(8,128)(2,1)} %get-tuple-element.12.kv_ref, bf16[1,32,2048,128]{3,2,1,0:T(8,128)(2,1)} %k_ref.1, ...), custom_call_target="tpu_custom_call" | custom-call | flops 10000000000 | bytes 67108864 | tf_op jit(solution)/shard_map/attend/pallas_call | solution.py:443
  88.8 1.2 reshape.27
  90.0 1.0 copy.19
  91.0 1.2 collective-permute-done.recv_l
  92.2 53.6 %finish.1 = bf16[4,64,768]{2,1,0:T(8,128)(2,1)S(1)} custom-call(bf16[2,6,32,512]{3,2,1,0:T(8,128)(2,1)} %bitcast.17, bf16[24,64,1024]{2,1,0:T(8,128)(2,1)} %get-tuple-element.14.keep, bf16[12,64,1024]{2,1,0:T(8,128)(2,1)} %get-tuple-element.15.recv_e, bf16[12,64,1024]{2,1,0:T(8,128)(2,1)} %collective-permute-done.recv_l, bf16[4,64,768]{2,1,0:T(8,128)(2,1)} %bitcast.16, ...), custom_call_target="tpu_custom_call" | custom-call | flops 12079595520 | bytes 47185920 | tf_op jit(solution)/shard_map/finish/pallas_call | solution.py:701
  145.7 0.7 copy.21
Async XLA Ops:
  58.2 34.0 %collective-permute-start = (bf16[12,64,1024]{2,1,0:T(8,128)(2,1)}, bf16[12,64,1024]{2,1,0:T(8,128)(2,1)}, u32[]{:S(2)}, u32[]{:S(2)}) collective-permute-start(bf16[12,64,1024]{2,1,0:T(8,128)(2,1)} %get-tuple-element.16), channel_id=1, source_target_pairs={{0,2},{1,3},{2,0},{3,1},{4,6},{5,7},{6,4},{7,5}} | collective-permute-start | bytes 4718600 | tf_op jit(solution)/shard_map/ppermute | solution.py:751
